TPU v7x, 32 devices: a whole 2x2x4 slice. The times are simulated.
32 devices in a mesh: row: 8 (over y, x, core), col: 4 (over z).
Axes of the slice: x: 2, y: 2, z: 4, core: 2. Of those that a mesh axis runs over, the one named last changes fastest.
Arguments:
- history: float32 [3, 512, 4096], P(None, None, ('row', 'col')), may hold values from -8 to 8
Outputs:
- orbitals: float32 [512, 4096], P(None, ('row', 'col'))
All inputs are finite; a program needn't handle non-finite values.
Results may differ from a plain program's by a relative error of at most 0.0003.
Values sent between devices are 32-bit elements; how exact they have to be, the bound alone decides.
No kernel may reach another device: no remote copies, remote signals or barrier semaphores. Data moves between devices by JAX's collectives and lax.ppermute only.
A program may use at most 64 MiB of HBM per device.

v0:
```python
import jax
import jax.numpy as jnp
from jax import lax
from jax.sharding import PartitionSpec as P


def on_device(history):
    precise = lax.Precision.HIGHEST
    npw_total = history.shape[2] * lax.axis_size("row") * lax.axis_size("col")
    newest = history[0]
    local_terms = tuple(
        (jnp.einsum("ip,jp->ij", newest, history[index], precision=precise) for index in range(3))
    )
    summed = lax.psum(local_terms, ("row", "col"))
    weights = (2.5, -2.0, 0.5)
    predicted = jnp.zeros(newest.shape, jnp.float32)
    for index in range(3):
        project = summed[index] / npw_total
        predicted = predicted + weights[index] * jnp.dot(project, history[index], precision=precise)
    local_gram = jnp.einsum("ip,jp->ij", predicted, predicted, precision=precise)
    gram = lax.psum(local_gram, ("row", "col"))
    factor = jnp.linalg.cholesky(gram / npw_total)
    return lax.linalg.triangular_solve(factor, predicted, left_side=True, lower=True)


def solution(mesh):
    return jax.shard_map(
        on_device,
        mesh=mesh,
        in_specs=(P(None, None, ("row", "col")),),
        out_specs=P(None, ("row", "col")),
        check_vma=False,
    )
```

profile of v0, /device:TPU:0, one launch (start us, length us, event | category | flops | bytes accessed | tf_op | source)
XLA Modules:
  0.0 441.6 jit_solution(1607792850113480831)
XLA Ops:
  6.5 3.1 fusion.11
  9.7 2.0 fusion.14
  11.6 2.0 fusion.19
  13.9 141.6 %all-reduce.7.cloned.1.call-done = (f32[512,512]{0,1:T(8,128)}, f32[512,512]{0,1:T(8,128)}, f32[512,512]{0,1:T(8,128)}) async-done(((f32[512,512]{0,1:T(8,128)}, f32[512,512]{0,1:T(8,128)}, f32[512,512]{0,1:T(8,128)}), (f32[512,512]{0,1:T(8,128)}, f32[512,512]{0,1:T(8,128)}, f32[512,512]{0,1:T(8,128)})) %all-reduce.7.cloned.1.call-update) | async-done | bytes 3145744 | tf_op jit(solution)/shard_map/psum | solution.py:14
  155.4 3.1 convolution_multiply_fusion.2
  158.6 1.8 fusion.1
  160.4 1.8 fusion
  162.2 2.0 fusion.61
  164.3 130.2 %all-reduce.5.cloned.1.call-done = f32[512,512]{0,1:T(8,128)} async-done(((f32[512,512]{0,1:T(8,128)}), f32[512,512]{0,1:T(8,128)}) %all-reduce.5.cloned.1.call-update) | async-done | bytes 1048592 | tf_op jit(solution)/shard_map/psum | solution.py:21
  294.5 1.3 broadcast_multiply_fusion
  296.2 0.9 copy-done.1
  297.3 11.7 %cholesky.104 = f32[128,128]{1,0:T(8,128)S(1)} custom-call(f32[128,128]{1,0:T(8,128)S(1)} %cholesky.266), custom_call_target="Cholesky" | custom-call | tf_op jit(solution)/shard_map/jit(cholesky)/cholesky | solution.py:22
  309.0 10.0 %custom-call.30 = f32[1,128,128]{1,2,0:T(8,128)S(1)} custom-call(f32[1,128,128]{2,1,0:T(8,128)S(1)} %get-tuple-element.35), custom_call_target="InvertDiagBlocksLowerTriangular" | custom-call | tf_op jit(solution)/shard_map/jit(cholesky)/cholesky | solution.py:22
  319.8 11.7 %cholesky.217 = f32[128,128]{1,0:T(8,128)S(1)} custom-call(f32[128,128]{1,0:T(8,128)S(1)} %cholesky.270), custom_call_target="Cholesky" | custom-call | tf_op jit(solution)/shard_map/jit(cholesky)/cholesky | solution.py:22
  331.6 9.8 %custom-call.31 = f32[1,128,128]{1,2,0:T(8,128)S(1)} custom-call(f32[1,128,128]{2,1,0:T(8,128)S(1)} %get-tuple-element.32), custom_call_target="InvertDiagBlocksLowerTriangular" | custom-call | tf_op jit(solution)/shard_map/jit(cholesky)/cholesky | solution.py:22
  342.1 11.7 %cholesky.238 = f32[128,128]{1,0:T(8,128)S(1)} custom-call(f32[128,128]{1,0:T(8,128)S(1)} %cholesky.275), custom_call_target="Cholesky" | custom-call | tf_op jit(solution)/shard_map/jit(cholesky)/cholesky | solution.py:22
  354.5 10.0 %custom-call.32 = f32[1,128,128]{1,2,0:T(8,128)S(1)} custom-call(f32[1,128,128]{2,1,0:T(8,128)S(1)} %get-tuple-element.29), custom_call_target="InvertDiagBlocksLowerTriangular" | custom-call | tf_op jit(solution)/shard_map/jit(cholesky)/cholesky | solution.py:22
  365.2 11.7 %cholesky.255 = f32[128,128]{1,0:T(8,128)S(1)} custom-call(f32[128,128]{1,0:T(8,128)S(1)} %convolution_subtract_fusion.5), custom_call_target="Cholesky" | custom-call | tf_op jit(solution)/shard_map/jit(cholesky)/cholesky | solution.py:22
  380.9 10.6 %while.1 = (s32[]{:T(128)}, f32[512,512]{1,0:T(8,128)S(1)}, s32[4,2]{0,1:T(2,128)S(1)}, f32[4,128,128]{2,1,0:T(8,128)}, s32[]{:T(128)}) while((s32[]{:T(128)}, f32[512,512]{1,0:T(8,128)S(1)}, s32[4,2]{0,1:T(2,128)S(1)}, f32[4,128,128]{2,1,0:T(8,128)}, s32[]{:T(128)}) %tuple.27), condition=%wide.while_cond, body=%wide.while_body.sunk | while | flops 2 | bytes 132705 | solution.py:23
  381.6 2.0 bitcast_dynamic-update-slice_fusion.2
  384.3 2.0 bitcast_dynamic-update-slice_fusion.2
  386.9 2.0 bitcast_dynamic-update-slice_fusion.2
  389.6 2.0 bitcast_dynamic-update-slice_fusion.2
  391.5 40.1 %custom-call.33 = f32[4,128,128]{1,2,0:T(8,128)S(1)} custom-call(f32[4,128,128]{2,1,0:T(8,128)} %get-tuple-element.12), custom_call_target="InvertDiagBlocksLowerTriangular" | custom-call | tf_op jit(solution)/shard_map/triangular_solve | solution.py:23
  (50 shorter events, 10.5 us)
Async XLA Ops:
  6.5 3.1 copy-start
  6.5 148.9 %all-reduce.7.cloned.1.call-start = ((), (), s32[]{:S(2)}) async-start(), calls=%async_computation.1 | async-start | bytes 6291456 | tf_op jit(solution)/shard_map/psum | solution.py:14
  13.6 280.9 %all-reduce.5.cloned.1.call-start = ((), (), s32[]{:S(2)}) async-start(), calls=%async_computation | async-start | bytes 2097152 | tf_op jit(solution)/shard_map/psum | solution.py:21
  155.4 3.1 copy-start.3
  158.5 1.8 copy-start.2
  295.8 1.2 copy-start.1
Sparse Core Ops, SparseCore 0:
  13.8 141.6 all-reduce.6
  164.4 130.0 all-reduce.4
where the time goes:
time: 445 us; the launch traced here: 442 us
  waiting for transfers between devices  272 us (61%)
  other arithmetic  121 us (27%)
  matrix products  19.7 us (4%)
  between operations  16.6 us (4%)
  local copies, waits for them, and re-layouts  11.9 us (3%)
    psum x1, waiting for transfers between devices, on_device(): summed = lax.psum(local_terms, ('row', 'col'))  142 us
    psum x1, waiting for transfers between devices, on_device(): gram = lax.psum(local_gram, ('row', 'col'))  130 us
    another operation x14, other arithmetic, on_device(): factor = jnp.linalg.cholesky(gram / npw_total)  78.9 us
    another operation x4, other arithmetic, on_device(): lax.linalg.triangular_solve(factor, predicted, left_side=True, lower=True)  41 us
    another operation x12, local copies, waits for them, and re-layouts  10.6 us
  transfers between devices with their start and end apart: 2, of which 2 were waited for; matrix products, arithmetic and copies ran while one was open for 0% of the time, Pallas kernels for 0%

commit v1 on v0

v1 whole, which is shorter than its diff:
```python
import functools

import jax
import jax.numpy as jnp
from jax import lax
from jax.experimental import pallas as pl
from jax.experimental.pallas import tpu as pltpu
from jax.sharding import PartitionSpec as P

HIGHEST = lax.Precision.HIGHEST
WEIGHTS = (2.5, -2.0, 0.5)
TILE = 128
PANEL = 32
GROUP = 16
AXES = ("row", "col")
NT = (((1,), (1,)), ((), ()))
NN = (((1,), (0,)), ((), ()))
TN = (((0,), (0,)), ((), ()))


def dot(a, b, dims):
    return lax.dot_general(a, b, dims, precision=HIGHEST, preferred_element_type=jnp.float32)


class Route:
    def __init__(self, mesh_rows, mesh_cols):
        self.rows, self.cols = mesh_rows, mesh_cols
        row_bits = list(range(1, mesh_rows.bit_length() - 1))
        col_bits = list(range(mesh_cols.bit_length() - 1))
        half = len(row_bits) // 2
        orders = (row_bits, row_bits[half:] + row_bits[:half])
        self.row_levels = len(row_bits)
        self.orders = tuple(
            [("row", b) for b in order] + [("col", b) for b in col_bits] for order in orders
        )
        self.levels = len(self.orders[0])

    def core_perm(self):
        c = self.cols
        return [(r * c + k, (r ^ 1) * c + k) for r in range(self.rows) for k in range(c)]

    def perm(self, level):
        pairs = []
        for r in range(self.rows):
            for k in range(self.cols):
                axis, bit = self.orders[r & 1][level]
                to = (r ^ (1 << bit), k) if axis == "row" else (r, k ^ (1 << bit))
                pairs.append((r * self.cols + k, to[0] * self.cols + to[1]))
        return pairs

    def place(self, core, levels):
        index = {"row": lax.axis_index("row"), "col": lax.axis_index("col")}
        numbers = []
        for order in self.orders:
            number = jnp.int32(0)
            for axis, bit in order[:levels]:
                number = number * 2 + ((index[axis] >> bit) & 1)
            numbers.append(number)
        return jnp.where(core == 0, numbers[0], numbers[1])


def swap(x, perm):
    return lax.ppermute(x, AXES, perm)


def all_reduce(route, keep, send, scatter, levels):
    for level in range(scatter):
        got = swap(send, route.perm(level))
        if level < scatter - 1:
            half = keep.shape[0] // 2
            keep, send = keep[:half] + got[:half], keep[half:] + got[half:]
        else:
            keep = keep + got
    for level in range(scatter, levels):
        keep = keep + swap(keep, route.perm(level))
    for level in reversed(range(scatter)):
        keep = jnp.concatenate([keep, swap(keep, route.perm(level))], axis=0)
    return keep


def project_kernel(blocks, where, own_ref, peer_ref, *refs):
    outs, (left, right) = refs[:-2], refs[-2:]
    rows, width = left.shape[0], own_ref.shape[2]
    core, place = where[0], where[1]
    size = rows // blocks
    for k in range(blocks):
        at = pl.multiple_of(core * rows + (place ^ k) * size, size)
        left[k * size : (k + 1) * size, :width] = own_ref[0, pl.ds(at, size), :]
        left[k * size : (k + 1) * size, width:] = peer_ref[0, pl.ds(at, size), :]
    for j in range(own_ref.shape[0]):
        right[:, :width] = own_ref[j]
        right[:, width:] = peer_ref[j]
        keep, send = outs[2 * j], outs[2 * j + 1]
        half = keep.shape[0]
        keep[...] = dot(left[:half, :], right[...], NT)
        send[...] = dot(left[half:, :], right[...], NT)


def predict_kernel(blocks, scales, where, m0, m1, m2, own_ref, peer_ref, out_ref, both, acc):
    rows, width = m0.shape[0], own_ref.shape[2]
    size = rows // blocks
    for j, m in enumerate((m0, m1, m2)):
        both[:, :width] = own_ref[j]
        both[:, width:] = peer_ref[j]
        term = dot(m[...], both[...], NN) * scales[j]
        if j == 0:
            acc[...] = term
        else:
            acc[...] += term
    place = where[1]
    for k in range(blocks):
        at = pl.multiple_of((place ^ k) * size, size)
        out_ref[pl.ds(at, size), :] = acc[k * size : (k + 1) * size, :]


def core_blocks(count):
    blocks = [(i, j) for i in range(count) for j in range(i, count)]
    half = (len(blocks) + 1) // 2
    return blocks[:half], blocks[half:]


def gram_kernel(parts, scale, where, p_ref, keep_ref, send_ref, acc):
    count = p_ref.shape[0] // TILE
    lists = core_blocks(count)
    core, place = where[0], where[1]
    for n in range(len(lists[0])):
        first = lists[0][n]
        second = lists[1][min(n, len(lists[1]) - 1)]
        i = jnp.where(core == 0, first[0], second[0])
        j = jnp.where(core == 0, first[1], second[1])
        a = p_ref[pl.ds(pl.multiple_of(i * TILE, TILE), TILE), :]
        b = p_ref[pl.ds(pl.multiple_of(j * TILE, TILE), TILE), :]
        acc[n * TILE : (n + 1) * TILE, :] = dot(a, b, NT) * scale
    size = acc.shape[0] // parts
    for k in range(parts):
        rows = acc[pl.ds(pl.multiple_of((place ^ k) * size, 8), size), :]
        if k < parts // 2:
            keep_ref[k * size : (k + 1) * size, :] = rows
        else:
            send_ref[(k - parts // 2) * size : (k - parts // 2 + 1) * size, :] = rows


def solve_kernel(parts, where, mine_ref, other_ref, p_ref, out_ref, natural, work):
    n, tile = p_ref.shape[0], TILE
    width = n + out_ref.shape[1]
    count, groups, per_panel, panels = n // tile, width // tile, PANEL // 8, tile // PANEL
    core, size = where[0], mine_ref.shape[0] // parts
    for ref, number, place in ((mine_ref, core, where[1]), (other_ref, 1 - core, where[2])):
        for k in range(parts):
            at = pl.multiple_of((place ^ k) * size, 8)
            natural[number, pl.ds(at, size), :] = ref[k * size : (k + 1) * size, :]
    for number, blocks in enumerate(core_blocks(count)):
        for at, (i, j) in enumerate(blocks):
            work[i * tile : (i + 1) * tile, j * tile : (j + 1) * tile] = natural[number, at * tile : (at + 1) * tile, :]
    work[:, n:] = p_ref[:, : out_ref.shape[1]]
    sub = lax.broadcasted_iota(jnp.int32, (8, tile), 0)

    def panel(r0, s):
        base = r0 + PANEL * s
        r = [
            [work[pl.ds(base + 8 * i, 8), c * tile : (c + 1) * tile] for c in range(groups)]
            + [work[pl.ds(base + 8 * i, 8), pl.ds(r0, tile)]]
            for i in range(per_panel)
        ]
        scale = [jnp.zeros((8, tile), jnp.float32)] * per_panel
        cols = {}
        for j in range(PANEL):
            if j % GROUP == 0:
                cols = {
                    k: {
                        i: jnp.broadcast_to(r[i][groups][:, PANEL * s + k : PANEL * s + k + 1], (8, tile))
                        for i in range(k // 8, per_panel)
                    }
                    for k in range(j, j + GROUP)
                }
            jb, js = j // 8, j % 8
            col = cols[j]
            pivot = jnp.broadcast_to(col[jb][js : js + 1, :], (8, tile))
            scale[jb] = jnp.where(sub == js, lax.rsqrt(pivot), scale[jb])
            inverse = 1.0 / pivot
            mult = {i: col[i] * inverse for i in range(jb, per_panel)}
            mult[jb] = jnp.where(sub > js, mult[jb], 0.0)
            first = jb if js < 7 else jb + 1
            for k in range(j + 1, (j // GROUP + 1) * GROUP):
                row = jnp.broadcast_to(col[k // 8][k % 8 : k % 8 + 1, :], (8, tile))
                for i in range(k // 8, per_panel):
                    cols[k][i] = cols[k][i] - mult[i] * row
            for c in range(groups + 1):
                row = jnp.broadcast_to(r[jb][c][js : js + 1, :], (8, tile))
                for i in range(first, per_panel):
                    r[i][c] = r[i][c] - mult[i] * row
        for i in range(per_panel):
            for c in range(groups):
                work[pl.ds(base + 8 * i, 8), c * tile : (c + 1) * tile] = r[i][c] * scale[i]
        return jnp.concatenate([r[i][groups] * scale[i] for i in range(per_panel)], axis=0)

    def block(b, carry):
        r0 = pl.multiple_of(b * tile, tile)
        for s in range(panels):
            left = panel(r0, s)
            if s < panels - 1:
                low = PANEL * (s + 1)
                update = dot(left, work[pl.ds(r0 + PANEL * s, PANEL), :], TN)
                work[pl.ds(r0 + low, tile - low), :] -= update[low:, :]

        def trail(i, inner):
            at = pl.multiple_of(i * tile, tile)
            work[pl.ds(at, tile), :] -= dot(work[pl.ds(r0, tile), pl.ds(at, tile)], work[pl.ds(r0, tile), :], TN)
            return inner

        lax.fori_loop(b + 1, count, trail, 0)
        return carry

    lax.fori_loop(0, count, block, 0)
    out_ref[...] = work[:, n:]


VMEM = pl.BlockSpec(memory_space=pltpu.VMEM)
SMEM = pl.BlockSpec(memory_space=pltpu.SMEM)


def f32(*shape):
    return jax.ShapeDtypeStruct(shape, jnp.float32)


def call(kernel, name, out_shape, scratch, *args):
    return pl.pallas_call(
        kernel,
        name=name,
        out_shape=out_shape,
        in_specs=[SMEM] + [VMEM] * (len(args) - 1),
        out_specs=jax.tree.map(lambda _: VMEM, out_shape),
        scratch_shapes=[pltpu.VMEM(s.shape, s.dtype) for s in scratch],
    )(*args)


def on_device(rows, cols, history):
    route = Route(rows, cols)
    terms, norb, width = history.shape
    total = width * rows * cols
    half = norb // 2
    core = lax.axis_index("row") & 1

    levels = route.levels
    scatter = min(levels, (half // 8).bit_length() - 1)
    blocks = 1 << scatter
    where_m = jnp.stack([core, route.place(core, scatter)])
    parts_levels = route.row_levels
    parts = 1 << parts_levels
    where_g = jnp.stack([core, route.place(core, parts_levels), route.place(1 - core, parts_levels)])

    peer = swap(history, route.core_perm())
    quarter = half // 2
    products = call(
        functools.partial(project_kernel, blocks),
        "project",
        [f32(quarter, norb)] * (2 * terms),
        [f32(half, 2 * width), f32(norb, 2 * width)],
        where_m,
        history,
        peer,
    )
    m = [all_reduce(route, products[2 * j], products[2 * j + 1], scatter, levels) for j in range(terms)]
    mine = call(
        functools.partial(predict_kernel, blocks, tuple(w / total for w in WEIGHTS)),
        "predict",
        f32(half, 2 * width),
        [f32(norb, 2 * width), f32(half, 2 * width)],
        where_m,
        *m,
        history,
        peer,
    )
    other = swap(mine, route.core_perm())
    other = jnp.concatenate([other[:, width:], other[:, :width]], axis=1)
    predicted = jnp.where(core == 0, jnp.concatenate([mine, other]), jnp.concatenate([other, mine]))

    shares = (norb // TILE) * (norb // TILE + 1) // 2
    share = (shares + 1) // 2 * TILE
    keep, send = call(
        functools.partial(gram_kernel, parts, 1.0 / total),
        "gram",
        [f32(share // 2, TILE)] * 2,
        [f32(share, TILE)],
        where_g,
        predicted,
    )
    gram = all_reduce(route, keep, send, parts_levels, levels)
    gram_other = swap(gram, route.core_perm())
    return call(
        functools.partial(solve_kernel, parts),
        "solve",
        f32(norb, width),
        [f32(2, share, TILE), f32(norb, norb + width)],
        where_g,
        gram,
        gram_other,
        predicted,
    )


def solution(mesh):
    return jax.shard_map(
        functools.partial(on_device, mesh.shape["row"], mesh.shape["col"]),
        mesh=mesh,
        in_specs=(P(None, None, ("row", "col")),),
        out_specs=P(None, ("row", "col")),
        check_vma=False,
    )
```

time: 445 us -> 134 us (0.30)
  waiting for transfers between devices: 272 us -> 39.9 us
  other arithmetic: 121 us -> 4.31 us
  starting transfers between devices: 0.22 us -> 53.9 us
  Pallas kernels: 0 us -> 32.6 us
  matrix products: 19.7 us -> 0 us
  between operations: 16.6 us -> 0.28 us
  local copies, waits for them, and re-layouts: 11.9 us -> 2.59 us
    psum x2 -> x0, waiting for transfers between devices: 272 us -> none  [the longest x1 142 us: on_device(): summed = lax.psum(local_terms, ('row', 'col'))]
    another operation x18 -> x2, other arithmetic: 120 us -> 1.17 us  [the longest x1 0.59 us: on_device(): where_m = jnp.stack([core, route.place(core, scatter)])]
    ppermute x0 -> x33, starting transfers between devices: none -> 53.9 us  [swap(): return lax.ppermute(x, AXES, perm)]
    ppermute x0 -> x33, waiting for transfers between devices: none -> 39.9 us  [swap(): return lax.ppermute(x, AXES, perm)]
    pallas_call x0 -> x4, Pallas kernels: none -> 32.6 us  [call(): pl.pallas_call(kernel, name=name, out_shape=out_shape, in_specs=[SMEM] +...]
    dot_general x7 -> x0, matrix products: 15.9 us -> none  [the longest x3 7.06 us: on_device(): jnp.einsum('ip,jp->ij', newest, history[index], precision=precise)]
    another operation x17 -> x0, local copies, waits for them, and re-layouts: 10.7 us -> none
  transfers between devices with their start and end apart: 2 -> 33, of which waited for: 2 -> 20; matrix products, arithmetic and copies ran while one was open for 0% -> 2% of each run, Pallas kernels for 0% -> 0%
where the time goes in v1:
time: 134 us; the launch traced here: 133 us
  starting transfers between devices  53.9 us (40%)
  waiting for transfers between devices  39.9 us (30%)
  Pallas kernels  32.6 us (24%)
  other arithmetic  4.31 us (3%)
  local copies, waits for them, and re-layouts  2.59 us (2%)
    ppermute x33, starting transfers between devices, swap(): return lax.ppermute(x, AXES, perm)  53.9 us
    ppermute x33, waiting for transfers between devices, swap(): return lax.ppermute(x, AXES, perm)  39.9 us
    pallas_call x4, Pallas kernels, call(): pl.pallas_call(kernel, name=name, out_shape=out_shape, in_specs=[SMEM] +...  32.6 us
  transfers between devices with their start and end apart: 33, of which 20 were waited for; matrix products, arithmetic and copies ran while one was open for 2% of the time, Pallas kernels for 0%

profile of v1, /device:TPU:0, one launch (start us, length us, event | category | flops | bytes accessed | tf_op | source)
XLA Modules:
  0.0 133.5 jit_solution(11693156606633195796)
XLA Ops:
  3.5 5.3 %project.1 = (f32[128,512]{1,0:T(8,128)}, f32[128,512]{1,0:T(8,128)}, f32[128,512]{1,0:T(8,128)}, f32[128,512]{1,0:T(8,128)}, f32[128,512]{1,0:T(8,128)}, /*index=5*/f32[128,512]{1,0:T(8,128)}) custom-call(s32[2]{0:T(128)} %pad_add_fusion.1.where, f32[3,512,128]{2,1,0:T(8,128)} %own_ref.3, f32[3,512,128]{2,1,0:T(8,128)} %copy-done), custom_call_target="tpu_custom_call" | custom-call | tf_op jit(solution)/shard_map/project/pallas_call | solution.py:227
  8.8 2.9 %collective-permute-start.1 = (f32[128,512]{1,0:T(8,128)}, f32[128,512]{1,0:T(8,128)S(1)}, u32[]{:S(2)}, u32[]{:S(2)}) collective-permute-start(f32[128,512]{1,0:T(8,128)} %get-tuple-element.14), channel_id=1, source_target_pairs={{0,8},{1,9},{2,10},{3,11},{4,20},{5,21},{6,22},{7,23},{8,0},{9,1},... | collective-permute-start | bytes 786440 | tf_op jit(solution)/shard_map/ppermute | solution.py:63
  13.7 2.5 %collective-permute-done.1 = f32[128,512]{1,0:T(8,128)S(1)} collective-permute-done((f32[128,512]{1,0:T(8,128)}, f32[128,512]{1,0:T(8,128)S(1)}, u32[]{:S(2)}, u32[]{:S(2)}) %collective-permute-start.1) | collective-permute-done | bytes 262176 | tf_op jit(solution)/shard_map/ppermute | solution.py:63
  17.3 2.1 %collective-permute-start.2 = (f32[64,512]{1,0:T(8,128)S(1)}, f32[64,512]{1,0:T(8,128)S(1)}, u32[]{:S(2)}, u32[]{:S(2)}) collective-permute-start(f32[64,512]{1,0:T(8,128)S(1)} %get-tuple-element.32), channel_id=1, source_target_pairs={{0,16},{1,17},{2,18},{3,19},{4,12},{5,13},{6,14},{7,15},{8,24},{9,... | collective-permute-start | bytes 393224 | tf_op jit(solution)/shard_map/ppermute | solution.py:63
  21.2 3.0 %collective-permute-done.17 = f32[128,512]{1,0:T(8,128)S(1)} collective-permute-done((f32[128,512]{1,0:T(8,128)}, f32[128,512]{1,0:T(8,128)S(1)}, u32[]{:S(2)}, u32[]{:S(2)}) %collective-permute-start.17) | collective-permute-done | bytes 262176 | tf_op jit(solution)/shard_map/ppermute | solution.py:63
  24.2 2.4 %collective-permute-start.18 = (f32[64,512]{1,0:T(8,128)S(1)}, f32[64,512]{1,0:T(8,128)S(1)}, u32[]{:S(2)}, u32[]{:S(2)}) collective-permute-start(f32[64,512]{1,0:T(8,128)S(1)} %get-tuple-element.28), channel_id=1, source_target_pairs={{0,16},{1,17},{2,18},{3,19},{4,12},{5,13},{6,14},{7,15},{8,24},{9,... | collective-permute-start | bytes 393224 | tf_op jit(solution)/shard_map/ppermute | solution.py:63
  29.6 2.1 %collective-permute-start.19 = (f32[32,512]{1,0:T(8,128)S(1)}, f32[32,512]{1,0:T(8,128)S(1)}, u32[]{:S(2)}, u32[]{:S(2)}) collective-permute-start(f32[32,512]{1,0:T(8,128)S(1)} %get-tuple-element.36), channel_id=1, source_target_pairs={{0,1},{1,0},{2,3},{3,2},{4,5},{5,4},{6,7},{7,6},{8,9},{9,8},{10,11... | collective-permute-start | bytes 196616 | tf_op jit(solution)/shard_map/ppermute | solution.py:63
  31.7 2.7 %collective-permute-start.4 = (f32[16,512]{1,0:T(8,128)S(1)}, f32[16,512]{1,0:T(8,128)S(1)}, u32[]{:S(2)}, u32[]{:S(2)}) collective-permute-start(f32[16,512]{1,0:T(8,128)S(1)} %slice_add_fusion.18), channel_id=1, source_target_pairs={{0,2},{1,3},{2,0},{3,1},{4,6},{5,7},{6,4},{7,5},{8,10},{9,11},{10,... | collective-permute-start | bytes 98312 | tf_op jit(solution)/shard_map/ppermute | solution.py:63
  34.4 2.6 %collective-permute-start.20 = (f32[16,512]{1,0:T(8,128)S(1)}, f32[16,512]{1,0:T(8,128)S(1)}, u32[]{:S(2)}, u32[]{:S(2)}) collective-permute-start(f32[16,512]{1,0:T(8,128)S(1)} %slice_add_fusion.14), channel_id=1, source_target_pairs={{0,2},{1,3},{2,0},{3,1},{4,6},{5,7},{6,4},{7,5},{8,10},{9,11},{10,... | collective-permute-start | bytes 98312 | tf_op jit(solution)/shard_map/ppermute | solution.py:63
  39.3 2.6 %collective-permute-start.21 = (f32[16,512]{1,0:T(8,128)S(1)}, f32[16,512]{1,0:T(8,128)S(1)}, u32[]{:S(2)}, u32[]{:S(2)}) collective-permute-start(f32[16,512]{1,0:T(8,128)S(1)} %get-tuple-element.22), channel_id=1, source_target_pairs={{0,2},{1,3},{2,0},{3,1},{4,6},{5,7},{6,4},{7,5},{8,10},{9,11},{10,... | collective-permute-start | bytes 98312 | tf_op jit(solution)/shard_map/ppermute | solution.py:63
  42.4 3.0 %collective-permute-start.5 = (f32[16,512]{1,0:T(8,128)S(1)}, f32[16,512]{1,0:T(8,128)S(1)}, u32[]{:S(2)}, u32[]{:S(2)}) collective-permute-start(f32[16,512]{1,0:T(8,128)S(1)} %get-tuple-element.26), channel_id=1, source_target_pairs={{0,2},{1,3},{2,0},{3,1},{4,6},{5,7},{6,4},{7,5},{8,10},{9,11},{10,... | collective-permute-start | bytes 98312 | tf_op jit(solution)/shard_map/ppermute | solution.py:63
  45.3 2.4 %collective-permute-start.22 = (f32[32,512]{1,0:T(8,128)S(1)}, f32[32,512]{1,0:T(8,128)S(1)}, u32[]{:S(2)}, u32[]{:S(2)}) collective-permute-start(f32[32,512]{1,0:T(8,128)S(1)} %pad_maximum_fusion.10), channel_id=1, source_target_pairs={{0,1},{1,0},{2,3},{3,2},{4,5},{5,4},{6,7},{7,6},{8,9},{9,8},{10,11... | collective-permute-start | bytes 196616 | tf_op jit(solution)/shard_map/ppermute | solution.py:63
  63.9 2.0 %collective-permute-done.16 = f32[128,512]{1,0:T(8,128)S(1)} collective-permute-done((f32[128,512]{1,0:T(8,128)S(1)}, f32[128,512]{1,0:T(8,128)S(1)}, u32[]{:S(2)}, u32[]{:S(2)}) %collective-permute-start.16) | collective-permute-done | bytes 262176 | tf_op jit(solution)/shard_map/ppermute | solution.py:63
  66.0 2.8 %collective-permute-done.8 = f32[128,512]{1,0:T(8,128)S(1)} collective-permute-done((f32[128,512]{1,0:T(8,128)S(1)}, f32[128,512]{1,0:T(8,128)S(1)}, u32[]{:S(2)}, u32[]{:S(2)}) %collective-permute-start.8) | collective-permute-done | bytes 262176 | tf_op jit(solution)/shard_map/ppermute | solution.py:63
  69.6 4.1 %predict.1 = f32[256,256]{1,0:T(8,128)} custom-call(s32[2]{0:T(128)} %pad_add_fusion.1.where, f32[256,512]{1,0:T(8,128)} %copy-done.5, f32[256,512]{1,0:T(8,128)} %copy-done.4, f32[256,512]{1,0:T(8,128)} %copy-done.3, f32[3,512,128]{2,1,0:T(8,128)} %own_ref.3, f32[3,512,128]{2,1,0:T(8,128)} %copy-done), custom_call_target="tpu_custom_call" | custom-call | tf_op jit(solution)/shard_map/predict/pallas_call | solution.py:227
  76.3 2.5 %gram.1 = (f32[320,128]{1,0:T(8,128)}, f32[320,128]{1,0:T(8,128)}) custom-call(s32[3]{0:T(128)} %pad_add_fusion.where, f32[512,256]{1,0:T(8,128)} %maximum_select_fusion.p_ref), custom_call_target="tpu_custom_call" | custom-call | tf_op jit(solution)/shard_map/gram/pallas_call | solution.py:227
  80.6 3.8 %collective-permute-done.26 = f32[320,128]{1,0:T(8,128)S(1)} collective-permute-done((f32[320,128]{1,0:T(8,128)}, f32[320,128]{1,0:T(8,128)S(1)}, u32[]{:S(2)}, u32[]{:S(2)}) %collective-permute-start.26) | collective-permute-done | bytes 163872 | tf_op jit(solution)/shard_map/ppermute | solution.py:63
  87.1 2.6 %collective-permute-done.27 = f32[160,128]{1,0:T(8,128)S(1)} collective-permute-done((f32[160,128]{1,0:T(8,128)S(1)}, f32[160,128]{1,0:T(8,128)S(1)}, u32[]{:S(2)}, u32[]{:S(2)}) %collective-permute-start.27) | collective-permute-done | bytes 81952 | tf_op jit(solution)/shard_map/ppermute | solution.py:63
  91.7 2.7 %collective-permute-done.28 = f32[160,128]{1,0:T(8,128)S(1)} collective-permute-done((f32[160,128]{1,0:T(8,128)S(1)}, f32[160,128]{1,0:T(8,128)S(1)}, u32[]{:S(2)}, u32[]{:S(2)}) %collective-permute-start.28) | collective-permute-done | bytes 81952 | tf_op jit(solution)/shard_map/ppermute | solution.py:63
  94.3 2.4 %collective-permute-start.29 = (f32[160,128]{1,0:T(8,128)S(1)}, f32[160,128]{1,0:T(8,128)S(1)}, u32[]{:S(2)}, u32[]{:S(2)}) collective-permute-start(f32[160,128]{1,0:T(8,128)S(1)} %add.130), channel_id=1, source_target_pairs={{0,2},{1,3},{2,0},{3,1},{4,6},{5,7},{6,4},{7,5},{8,10},{9,11},{10,... | collective-permute-start | bytes 245768 | tf_op jit(solution)/shard_map/ppermute | solution.py:63
  96.7 3.0 %collective-permute-done.29 = f32[160,128]{1,0:T(8,128)S(1)} collective-permute-done((f32[160,128]{1,0:T(8,128)S(1)}, f32[160,128]{1,0:T(8,128)S(1)}, u32[]{:S(2)}, u32[]{:S(2)}) %collective-permute-start.29) | collective-permute-done | bytes 81952 | tf_op jit(solution)/shard_map/ppermute | solution.py:63
  101.6 3.4 %collective-permute-done.30 = f32[160,128]{1,0:T(8,128)S(1)} collective-permute-done((f32[160,128]{1,0:T(8,128)S(1)}, f32[160,128]{1,0:T(8,128)S(1)}, u32[]{:S(2)}, u32[]{:S(2)}) %collective-permute-start.30) | collective-permute-done | bytes 81952 | tf_op jit(solution)/shard_map/ppermute | solution.py:63
  106.8 3.6 %collective-permute-done.31 = f32[320,128]{1,0:T(8,128)S(1)} collective-permute-done((f32[320,128]{1,0:T(8,128)S(1)}, f32[320,128]{1,0:T(8,128)S(1)}, u32[]{:S(2)}, u32[]{:S(2)}) %collective-permute-start.31) | collective-permute-done | bytes 163872 | tf_op jit(solution)/shard_map/ppermute | solution.py:63
  112.9 20.6 %solve.1 = f32[512,128]{1,0:T(8,128)} custom-call(s32[3]{0:T(128)} %pad_add_fusion.where, f32[640,128]{1,0:T(8,128)} %copy-done.1, f32[640,128]{1,0:T(8,128)} %copy-done.6, f32[512,256]{1,0:T(8,128)} %maximum_select_fusion.p_ref), custom_call_target="tpu_custom_call" | custom-call | tf_op jit(solution)/shard_map/solve/pallas_call | solution.py:227
  (109 shorter events, 46.2 us)
Async XLA Ops:
  8.8 7.4 %collective-permute-start.1 = (f32[128,512]{1,0:T(8,128)}, f32[128,512]{1,0:T(8,128)S(1)}, u32[]{:S(2)}, u32[]{:S(2)}) collective-permute-start(f32[128,512]{1,0:T(8,128)} %get-tuple-element.14), channel_id=1, source_target_pairs={{0,8},{1,9},{2,10},{3,11},{4,20},{5,21},{6,22},{7,23},{8,0},{9,1},... | collective-permute-start | bytes 786440 | tf_op jit(solution)/shard_map/ppermute | solution.py:63
  11.6 7.7 %collective-permute-start.9 = (f32[128,512]{1,0:T(8,128)}, f32[128,512]{1,0:T(8,128)S(1)}, u32[]{:S(2)}, u32[]{:S(2)}) collective-permute-start(f32[128,512]{1,0:T(8,128)} %get-tuple-element.16), channel_id=1, source_target_pairs={{0,8},{1,9},{2,10},{3,11},{4,20},{5,21},{6,22},{7,23},{8,0},{9,1},... | collective-permute-start | bytes 786440 | tf_op jit(solution)/shard_map/ppermute | solution.py:63
  11.7 12.5 %collective-permute-start.17 = (f32[128,512]{1,0:T(8,128)}, f32[128,512]{1,0:T(8,128)S(1)}, u32[]{:S(2)}, u32[]{:S(2)}) collective-permute-start(f32[128,512]{1,0:T(8,128)} %get-tuple-element.18), channel_id=1, source_target_pairs={{0,8},{1,9},{2,10},{3,11},{4,20},{5,21},{6,22},{7,23},{8,0},{9,1},... | collective-permute-start | bytes 786440 | tf_op jit(solution)/shard_map/ppermute | solution.py:63
  17.3 9.3 %collective-permute-start.2 = (f32[64,512]{1,0:T(8,128)S(1)}, f32[64,512]{1,0:T(8,128)S(1)}, u32[]{:S(2)}, u32[]{:S(2)}) collective-permute-start(f32[64,512]{1,0:T(8,128)S(1)} %get-tuple-element.32), channel_id=1, source_target_pairs={{0,16},{1,17},{2,18},{3,19},{4,12},{5,13},{6,14},{7,15},{8,24},{9,... | collective-permute-start | bytes 393224 | tf_op jit(solution)/shard_map/ppermute | solution.py:63
  19.4 8.8 %collective-permute-start.10 = (f32[64,512]{1,0:T(8,128)S(1)}, f32[64,512]{1,0:T(8,128)S(1)}, u32[]{:S(2)}, u32[]{:S(2)}) collective-permute-start(f32[64,512]{1,0:T(8,128)S(1)} %get-tuple-element.30), channel_id=1, source_target_pairs={{0,16},{1,17},{2,18},{3,19},{4,12},{5,13},{6,14},{7,15},{8,24},{9,... | collective-permute-start | bytes 393224 | tf_op jit(solution)/shard_map/ppermute | solution.py:63
  24.2 5.4 %collective-permute-start.18 = (f32[64,512]{1,0:T(8,128)S(1)}, f32[64,512]{1,0:T(8,128)S(1)}, u32[]{:S(2)}, u32[]{:S(2)}) collective-permute-start(f32[64,512]{1,0:T(8,128)S(1)} %get-tuple-element.28), channel_id=1, source_target_pairs={{0,16},{1,17},{2,18},{3,19},{4,12},{5,13},{6,14},{7,15},{8,24},{9,... | collective-permute-start | bytes 393224 | tf_op jit(solution)/shard_map/ppermute | solution.py:63
  26.6 5.1 %collective-permute-start.3 = (f32[32,512]{1,0:T(8,128)S(1)}, f32[32,512]{1,0:T(8,128)S(1)}, u32[]{:S(2)}, u32[]{:S(2)}) collective-permute-start(f32[32,512]{1,0:T(8,128)S(1)} %get-tuple-element.40), channel_id=1, source_target_pairs={{0,1},{1,0},{2,3},{3,2},{4,5},{5,4},{6,7},{7,6},{8,9},{9,8},{10,11... | collective-permute-start | bytes 196616 | tf_op jit(solution)/shard_map/ppermute | solution.py:63
  28.3 8.7 %collective-permute-start.11 = (f32[32,512]{1,0:T(8,128)S(1)}, f32[32,512]{1,0:T(8,128)S(1)}, u32[]{:S(2)}, u32[]{:S(2)}) collective-permute-start(f32[32,512]{1,0:T(8,128)S(1)} %get-tuple-element.38), channel_id=1, source_target_pairs={{0,1},{1,0},{2,3},{3,2},{4,5},{5,4},{6,7},{7,6},{8,9},{9,8},{10,11... | collective-permute-start | bytes 196616 | tf_op jit(solution)/shard_map/ppermute | solution.py:63
  31.7 10.6 %collective-permute-start.4 = (f32[16,512]{1,0:T(8,128)S(1)}, f32[16,512]{1,0:T(8,128)S(1)}, u32[]{:S(2)}, u32[]{:S(2)}) collective-permute-start(f32[16,512]{1,0:T(8,128)S(1)} %slice_add_fusion.18), channel_id=1, source_target_pairs={{0,2},{1,3},{2,0},{3,1},{4,6},{5,7},{6,4},{7,5},{8,10},{9,11},{10,... | collective-permute-start | bytes 98312 | tf_op jit(solution)/shard_map/ppermute | solution.py:63
  34.4 4.9 %collective-permute-start.20 = (f32[16,512]{1,0:T(8,128)S(1)}, f32[16,512]{1,0:T(8,128)S(1)}, u32[]{:S(2)}, u32[]{:S(2)}) collective-permute-start(f32[16,512]{1,0:T(8,128)S(1)} %slice_add_fusion.14), channel_id=1, source_target_pairs={{0,2},{1,3},{2,0},{3,1},{4,6},{5,7},{6,4},{7,5},{8,10},{9,11},{10,... | collective-permute-start | bytes 98312 | tf_op jit(solution)/shard_map/ppermute | solution.py:63
  37.0 5.2 %collective-permute-start.12 = (f32[16,512]{1,0:T(8,128)S(1)}, f32[16,512]{1,0:T(8,128)S(1)}, u32[]{:S(2)}, u32[]{:S(2)}) collective-permute-start(f32[16,512]{1,0:T(8,128)S(1)} %slice_add_fusion.16), channel_id=1, source_target_pairs={{0,2},{1,3},{2,0},{3,1},{4,6},{5,7},{6,4},{7,5},{8,10},{9,11},{10,... | collective-permute-start | bytes 98312 | tf_op jit(solution)/shard_map/ppermute | solution.py:63
  39.3 6.1 %collective-permute-start.21 = (f32[16,512]{1,0:T(8,128)S(1)}, f32[16,512]{1,0:T(8,128)S(1)}, u32[]{:S(2)}, u32[]{:S(2)}) collective-permute-start(f32[16,512]{1,0:T(8,128)S(1)} %get-tuple-element.22), channel_id=1, source_target_pairs={{0,2},{1,3},{2,0},{3,1},{4,6},{5,7},{6,4},{7,5},{8,10},{9,11},{10,... | collective-permute-start | bytes 98312 | tf_op jit(solution)/shard_map/ppermute | solution.py:63
  42.3 5.5 %collective-permute-start.13 = (f32[16,512]{1,0:T(8,128)S(1)}, f32[16,512]{1,0:T(8,128)S(1)}, u32[]{:S(2)}, u32[]{:S(2)}) collective-permute-start(f32[16,512]{1,0:T(8,128)S(1)} %get-tuple-element.24), channel_id=1, source_target_pairs={{0,2},{1,3},{2,0},{3,1},{4,6},{5,7},{6,4},{7,5},{8,10},{9,11},{10,... | collective-permute-start | bytes 98312 | tf_op jit(solution)/shard_map/ppermute | solution.py:63
  42.4 7.1 %collective-permute-start.5 = (f32[16,512]{1,0:T(8,128)S(1)}, f32[16,512]{1,0:T(8,128)S(1)}, u32[]{:S(2)}, u32[]{:S(2)}) collective-permute-start(f32[16,512]{1,0:T(8,128)S(1)} %get-tuple-element.26), channel_id=1, source_target_pairs={{0,2},{1,3},{2,0},{3,1},{4,6},{5,7},{6,4},{7,5},{8,10},{9,11},{10,... | collective-permute-start | bytes 98312 | tf_op jit(solution)/shard_map/ppermute | solution.py:63
  50.2 6.4 %collective-permute-start.23 = (f32[64,512]{1,0:T(8,128)S(1)}, f32[64,512]{1,0:T(8,128)S(1)}, u32[]{:S(2)}, u32[]{:S(2)}) collective-permute-start(f32[64,512]{1,0:T(8,128)S(1)} %pad_maximum_fusion.7), channel_id=1, source_target_pairs={{0,16},{1,17},{2,18},{3,19},{4,12},{5,13},{6,14},{7,15},{8,24},{9,... | collective-permute-start | bytes 393224 | tf_op jit(solution)/shard_map/ppermute | solution.py:63
  52.1 7.4 %collective-permute-start.15 = (f32[64,512]{1,0:T(8,128)S(1)}, f32[64,512]{1,0:T(8,128)S(1)}, u32[]{:S(2)}, u32[]{:S(2)}) collective-permute-start(f32[64,512]{1,0:T(8,128)S(1)} %pad_maximum_fusion.6), channel_id=1, source_target_pairs={{0,16},{1,17},{2,18},{3,19},{4,12},{5,13},{6,14},{7,15},{8,24},{9,... | collective-permute-start | bytes 393224 | tf_op jit(solution)/shard_map/ppermute | solution.py:63
  53.8 8.4 %collective-permute-start.7 = (f32[64,512]{1,0:T(8,128)S(1)}, f32[64,512]{1,0:T(8,128)S(1)}, u32[]{:S(2)}, u32[]{:S(2)}) collective-permute-start(f32[64,512]{1,0:T(8,128)S(1)} %pad_maximum_fusion.5), channel_id=1, source_target_pairs={{0,16},{1,17},{2,18},{3,19},{4,12},{5,13},{6,14},{7,15},{8,24},{9,... | collective-permute-start | bytes 393224 | tf_op jit(solution)/shard_map/ppermute | solution.py:63
  56.7 7.2 %collective-permute-start.24 = (f32[128,512]{1,0:T(8,128)S(1)}, f32[128,512]{1,0:T(8,128)S(1)}, u32[]{:S(2)}, u32[]{:S(2)}) collective-permute-start(f32[128,512]{1,0:T(8,128)S(1)} %pad_maximum_fusion.3), channel_id=1, source_target_pairs={{0,8},{1,9},{2,10},{3,11},{4,20},{5,21},{6,22},{7,23},{8,0},{9,1},... | collective-permute-start | bytes 786440 | tf_op jit(solution)/shard_map/ppermute | solution.py:63
  59.5 6.4 %collective-permute-start.16 = (f32[128,512]{1,0:T(8,128)S(1)}, f32[128,512]{1,0:T(8,128)S(1)}, u32[]{:S(2)}, u32[]{:S(2)}) collective-permute-start(f32[128,512]{1,0:T(8,128)S(1)} %pad_maximum_fusion.2), channel_id=1, source_target_pairs={{0,8},{1,9},{2,10},{3,11},{4,20},{5,21},{6,22},{7,23},{8,0},{9,1},... | collective-permute-start | bytes 786440 | tf_op jit(solution)/shard_map/ppermute | solution.py:63
  62.2 6.5 %collective-permute-start.8 = (f32[128,512]{1,0:T(8,128)S(1)}, f32[128,512]{1,0:T(8,128)S(1)}, u32[]{:S(2)}, u32[]{:S(2)}) collective-permute-start(f32[128,512]{1,0:T(8,128)S(1)} %pad_maximum_fusion.1), channel_id=1, source_target_pairs={{0,8},{1,9},{2,10},{3,11},{4,20},{5,21},{6,22},{7,23},{8,0},{9,1},... | collective-permute-start | bytes 786440 | tf_op jit(solution)/shard_map/ppermute | solution.py:63
  78.9 5.5 %collective-permute-start.26 = (f32[320,128]{1,0:T(8,128)}, f32[320,128]{1,0:T(8,128)S(1)}, u32[]{:S(2)}, u32[]{:S(2)}) collective-permute-start(f32[320,128]{1,0:T(8,128)} %get-tuple-element.20), channel_id=1, source_target_pairs={{0,8},{1,9},{2,10},{3,11},{4,20},{5,21},{6,22},{7,23},{8,0},{9,1},... | collective-permute-start | bytes 491528 | tf_op jit(solution)/shard_map/ppermute | solution.py:63
  94.3 5.4 %collective-permute-start.29 = (f32[160,128]{1,0:T(8,128)S(1)}, f32[160,128]{1,0:T(8,128)S(1)}, u32[]{:S(2)}, u32[]{:S(2)}) collective-permute-start(f32[160,128]{1,0:T(8,128)S(1)} %add.130), channel_id=1, source_target_pairs={{0,2},{1,3},{2,0},{3,1},{4,6},{5,7},{6,4},{7,5},{8,10},{9,11},{10,... | collective-permute-start | bytes 245768 | tf_op jit(solution)/shard_map/ppermute | solution.py:63
  99.8 5.2 %collective-permute-start.30 = (f32[160,128]{1,0:T(8,128)S(1)}, f32[160,128]{1,0:T(8,128)S(1)}, u32[]{:S(2)}, u32[]{:S(2)}) collective-permute-start(f32[160,128]{1,0:T(8,128)S(1)} %add.131), channel_id=1, source_target_pairs={{0,16},{1,17},{2,18},{3,19},{4,12},{5,13},{6,14},{7,15},{8,24},{9,... | collective-permute-start | bytes 245768 | tf_op jit(solution)/shard_map/ppermute | solution.py:63
  105.0 5.4 %collective-permute-start.31 = (f32[320,128]{1,0:T(8,128)S(1)}, f32[320,128]{1,0:T(8,128)S(1)}, u32[]{:S(2)}, u32[]{:S(2)}) collective-permute-start(f32[320,128]{1,0:T(8,128)S(1)} %pad_maximum_fusion.4), channel_id=1, source_target_pairs={{0,8},{1,9},{2,10},{3,11},{4,20},{5,21},{6,22},{7,23},{8,0},{9,1},... | collective-permute-start | bytes 491528 | tf_op jit(solution)/shard_map/ppermute | solution.py:63
  (19 other events, 65.3 us)

commit v2 on v1

--- a/solution.py
+++ b/solution.py
@@ -12,6 +12,7 @@
 TILE = 128
 PANEL = 32
 GROUP = 16
+VMEM_LIMIT = 16 << 20
 AXES = ("row", "col")
 NT = (((1,), (1,)), ((), ()))
 NN = (((1,), (0,)), ((), ()))
@@ -20,6 +21,22 @@
 
 def dot(a, b, dims):
     return lax.dot_general(a, b, dims, precision=HIGHEST, preferred_element_type=jnp.float32)
+
+
+def bf16_dot(a, b, dims):
+    return lax.dot_general(a, b, dims, preferred_element_type=jnp.float32)
+
+
+def split(x):
+    high = x.astype(jnp.bfloat16)
+    rest = x - high.astype(jnp.float32)
+    middle = rest.astype(jnp.bfloat16)
+    return high, middle, (rest - middle.astype(jnp.float32)).astype(jnp.bfloat16)
+
+
+def stacked(x, axis):
+    h, m, low = split(x)
+    return jnp.concatenate([h, h, m, h, low, m], axis=axis), jnp.concatenate([h, m, h, low, h, m], axis=axis)
 
 
 class Route:
@@ -119,17 +136,24 @@
     return blocks[:half], blocks[half:]
 
 
-def gram_kernel(parts, scale, where, p_ref, keep_ref, send_ref, acc):
-    count = p_ref.shape[0] // TILE
+def gram_kernel(parts, scale, where, mine_ref, other_ref, keep_ref, send_ref, own_ref, p, acc):
+    half, width = mine_ref.shape[0], own_ref.shape[1]
+    count = 2 * half // TILE
     lists = core_blocks(count)
     core, place = where[0], where[1]
+    here = pl.ds(pl.multiple_of(core * half, half), half)
+    there = pl.ds(pl.multiple_of((1 - core) * half, half), half)
+    p[here, :] = mine_ref[...]
+    p[there, :width] = other_ref[:, width:]
+    p[there, width:] = other_ref[:, :width]
+    own_ref[...] = p[:, :width]
     for n in range(len(lists[0])):
         first = lists[0][n]
         second = lists[1][min(n, len(lists[1]) - 1)]
         i = jnp.where(core == 0, first[0], second[0])
         j = jnp.where(core == 0, first[1], second[1])
-        a = p_ref[pl.ds(pl.multiple_of(i * TILE, TILE), TILE), :]
-        b = p_ref[pl.ds(pl.multiple_of(j * TILE, TILE), TILE), :]
+        a = p[pl.ds(pl.multiple_of(i * TILE, TILE), TILE), :]
+        b = p[pl.ds(pl.multiple_of(j * TILE, TILE), TILE), :]
         acc[n * TILE : (n + 1) * TILE, :] = dot(a, b, NT) * scale
     size = acc.shape[0] // parts
     for k in range(parts):
@@ -140,9 +164,9 @@
             send_ref[(k - parts // 2) * size : (k - parts // 2 + 1) * size, :] = rows
 
 
-def solve_kernel(parts, where, mine_ref, other_ref, p_ref, out_ref, natural, work):
+def solve_kernel(parts, where, mine_ref, other_ref, p_ref, out_ref, natural, work, stack_a, stack_b):
     n, tile = p_ref.shape[0], TILE
-    width = n + out_ref.shape[1]
+    width = n + p_ref.shape[1]
     count, groups, per_panel, panels = n // tile, width // tile, PANEL // 8, tile // PANEL
     core, size = where[0], mine_ref.shape[0] // parts
     for ref, number, place in ((mine_ref, core, where[1]), (other_ref, 1 - core, where[2])):
@@ -152,14 +176,14 @@
     for number, blocks in enumerate(core_blocks(count)):
         for at, (i, j) in enumerate(blocks):
             work[i * tile : (i + 1) * tile, j * tile : (j + 1) * tile] = natural[number, at * tile : (at + 1) * tile, :]
-    work[:, n:] = p_ref[:, : out_ref.shape[1]]
+    work[:, n:] = p_ref[...]
     sub = lax.broadcasted_iota(jnp.int32, (8, tile), 0)
-
-    def panel(r0, s):
-        base = r0 + PANEL * s
+    deep = 6 * PANEL
+
+    def panel(b, s):
+        base = b * tile + PANEL * s
         r = [
-            [work[pl.ds(base + 8 * i, 8), c * tile : (c + 1) * tile] for c in range(groups)]
-            + [work[pl.ds(base + 8 * i, 8), pl.ds(r0, tile)]]
+            [work[base + 8 * i : base + 8 * i + 8, c * tile : (c + 1) * tile] for c in range(b, groups)]
             for i in range(per_panel)
         ]
         scale = [jnp.zeros((8, tile), jnp.float32)] * per_panel
@@ -168,7 +192,7 @@
             if j % GROUP == 0:
                 cols = {
                     k: {
-                        i: jnp.broadcast_to(r[i][groups][:, PANEL * s + k : PANEL * s + k + 1], (8, tile))
+                        i: jnp.broadcast_to(r[i][0][:, PANEL * s + k : PANEL * s + k + 1], (8, tile))
                         for i in range(k // 8, per_panel)
                     }
                     for k in range(j, j + GROUP)
@@ -185,34 +209,32 @@
                 row = jnp.broadcast_to(col[k // 8][k % 8 : k % 8 + 1, :], (8, tile))
                 for i in range(k // 8, per_panel):
                     cols[k][i] = cols[k][i] - mult[i] * row
-            for c in range(groups + 1):
+            for c in range(groups - b):
                 row = jnp.broadcast_to(r[jb][c][js : js + 1, :], (8, tile))
                 for i in range(first, per_panel):
                     r[i][c] = r[i][c] - mult[i] * row
-        for i in range(per_panel):
-            for c in range(groups):
-                work[pl.ds(base + 8 * i, 8), c * tile : (c + 1) * tile] = r[i][c] * scale[i]
-        return jnp.concatenate([r[i][groups] * scale[i] for i in range(per_panel)], axis=0)
-
-    def block(b, carry):
-        r0 = pl.multiple_of(b * tile, tile)
+        return jnp.concatenate(
+            [jnp.concatenate([x * scale[i] for x in r[i]], axis=1) for i in range(per_panel)], axis=0
+        )
+
+    for b in range(count):
+        start = b * tile
         for s in range(panels):
-            left = panel(r0, s)
+            u = panel(b, s)
+            out_ref[start + PANEL * s : start + PANEL * (s + 1), :] = u[:, n - start :]
+            if b == count - 1 and s == panels - 1:
+                break
+            left, right = stacked(u, axis=0)
             if s < panels - 1:
                 low = PANEL * (s + 1)
-                update = dot(left, work[pl.ds(r0 + PANEL * s, PANEL), :], TN)
-                work[pl.ds(r0 + low, tile - low), :] -= update[low:, :]
-
-        def trail(i, inner):
-            at = pl.multiple_of(i * tile, tile)
-            work[pl.ds(at, tile), :] -= dot(work[pl.ds(r0, tile), pl.ds(at, tile)], work[pl.ds(r0, tile), :], TN)
-            return inner
-
-        lax.fori_loop(b + 1, count, trail, 0)
-        return carry
-
-    lax.fori_loop(0, count, block, 0)
-    out_ref[...] = work[:, n:]
+                update = bf16_dot(left[:, :tile], right, TN)
+                work[start + low : start + tile, start:] -= update[low:, :]
+            if b < count - 1:
+                stack_a[deep * s : deep * (s + 1), start:n] = left[:, : n - start]
+                stack_b[deep * s : deep * (s + 1), start:] = right
+        for i in range(b + 1, count):
+            at = i * tile
+            work[at : at + tile, at:] -= bf16_dot(stack_a[:, at : at + tile], stack_b[:, at:], TN)
 
 
 VMEM = pl.BlockSpec(memory_space=pltpu.VMEM)
@@ -231,6 +253,7 @@
         in_specs=[SMEM] + [VMEM] * (len(args) - 1),
         out_specs=jax.tree.map(lambda _: VMEM, out_shape),
         scratch_shapes=[pltpu.VMEM(s.shape, s.dtype) for s in scratch],
+        compiler_params=pltpu.CompilerParams(vmem_limit_bytes=VMEM_LIMIT),
     )(*args)
 
 
@@ -272,18 +295,17 @@
         peer,
     )
     other = swap(mine, route.core_perm())
-    other = jnp.concatenate([other[:, width:], other[:, :width]], axis=1)
-    predicted = jnp.where(core == 0, jnp.concatenate([mine, other]), jnp.concatenate([other, mine]))
 
     shares = (norb // TILE) * (norb // TILE + 1) // 2
     share = (shares + 1) // 2 * TILE
-    keep, send = call(
+    keep, send, predicted = call(
         functools.partial(gram_kernel, parts, 1.0 / total),
         "gram",
-        [f32(share // 2, TILE)] * 2,
-        [f32(share, TILE)],
+        [f32(share // 2, TILE)] * 2 + [f32(norb, width)],
+        [f32(norb, 2 * width), f32(share, TILE)],
         where_g,
-        predicted,
+        mine,
+        other,
     )
     gram = all_reduce(route, keep, send, parts_levels, levels)
     gram_other = swap(gram, route.core_perm())
@@ -291,7 +313,12 @@
         functools.partial(solve_kernel, parts),
         "solve",
         f32(norb, width),
-        [f32(2, share, TILE), f32(norb, norb + width)],
+        [
+            f32(2, share, TILE),
+            f32(norb, norb + width),
+            jax.ShapeDtypeStruct((6 * TILE, norb), jnp.bfloat16),
+            jax.ShapeDtypeStruct((6 * TILE, norb + width), jnp.bfloat16),
+        ],
         where_g,
         gram,
         gram_other,

time: 134 us -> 119 us (0.89)
  Pallas kernels: 32.6 us -> 21.5 us
  other arithmetic: 4.31 us -> 0.57 us
  waiting for transfers between devices: 39.9 us -> 42.2 us
    pallas_call x4, Pallas kernels: 32.6 us -> 21.5 us  [call(): pl.pallas_call(kernel, name=name, out_shape=out_shape, in_specs=[SMEM] +...]
    ppermute x33, waiting for transfers between devices: 39.9 us -> 42.2 us  [swap(): return lax.ppermute(x, AXES, perm)]
    add x10, other arithmetic: 2.1 us -> 0.21 us  [all_reduce(): keep, send = (keep[:half] + got[:half], keep[half:] + got[half:])]
  transfers between devices with their start and end apart: 33 -> 33, of which waited for: 20 -> 22; matrix products, arithmetic and copies ran while one was open for 2% -> 0% of each run, Pallas kernels for 0% -> 0%
where the time goes in v2:
time: 119 us
  starting transfers between devices  53.2 us (45%)
  waiting for transfers between devices  42.2 us (35%)
  Pallas kernels  21.5 us (18%)
  local copies, waits for them, and re-layouts  1.25 us (1%)
    ppermute x33, starting transfers between devices, swap(): return lax.ppermute(x, AXES, perm)  53.2 us
    ppermute x33, waiting for transfers between devices, swap(): return lax.ppermute(x, AXES, perm)  42.2 us
    pallas_call x4, Pallas kernels, call(): pl.pallas_call(kernel, name=name, out_shape=out_shape, in_specs=[SMEM] +...  21.5 us
  transfers between devices with their start and end apart: 33, of which 22 were waited for; matrix products, arithmetic and copies ran while one was open for 0% of the time, Pallas kernels for 0%

profile of v2, /device:TPU:0, one launch (start us, length us, event | category | flops | bytes accessed | tf_op | source)
XLA Modules:
  0.0 119.0 jit_solution(12658061857337242145)
XLA Ops:
  0.6 2.0 %collective-permute-done.peer_ref = f32[3,512,128]{2,1,0:T(8,128)S(1)} collective-permute-done((f32[3,512,128]{2,1,0:T(8,128)}, f32[3,512,128]{2,1,0:T(8,128)S(1)}, u32[]{:S(2)}, u32[]{:S(2)}) %collective-permute-start) | collective-permute-done | bytes 786464 | tf_op jit(solution)/shard_map/ppermute | solution.py:80
  3.8 3.8 %project.1 = (f32[128,512]{1,0:T(8,128)S(1)}, f32[128,512]{1,0:T(8,128)S(1)}, f32[128,512]{1,0:T(8,128)S(1)}, f32[128,512]{1,0:T(8,128)S(1)}, f32[128,512]{1,0:T(8,128)S(1)}, /*index=5*/f32[128,512]{1,0:T(8,128)S(1)}) custom-call(s32[2]{0:T(128)S(1)} %pad_add_fusion.1.where, f32[3,512,128]{2,1,0:T(8,128)S(1)} %copy-done, ...), custom_call_target="tpu_custom_call" | custom-call | tf_op jit(solution)/shard_map/project/pallas_call | solution.py:249
  7.5 2.9 %collective-permute-start.1 = (f32[128,512]{1,0:T(8,128)S(1)}, f32[128,512]{1,0:T(8,128)S(1)}, u32[]{:S(2)}, u32[]{:S(2)}) collective-permute-start(f32[128,512]{1,0:T(8,128)S(1)} %get-tuple-element.15), channel_id=1, source_target_pairs={{0,8},{1,9},{2,10},{3,11},{4,20},{5,21},{6,22},{7,23},{8,0},{9,1},... | collective-permute-start | bytes 786440 | tf_op jit(solution)/shard_map/ppermute | solution.py:80
  12.5 2.3 %collective-permute-done.1 = f32[128,512]{1,0:T(8,128)S(1)} collective-permute-done((f32[128,512]{1,0:T(8,128)S(1)}, f32[128,512]{1,0:T(8,128)S(1)}, u32[]{:S(2)}, u32[]{:S(2)}) %collective-permute-start.1) | collective-permute-done | bytes 262176 | tf_op jit(solution)/shard_map/ppermute | solution.py:80
  14.8 2.1 %collective-permute-start.2 = (f32[64,512]{1,0:T(8,128)S(1)}, f32[64,512]{1,0:T(8,128)S(1)}, u32[]{:S(2)}, u32[]{:S(2)}) collective-permute-start(f32[64,512]{1,0:T(8,128)S(1)} %get-tuple-element.34), channel_id=1, source_target_pairs={{0,16},{1,17},{2,18},{3,19},{4,12},{5,13},{6,14},{7,15},{8,24},{9,... | collective-permute-start | bytes 393224 | tf_op jit(solution)/shard_map/ppermute | solution.py:80
  18.2 2.4 %collective-permute-start.10 = (f32[64,512]{1,0:T(8,128)S(1)}, f32[64,512]{1,0:T(8,128)S(1)}, u32[]{:S(2)}, u32[]{:S(2)}) collective-permute-start(f32[64,512]{1,0:T(8,128)S(1)} %get-tuple-element.32), channel_id=1, source_target_pairs={{0,16},{1,17},{2,18},{3,19},{4,12},{5,13},{6,14},{7,15},{8,24},{9,... | collective-permute-start | bytes 393224 | tf_op jit(solution)/shard_map/ppermute | solution.py:80
  20.6 2.6 %collective-permute-done.17 = f32[128,512]{1,0:T(8,128)S(1)} collective-permute-done((f32[128,512]{1,0:T(8,128)S(1)}, f32[128,512]{1,0:T(8,128)S(1)}, u32[]{:S(2)}, u32[]{:S(2)}) %collective-permute-start.17) | collective-permute-done | bytes 262176 | tf_op jit(solution)/shard_map/ppermute | solution.py:80
  23.3 2.1 %collective-permute-start.18 = (f32[64,512]{1,0:T(8,128)S(1)}, f32[64,512]{1,0:T(8,128)S(1)}, u32[]{:S(2)}, u32[]{:S(2)}) collective-permute-start(f32[64,512]{1,0:T(8,128)S(1)} %get-tuple-element.30), channel_id=1, source_target_pairs={{0,16},{1,17},{2,18},{3,19},{4,12},{5,13},{6,14},{7,15},{8,24},{9,... | collective-permute-start | bytes 393224 | tf_op jit(solution)/shard_map/ppermute | solution.py:80
  28.3 2.1 %collective-permute-start.19 = (f32[32,512]{1,0:T(8,128)S(1)}, f32[32,512]{1,0:T(8,128)S(1)}, u32[]{:S(2)}, u32[]{:S(2)}) collective-permute-start(f32[32,512]{1,0:T(8,128)S(1)} %get-tuple-element.36), channel_id=1, source_target_pairs={{0,1},{1,0},{2,3},{3,2},{4,5},{5,4},{6,7},{7,6},{8,9},{9,8},{10,11... | collective-permute-start | bytes 196616 | tf_op jit(solution)/shard_map/ppermute | solution.py:80
  30.5 2.7 %collective-permute-start.4 = (f32[16,512]{1,0:T(8,128)S(1)}, f32[16,512]{1,0:T(8,128)S(1)}, u32[]{:S(2)}, u32[]{:S(2)}) collective-permute-start(f32[16,512]{1,0:T(8,128)S(1)} %slice_add_fusion.18), channel_id=1, source_target_pairs={{0,2},{1,3},{2,0},{3,1},{4,6},{5,7},{6,4},{7,5},{8,10},{9,11},{10,... | collective-permute-start | bytes 98312 | tf_op jit(solution)/shard_map/ppermute | solution.py:80
  33.2 2.6 %collective-permute-start.20 = (f32[16,512]{1,0:T(8,128)S(1)}, f32[16,512]{1,0:T(8,128)S(1)}, u32[]{:S(2)}, u32[]{:S(2)}) collective-permute-start(f32[16,512]{1,0:T(8,128)S(1)} %slice_add_fusion.14), channel_id=1, source_target_pairs={{0,2},{1,3},{2,0},{3,1},{4,6},{5,7},{6,4},{7,5},{8,10},{9,11},{10,... | collective-permute-start | bytes 98312 | tf_op jit(solution)/shard_map/ppermute | solution.py:80
  38.0 2.6 %collective-permute-start.21 = (f32[16,512]{1,0:T(8,128)S(1)}, f32[16,512]{1,0:T(8,128)S(1)}, u32[]{:S(2)}, u32[]{:S(2)}) collective-permute-start(f32[16,512]{1,0:T(8,128)S(1)} %get-tuple-element.24), channel_id=1, source_target_pairs={{0,2},{1,3},{2,0},{3,1},{4,6},{5,7},{6,4},{7,5},{8,10},{9,11},{10,... | collective-permute-start | bytes 98312 | tf_op jit(solution)/shard_map/ppermute | solution.py:80
  41.1 3.0 %collective-permute-start.5 = (f32[16,512]{1,0:T(8,128)S(1)}, f32[16,512]{1,0:T(8,128)S(1)}, u32[]{:S(2)}, u32[]{:S(2)}) collective-permute-start(f32[16,512]{1,0:T(8,128)S(1)} %get-tuple-element.28), channel_id=1, source_target_pairs={{0,2},{1,3},{2,0},{3,1},{4,6},{5,7},{6,4},{7,5},{8,10},{9,11},{10,... | collective-permute-start | bytes 98312 | tf_op jit(solution)/shard_map/ppermute | solution.py:80
  44.1 2.4 %collective-permute-start.22 = (f32[32,512]{1,0:T(8,128)S(1)}, f32[32,512]{1,0:T(8,128)S(1)}, u32[]{:S(2)}, u32[]{:S(2)}) collective-permute-start(f32[32,512]{1,0:T(8,128)S(1)} %pad_maximum_fusion.10), channel_id=1, source_target_pairs={{0,1},{1,0},{2,3},{3,2},{4,5},{5,4},{6,7},{7,6},{8,9},{9,8},{10,11... | collective-permute-start | bytes 196616 | tf_op jit(solution)/shard_map/ppermute | solution.py:80
  64.7 2.8 %collective-permute-done.8 = f32[128,512]{1,0:T(8,128)S(1)} collective-permute-done((f32[128,512]{1,0:T(8,128)S(1)}, f32[128,512]{1,0:T(8,128)S(1)}, u32[]{:S(2)}, u32[]{:S(2)}) %collective-permute-start.8) | collective-permute-done | bytes 262176 | tf_op jit(solution)/shard_map/ppermute | solution.py:80
  67.5 2.1 %predict.1.mine_ref = f32[256,256]{1,0:T(8,128)S(1)} custom-call(s32[2]{0:T(128)S(1)} %pad_add_fusion.1.where, f32[256,512]{1,0:T(8,128)S(1)} %constant_dynamic-update-slice_fusion.m0, f32[256,512]{1,0:T(8,128)S(1)} %constant_dynamic-update-slice_fusion.5.m1, f32[256,512]{1,0:T(8,128)S(1)} %constant_dynamic-update-slice_fusion.10.m2, ...), custom_call_target="tpu_custom_call" | custom-call | tf_op jit(solution)/shard_map/predict/pallas_call | solution.py:249
  74.4 3.5 %collective-permute-done.26 = f32[320,128]{1,0:T(8,128)S(1)} collective-permute-done((f32[320,128]{1,0:T(8,128)S(1)}, f32[320,128]{1,0:T(8,128)S(1)}, u32[]{:S(2)}, u32[]{:S(2)}) %collective-permute-start.26) | collective-permute-done | bytes 163872 | tf_op jit(solution)/shard_map/ppermute | solution.py:80
  79.4 3.1 %collective-permute-done.27 = f32[160,128]{1,0:T(8,128)S(1)} collective-permute-done((f32[160,128]{1,0:T(8,128)S(1)}, f32[160,128]{1,0:T(8,128)S(1)}, u32[]{:S(2)}, u32[]{:S(2)}) %collective-permute-start.27) | collective-permute-done | bytes 81952 | tf_op jit(solution)/shard_map/ppermute | solution.py:80
  84.3 2.7 %collective-permute-done.28 = f32[160,128]{1,0:T(8,128)S(1)} collective-permute-done((f32[160,128]{1,0:T(8,128)S(1)}, f32[160,128]{1,0:T(8,128)S(1)}, u32[]{:S(2)}, u32[]{:S(2)}) %collective-permute-start.28) | collective-permute-done | bytes 81952 | tf_op jit(solution)/shard_map/ppermute | solution.py:80
  87.0 2.4 %collective-permute-start.29 = (f32[160,128]{1,0:T(8,128)S(1)}, f32[160,128]{1,0:T(8,128)S(1)}, u32[]{:S(2)}, u32[]{:S(2)}) collective-permute-start(f32[160,128]{1,0:T(8,128)S(1)} %add.130), channel_id=1, source_target_pairs={{0,2},{1,3},{2,0},{3,1},{4,6},{5,7},{6,4},{7,5},{8,10},{9,11},{10,... | collective-permute-start | bytes 245768 | tf_op jit(solution)/shard_map/ppermute | solution.py:80
  89.4 3.0 %collective-permute-done.29 = f32[160,128]{1,0:T(8,128)S(1)} collective-permute-done((f32[160,128]{1,0:T(8,128)S(1)}, f32[160,128]{1,0:T(8,128)S(1)}, u32[]{:S(2)}, u32[]{:S(2)}) %collective-permute-start.29) | collective-permute-done | bytes 81952 | tf_op jit(solution)/shard_map/ppermute | solution.py:80
  93.8 3.7 %collective-permute-done.30 = f32[160,128]{1,0:T(8,128)S(1)} collective-permute-done((f32[160,128]{1,0:T(8,128)S(1)}, f32[160,128]{1,0:T(8,128)S(1)}, u32[]{:S(2)}, u32[]{:S(2)}) %collective-permute-start.30) | collective-permute-done | bytes 81952 | tf_op jit(solution)/shard_map/ppermute | solution.py:80
  99.4 3.6 %collective-permute-done.31 = f32[320,128]{1,0:T(8,128)S(1)} collective-permute-done((f32[320,128]{1,0:T(8,128)S(1)}, f32[320,128]{1,0:T(8,128)S(1)}, u32[]{:S(2)}, u32[]{:S(2)}) %collective-permute-start.31) | collective-permute-done | bytes 163872 | tf_op jit(solution)/shard_map/ppermute | solution.py:80
  104.7 14.3 %solve.1 = f32[512,128]{1,0:T(8,128)} custom-call(s32[3]{0:T(128)S(1)} %pad_add_fusion.where, f32[640,128]{1,0:T(8,128)S(1)} %pad_maximum_fusion.mine_ref, f32[640,128]{1,0:T(8,128)S(1)} %collective-permute-done.32.other_ref, f32[512,128]{1,0:T(8,128)S(1)} %get-tuple-element.22.p_ref), custom_call_target="tpu_custom_call" | custom-call | tf_op jit(solution)/shard_map/solve/pallas_call | solution.py:249
  (89 shorter events, 41.8 us)
Async XLA Ops:
  7.5 7.3 %collective-permute-start.1 = (f32[128,512]{1,0:T(8,128)S(1)}, f32[128,512]{1,0:T(8,128)S(1)}, u32[]{:S(2)}, u32[]{:S(2)}) collective-permute-start(f32[128,512]{1,0:T(8,128)S(1)} %get-tuple-element.15), channel_id=1, source_target_pairs={{0,8},{1,9},{2,10},{3,11},{4,20},{5,21},{6,22},{7,23},{8,0},{9,1},... | collective-permute-start | bytes 786440 | tf_op jit(solution)/shard_map/ppermute | solution.py:80
  10.4 7.7 %collective-permute-start.9 = (f32[128,512]{1,0:T(8,128)S(1)}, f32[128,512]{1,0:T(8,128)S(1)}, u32[]{:S(2)}, u32[]{:S(2)}) collective-permute-start(f32[128,512]{1,0:T(8,128)S(1)} %get-tuple-element.17), channel_id=1, source_target_pairs={{0,8},{1,9},{2,10},{3,11},{4,20},{5,21},{6,22},{7,23},{8,0},{9,1},... | collective-permute-start | bytes 786440 | tf_op jit(solution)/shard_map/ppermute | solution.py:80
  10.5 12.7 %collective-permute-start.17 = (f32[128,512]{1,0:T(8,128)S(1)}, f32[128,512]{1,0:T(8,128)S(1)}, u32[]{:S(2)}, u32[]{:S(2)}) collective-permute-start(f32[128,512]{1,0:T(8,128)S(1)} %get-tuple-element.19), channel_id=1, source_target_pairs={{0,8},{1,9},{2,10},{3,11},{4,20},{5,21},{6,22},{7,23},{8,0},{9,1},... | collective-permute-start | bytes 786440 | tf_op jit(solution)/shard_map/ppermute | solution.py:80
  14.8 10.5 %collective-permute-start.2 = (f32[64,512]{1,0:T(8,128)S(1)}, f32[64,512]{1,0:T(8,128)S(1)}, u32[]{:S(2)}, u32[]{:S(2)}) collective-permute-start(f32[64,512]{1,0:T(8,128)S(1)} %get-tuple-element.34), channel_id=1, source_target_pairs={{0,16},{1,17},{2,18},{3,19},{4,12},{5,13},{6,14},{7,15},{8,24},{9,... | collective-permute-start | bytes 393224 | tf_op jit(solution)/shard_map/ppermute | solution.py:80
  18.2 8.9 %collective-permute-start.10 = (f32[64,512]{1,0:T(8,128)S(1)}, f32[64,512]{1,0:T(8,128)S(1)}, u32[]{:S(2)}, u32[]{:S(2)}) collective-permute-start(f32[64,512]{1,0:T(8,128)S(1)} %get-tuple-element.32), channel_id=1, source_target_pairs={{0,16},{1,17},{2,18},{3,19},{4,12},{5,13},{6,14},{7,15},{8,24},{9,... | collective-permute-start | bytes 393224 | tf_op jit(solution)/shard_map/ppermute | solution.py:80
  23.3 5.1 %collective-permute-start.18 = (f32[64,512]{1,0:T(8,128)S(1)}, f32[64,512]{1,0:T(8,128)S(1)}, u32[]{:S(2)}, u32[]{:S(2)}) collective-permute-start(f32[64,512]{1,0:T(8,128)S(1)} %get-tuple-element.30), channel_id=1, source_target_pairs={{0,16},{1,17},{2,18},{3,19},{4,12},{5,13},{6,14},{7,15},{8,24},{9,... | collective-permute-start | bytes 393224 | tf_op jit(solution)/shard_map/ppermute | solution.py:80
  25.4 5.1 %collective-permute-start.3 = (f32[32,512]{1,0:T(8,128)S(1)}, f32[32,512]{1,0:T(8,128)S(1)}, u32[]{:S(2)}, u32[]{:S(2)}) collective-permute-start(f32[32,512]{1,0:T(8,128)S(1)} %get-tuple-element.40), channel_id=1, source_target_pairs={{0,1},{1,0},{2,3},{3,2},{4,5},{5,4},{6,7},{7,6},{8,9},{9,8},{10,11... | collective-permute-start | bytes 196616 | tf_op jit(solution)/shard_map/ppermute | solution.py:80
  27.1 8.7 %collective-permute-start.11 = (f32[32,512]{1,0:T(8,128)S(1)}, f32[32,512]{1,0:T(8,128)S(1)}, u32[]{:S(2)}, u32[]{:S(2)}) collective-permute-start(f32[32,512]{1,0:T(8,128)S(1)} %get-tuple-element.38), channel_id=1, source_target_pairs={{0,1},{1,0},{2,3},{3,2},{4,5},{5,4},{6,7},{7,6},{8,9},{9,8},{10,11... | collective-permute-start | bytes 196616 | tf_op jit(solution)/shard_map/ppermute | solution.py:80
  30.5 10.6 %collective-permute-start.4 = (f32[16,512]{1,0:T(8,128)S(1)}, f32[16,512]{1,0:T(8,128)S(1)}, u32[]{:S(2)}, u32[]{:S(2)}) collective-permute-start(f32[16,512]{1,0:T(8,128)S(1)} %slice_add_fusion.18), channel_id=1, source_target_pairs={{0,2},{1,3},{2,0},{3,1},{4,6},{5,7},{6,4},{7,5},{8,10},{9,11},{10,... | collective-permute-start | bytes 98312 | tf_op jit(solution)/shard_map/ppermute | solution.py:80
  33.2 4.9 %collective-permute-start.20 = (f32[16,512]{1,0:T(8,128)S(1)}, f32[16,512]{1,0:T(8,128)S(1)}, u32[]{:S(2)}, u32[]{:S(2)}) collective-permute-start(f32[16,512]{1,0:T(8,128)S(1)} %slice_add_fusion.14), channel_id=1, source_target_pairs={{0,2},{1,3},{2,0},{3,1},{4,6},{5,7},{6,4},{7,5},{8,10},{9,11},{10,... | collective-permute-start | bytes 98312 | tf_op jit(solution)/shard_map/ppermute | solution.py:80
  35.8 5.2 %collective-permute-start.12 = (f32[16,512]{1,0:T(8,128)S(1)}, f32[16,512]{1,0:T(8,128)S(1)}, u32[]{:S(2)}, u32[]{:S(2)}) collective-permute-start(f32[16,512]{1,0:T(8,128)S(1)} %slice_add_fusion.16), channel_id=1, source_target_pairs={{0,2},{1,3},{2,0},{3,1},{4,6},{5,7},{6,4},{7,5},{8,10},{9,11},{10,... | collective-permute-start | bytes 98312 | tf_op jit(solution)/shard_map/ppermute | solution.py:80
  38.0 6.0 %collective-permute-start.21 = (f32[16,512]{1,0:T(8,128)S(1)}, f32[16,512]{1,0:T(8,128)S(1)}, u32[]{:S(2)}, u32[]{:S(2)}) collective-permute-start(f32[16,512]{1,0:T(8,128)S(1)} %get-tuple-element.24), channel_id=1, source_target_pairs={{0,2},{1,3},{2,0},{3,1},{4,6},{5,7},{6,4},{7,5},{8,10},{9,11},{10,... | collective-permute-start | bytes 98312 | tf_op jit(solution)/shard_map/ppermute | solution.py:80
  41.0 5.5 %collective-permute-start.13 = (f32[16,512]{1,0:T(8,128)S(1)}, f32[16,512]{1,0:T(8,128)S(1)}, u32[]{:S(2)}, u32[]{:S(2)}) collective-permute-start(f32[16,512]{1,0:T(8,128)S(1)} %get-tuple-element.26), channel_id=1, source_target_pairs={{0,2},{1,3},{2,0},{3,1},{4,6},{5,7},{6,4},{7,5},{8,10},{9,11},{10,... | collective-permute-start | bytes 98312 | tf_op jit(solution)/shard_map/ppermute | solution.py:80
  41.1 7.1 %collective-permute-start.5 = (f32[16,512]{1,0:T(8,128)S(1)}, f32[16,512]{1,0:T(8,128)S(1)}, u32[]{:S(2)}, u32[]{:S(2)}) collective-permute-start(f32[16,512]{1,0:T(8,128)S(1)} %get-tuple-element.28), channel_id=1, source_target_pairs={{0,2},{1,3},{2,0},{3,1},{4,6},{5,7},{6,4},{7,5},{8,10},{9,11},{10,... | collective-permute-start | bytes 98312 | tf_op jit(solution)/shard_map/ppermute | solution.py:80
  49.0 6.4 %collective-permute-start.23 = (f32[64,512]{1,0:T(8,128)S(1)}, f32[64,512]{1,0:T(8,128)S(1)}, u32[]{:S(2)}, u32[]{:S(2)}) collective-permute-start(f32[64,512]{1,0:T(8,128)S(1)} %pad_maximum_fusion.7), channel_id=1, source_target_pairs={{0,16},{1,17},{2,18},{3,19},{4,12},{5,13},{6,14},{7,15},{8,24},{9,... | collective-permute-start | bytes 393224 | tf_op jit(solution)/shard_map/ppermute | solution.py:80
  50.8 7.4 %collective-permute-start.15 = (f32[64,512]{1,0:T(8,128)S(1)}, f32[64,512]{1,0:T(8,128)S(1)}, u32[]{:S(2)}, u32[]{:S(2)}) collective-permute-start(f32[64,512]{1,0:T(8,128)S(1)} %pad_maximum_fusion.6), channel_id=1, source_target_pairs={{0,16},{1,17},{2,18},{3,19},{4,12},{5,13},{6,14},{7,15},{8,24},{9,... | collective-permute-start | bytes 393224 | tf_op jit(solution)/shard_map/ppermute | solution.py:80
  52.6 8.5 %collective-permute-start.7 = (f32[64,512]{1,0:T(8,128)S(1)}, f32[64,512]{1,0:T(8,128)S(1)}, u32[]{:S(2)}, u32[]{:S(2)}) collective-permute-start(f32[64,512]{1,0:T(8,128)S(1)} %pad_maximum_fusion.5), channel_id=1, source_target_pairs={{0,16},{1,17},{2,18},{3,19},{4,12},{5,13},{6,14},{7,15},{8,24},{9,... | collective-permute-start | bytes 393224 | tf_op jit(solution)/shard_map/ppermute | solution.py:80
  55.4 7.5 %collective-permute-start.24 = (f32[128,512]{1,0:T(8,128)S(1)}, f32[128,512]{1,0:T(8,128)S(1)}, u32[]{:S(2)}, u32[]{:S(2)}) collective-permute-start(f32[128,512]{1,0:T(8,128)S(1)} %pad_maximum_fusion.3), channel_id=1, source_target_pairs={{0,8},{1,9},{2,10},{3,11},{4,20},{5,21},{6,22},{7,23},{8,0},{9,1},... | collective-permute-start | bytes 786440 | tf_op jit(solution)/shard_map/ppermute | solution.py:80
  58.3 6.4 %collective-permute-start.16 = (f32[128,512]{1,0:T(8,128)S(1)}, f32[128,512]{1,0:T(8,128)S(1)}, u32[]{:S(2)}, u32[]{:S(2)}) collective-permute-start(f32[128,512]{1,0:T(8,128)S(1)} %pad_maximum_fusion.2), channel_id=1, source_target_pairs={{0,8},{1,9},{2,10},{3,11},{4,20},{5,21},{6,22},{7,23},{8,0},{9,1},... | collective-permute-start | bytes 786440 | tf_op jit(solution)/shard_map/ppermute | solution.py:80
  61.1 6.4 %collective-permute-start.8 = (f32[128,512]{1,0:T(8,128)S(1)}, f32[128,512]{1,0:T(8,128)S(1)}, u32[]{:S(2)}, u32[]{:S(2)}) collective-permute-start(f32[128,512]{1,0:T(8,128)S(1)} %pad_maximum_fusion.1), channel_id=1, source_target_pairs={{0,8},{1,9},{2,10},{3,11},{4,20},{5,21},{6,22},{7,23},{8,0},{9,1},... | collective-permute-start | bytes 786440 | tf_op jit(solution)/shard_map/ppermute | solution.py:80
  72.6 5.4 %collective-permute-start.26 = (f32[320,128]{1,0:T(8,128)S(1)}, f32[320,128]{1,0:T(8,128)S(1)}, u32[]{:S(2)}, u32[]{:S(2)}) collective-permute-start(f32[320,128]{1,0:T(8,128)S(1)} %get-tuple-element.21), channel_id=1, source_target_pairs={{0,8},{1,9},{2,10},{3,11},{4,20},{5,21},{6,22},{7,23},{8,0},{9,1},... | collective-permute-start | bytes 491528 | tf_op jit(solution)/shard_map/ppermute | solution.py:80
  87.0 5.4 %collective-permute-start.29 = (f32[160,128]{1,0:T(8,128)S(1)}, f32[160,128]{1,0:T(8,128)S(1)}, u32[]{:S(2)}, u32[]{:S(2)}) collective-permute-start(f32[160,128]{1,0:T(8,128)S(1)} %add.130), channel_id=1, source_target_pairs={{0,2},{1,3},{2,0},{3,1},{4,6},{5,7},{6,4},{7,5},{8,10},{9,11},{10,... | collective-permute-start | bytes 245768 | tf_op jit(solution)/shard_map/ppermute | solution.py:80
  92.4 5.1 %collective-permute-start.30 = (f32[160,128]{1,0:T(8,128)S(1)}, f32[160,128]{1,0:T(8,128)S(1)}, u32[]{:S(2)}, u32[]{:S(2)}) collective-permute-start(f32[160,128]{1,0:T(8,128)S(1)} %add.131), channel_id=1, source_target_pairs={{0,16},{1,17},{2,18},{3,19},{4,12},{5,13},{6,14},{7,15},{8,24},{9,... | collective-permute-start | bytes 245768 | tf_op jit(solution)/shard_map/ppermute | solution.py:80
  97.6 5.4 %collective-permute-start.31 = (f32[320,128]{1,0:T(8,128)S(1)}, f32[320,128]{1,0:T(8,128)S(1)}, u32[]{:S(2)}, u32[]{:S(2)}) collective-permute-start(f32[320,128]{1,0:T(8,128)S(1)} %pad_maximum_fusion.4), channel_id=1, source_target_pairs={{0,8},{1,9},{2,10},{3,11},{4,20},{5,21},{6,22},{7,23},{8,0},{9,1},... | collective-permute-start | bytes 491528 | tf_op jit(solution)/shard_map/ppermute | solution.py:80
  (10 other events, 34.4 us)

commit v3 on v2

--- a/solution.py
+++ b/solution.py
@@ -56,14 +56,21 @@
         c = self.cols
         return [(r * c + k, (r ^ 1) * c + k) for r in range(self.rows) for k in range(c)]
 
-    def perm(self, level):
+    def perm(self, *levels):
         pairs = []
         for r in range(self.rows):
             for k in range(self.cols):
-                axis, bit = self.orders[r & 1][level]
-                to = (r ^ (1 << bit), k) if axis == "row" else (r, k ^ (1 << bit))
-                pairs.append((r * self.cols + k, to[0] * self.cols + to[1]))
+                flip = {"row": 0, "col": 0}
+                for level in levels:
+                    axis, bit = self.orders[r & 1][level]
+                    flip[axis] ^= 1 << bit
+                pairs.append((r * self.cols + k, (r ^ flip["row"]) * self.cols + (k ^ flip["col"])))
         return pairs
+
+    def perms(self, first, count):
+        return [
+            self.perm(*[first + i for i in range(count) if q >> (count - 1 - i) & 1]) for q in range(1, 1 << count)
+        ]
 
     def place(self, core, levels):
         index = {"row": lax.axis_index("row"), "col": lax.axis_index("col")}
@@ -95,39 +102,48 @@
     return keep
 
 
-def project_kernel(blocks, where, own_ref, peer_ref, *refs):
-    outs, (left, right) = refs[:-2], refs[-2:]
-    rows, width = left.shape[0], own_ref.shape[2]
+def phases(first, last):
+    return [(level, min(2, last - level)) for level in range(first, last, 2)]
+
+
+def direct_all_reduce(route, pieces, scatter, levels):
+    for number, (level, count) in enumerate(phases(0, scatter)):
+        if number > 0:
+            size = keep.shape[0] >> count
+            pieces = [keep[q * size : (q + 1) * size] for q in range(1 << count)]
+        got = [swap(piece, perm) for piece, perm in zip(pieces[1:], route.perms(level, count))]
+        keep = functools.reduce(jnp.add, got, pieces[0])
+    for level, count in phases(scatter, levels):
+        keep = functools.reduce(jnp.add, [swap(keep, perm) for perm in route.perms(level, count)], keep)
+    for level, count in reversed(phases(0, scatter)):
+        keep = jnp.concatenate([keep] + [swap(keep, perm) for perm in route.perms(level, count)])
+    return keep
+
+
+def arrange_kernel(blocks, where, own_ref, peer_ref, out_ref, left):
+    rows, width = left.shape[0], own_ref.shape[1]
     core, place = where[0], where[1]
     size = rows // blocks
     for k in range(blocks):
         at = pl.multiple_of(core * rows + (place ^ k) * size, size)
-        left[k * size : (k + 1) * size, :width] = own_ref[0, pl.ds(at, size), :]
-        left[k * size : (k + 1) * size, width:] = peer_ref[0, pl.ds(at, size), :]
-    for j in range(own_ref.shape[0]):
-        right[:, :width] = own_ref[j]
-        right[:, width:] = peer_ref[j]
-        keep, send = outs[2 * j], outs[2 * j + 1]
-        half = keep.shape[0]
-        keep[...] = dot(left[:half, :], right[...], NT)
-        send[...] = dot(left[half:, :], right[...], NT)
-
-
-def predict_kernel(blocks, scales, where, m0, m1, m2, own_ref, peer_ref, out_ref, both, acc):
-    rows, width = m0.shape[0], own_ref.shape[2]
-    size = rows // blocks
-    for j, m in enumerate((m0, m1, m2)):
-        both[:, :width] = own_ref[j]
-        both[:, width:] = peer_ref[j]
-        term = dot(m[...], both[...], NN) * scales[j]
-        if j == 0:
-            acc[...] = term
-        else:
-            acc[...] += term
-    place = where[1]
-    for k in range(blocks):
-        at = pl.multiple_of((place ^ k) * size, size)
-        out_ref[pl.ds(at, size), :] = acc[k * size : (k + 1) * size, :]
+        left[k * size : (k + 1) * size, :width] = own_ref[pl.ds(at, size), :]
+        left[k * size : (k + 1) * size, width:] = peer_ref[pl.ds(at, size), :]
+    out_ref[...] = stacked(left[...], axis=1)[0]
+
+
+def project_kernel(left_ref, own_ref, peer_ref, keep_ref, send_ref):
+    half = keep_ref.shape[0]
+    right = stacked(jnp.concatenate([own_ref[...], peer_ref[...]], axis=1), axis=1)[1]
+    keep_ref[...] = bf16_dot(left_ref[:half, :], right, NT)
+    send_ref[...] = bf16_dot(left_ref[half:, :], right, NT)
+
+
+def predict_kernel(scale, m_ref, own_ref, peer_ref, *refs):
+    out_ref = refs[-1]
+    left = stacked(m_ref[...], axis=1)[0]
+    right = stacked(jnp.concatenate([own_ref[...], peer_ref[...]], axis=1), axis=0)[1]
+    term = bf16_dot(left, right, NN) * scale
+    out_ref[...] = term + refs[0][...] if len(refs) > 1 else term
 
 
 def core_blocks(count):
@@ -136,7 +152,14 @@
     return blocks[:half], blocks[half:]
 
 
-def gram_kernel(parts, scale, where, mine_ref, other_ref, keep_ref, send_ref, own_ref, p, acc):
+def restore_kernel(blocks, where, in_ref, out_ref):
+    size = in_ref.shape[0] // blocks
+    for k in range(blocks):
+        out_ref[pl.ds(pl.multiple_of((where[1] ^ k) * size, size), size), :] = in_ref[k * size : (k + 1) * size, :]
+
+
+def gram_kernel(parts, scale, where, mine_ref, other_ref, *refs):
+    outs, own_ref, p, acc = refs[:-3], refs[-3], refs[-2], refs[-1]
     half, width = mine_ref.shape[0], own_ref.shape[1]
     count = 2 * half // TILE
     lists = core_blocks(count)
@@ -157,11 +180,8 @@
         acc[n * TILE : (n + 1) * TILE, :] = dot(a, b, NT) * scale
     size = acc.shape[0] // parts
     for k in range(parts):
-        rows = acc[pl.ds(pl.multiple_of((place ^ k) * size, 8), size), :]
-        if k < parts // 2:
-            keep_ref[k * size : (k + 1) * size, :] = rows
-        else:
-            send_ref[(k - parts // 2) * size : (k - parts // 2 + 1) * size, :] = rows
+        each = parts // len(outs)
+        outs[k // each][k % each * size : (k % each + 1) * size, :] = acc[pl.ds(pl.multiple_of((place ^ k) * size, 8), size), :]
 
 
 def solve_kernel(parts, where, mine_ref, other_ref, p_ref, out_ref, natural, work, stack_a, stack_b):
@@ -245,16 +265,16 @@
     return jax.ShapeDtypeStruct(shape, jnp.float32)
 
 
-def call(kernel, name, out_shape, scratch, *args):
+def call(kernel, name, out_shape, scratch, args, scalars=None):
     return pl.pallas_call(
         kernel,
         name=name,
         out_shape=out_shape,
-        in_specs=[SMEM] + [VMEM] * (len(args) - 1),
+        in_specs=([] if scalars is None else [SMEM]) + [VMEM] * len(args),
         out_specs=jax.tree.map(lambda _: VMEM, out_shape),
         scratch_shapes=[pltpu.VMEM(s.shape, s.dtype) for s in scratch],
         compiler_params=pltpu.CompilerParams(vmem_limit_bytes=VMEM_LIMIT),
-    )(*args)
+    )(*([] if scalars is None else [scalars]), *args)
 
 
 def on_device(rows, cols, history):
@@ -272,42 +292,39 @@
     parts = 1 << parts_levels
     where_g = jnp.stack([core, route.place(core, parts_levels), route.place(1 - core, parts_levels)])
 
-    peer = swap(history, route.core_perm())
-    quarter = half // 2
-    products = call(
-        functools.partial(project_kernel, blocks),
-        "project",
-        [f32(quarter, norb)] * (2 * terms),
-        [f32(half, 2 * width), f32(norb, 2 * width)],
+    own = [history[j] for j in range(terms)]
+    peer = [swap(h, route.core_perm()) for h in own]
+    left = call(
+        functools.partial(arrange_kernel, blocks),
+        "arrange",
+        jax.ShapeDtypeStruct((half, 12 * width), jnp.bfloat16),
+        [f32(half, 2 * width)],
+        [own[0], peer[0]],
         where_m,
-        history,
-        peer,
     )
-    m = [all_reduce(route, products[2 * j], products[2 * j + 1], scatter, levels) for j in range(terms)]
-    mine = call(
-        functools.partial(predict_kernel, blocks, tuple(w / total for w in WEIGHTS)),
-        "predict",
-        f32(half, 2 * width),
-        [f32(norb, 2 * width), f32(half, 2 * width)],
-        where_m,
-        *m,
-        history,
-        peer,
-    )
+    m = []
+    for j in range(terms):
+        keep, send = call(project_kernel, "project", [f32(half // 2, norb)] * 2, [], [left, own[j], peer[j]])
+        m.append(all_reduce(route, keep, send, scatter, levels))
+    mine = []
+    for j in range(terms):
+        scale = WEIGHTS[j] / total
+        mine = [call(functools.partial(predict_kernel, scale), "predict", f32(half, 2 * width), [], [m[j], own[j], peer[j]] + mine)]
+    mine = call(functools.partial(restore_kernel, blocks), "restore", f32(half, 2 * width), [], mine, where_m)
     other = swap(mine, route.core_perm())
 
     shares = (norb // TILE) * (norb // TILE + 1) // 2
     share = (shares + 1) // 2 * TILE
-    keep, send, predicted = call(
+    ways = 1 << min(2, parts_levels)
+    *pieces, predicted = call(
         functools.partial(gram_kernel, parts, 1.0 / total),
         "gram",
-        [f32(share // 2, TILE)] * 2 + [f32(norb, width)],
+        [f32(share // ways, TILE)] * ways + [f32(norb, width)],
         [f32(norb, 2 * width), f32(share, TILE)],
+        [mine, other],
         where_g,
-        mine,
-        other,
     )
-    gram = all_reduce(route, keep, send, parts_levels, levels)
+    gram = direct_all_reduce(route, pieces, parts_levels, levels)
     gram_other = swap(gram, route.core_perm())
     return call(
         functools.partial(solve_kernel, parts),
@@ -319,10 +336,8 @@
             jax.ShapeDtypeStruct((6 * TILE, norb), jnp.bfloat16),
             jax.ShapeDtypeStruct((6 * TILE, norb + width), jnp.bfloat16),
         ],
+        [gram, gram_other, predicted],
         where_g,
-        gram,
-        gram_other,
-        predicted,
     )
 
 

time: 119 us -> 107 us (0.90)
  waiting for transfers between devices: 42.2 us -> 33.1 us
  starting transfers between devices: 53.2 us -> 49.8 us
    ppermute x33 -> x38, waiting for transfers between devices: 42.2 us -> 33.1 us  [swap(): return lax.ppermute(x, AXES, perm)]
    ppermute x33 -> x38, starting transfers between devices: 53.2 us -> 49.8 us  [swap(): return lax.ppermute(x, AXES, perm)]
    pallas_call x4 -> x10, Pallas kernels: 21.5 us -> 22.1 us  [call(): pl.pallas_call(kernel, name=name, out_shape=out_shape, in_specs=([] if sc...]
  transfers between devices with their start and end apart: 33 -> 38, of which waited for: 22 -> 24; matrix products, arithmetic and copies ran while one was open for 0% -> 1% of each run, Pallas kernels for 0% -> 5%
where the time goes in v3:
time: 107 us
  starting transfers between devices  49.8 us (47%)
  waiting for transfers between devices  33.1 us (31%)
  Pallas kernels  22.1 us (21%)
  local copies, waits for them, and re-layouts  1.28 us (1%)
    ppermute x38, starting transfers between devices, swap(): return lax.ppermute(x, AXES, perm)  49.8 us
    ppermute x38, waiting for transfers between devices, swap(): return lax.ppermute(x, AXES, perm)  33.1 us
    pallas_call x10, Pallas kernels, call(): pl.pallas_call(kernel, name=name, out_shape=out_shape, in_specs=([] if sc...  22.1 us
  transfers between devices with their start and end apart: 38, of which 24 were waited for; matrix products, arithmetic and copies ran while one was open for 1% of the time, Pallas kernels for 5%

profile of v3, /device:TPU:0, one launch (start us, length us, event | category | flops | bytes accessed | tf_op | source)
XLA Modules:
  0.0 107.2 jit_solution(2966676816891402466)
XLA Ops:
  4.7 2.9 %collective-permute-start.19 = (f32[128,512]{1,0:T(8,128)S(1)}, f32[128,512]{1,0:T(8,128)S(1)}, u32[]{:S(2)}, u32[]{:S(2)}) collective-permute-start(f32[128,512]{1,0:T(8,128)S(1)} %get-tuple-element.21), channel_id=1, source_target_pairs={{0,8},{1,9},{2,10},{3,11},{4,20},{5,21},{6,22},{7,23},{8,0},{9,1},... | collective-permute-start | bytes 786440 | tf_op jit(solution)/shard_map/ppermute | solution.py:87
  10.0 2.1 %collective-permute-start.2 = (f32[128,512]{1,0:T(8,128)S(1)}, f32[128,512]{1,0:T(8,128)S(1)}, u32[]{:S(2)}, u32[]{:S(2)}) collective-permute-start(f32[128,512]{1,0:T(8,128)S(1)} %get-tuple-element.17), channel_id=1, source_target_pairs={{0,8},{1,9},{2,10},{3,11},{4,20},{5,21},{6,22},{7,23},{8,0},{9,1},... | collective-permute-start | bytes 786440 | tf_op jit(solution)/shard_map/ppermute | solution.py:87
  12.1 2.0 %collective-permute-start.20 = (f32[64,512]{1,0:T(8,128)S(1)}, f32[64,512]{1,0:T(8,128)S(1)}, u32[]{:S(2)}, u32[]{:S(2)}) collective-permute-start(f32[64,512]{1,0:T(8,128)S(1)} %get-tuple-element.37), channel_id=1, source_target_pairs={{0,16},{1,17},{2,18},{3,19},{4,12},{5,13},{6,14},{7,15},{8,24},{9,... | collective-permute-start | bytes 393224 | tf_op jit(solution)/shard_map/ppermute | solution.py:87
  14.1 2.1 %collective-permute-done.11 = f32[128,512]{1,0:T(8,128)S(1)} collective-permute-done((f32[128,512]{1,0:T(8,128)S(1)}, f32[128,512]{1,0:T(8,128)S(1)}, u32[]{:S(2)}, u32[]{:S(2)}) %collective-permute-start.11) | collective-permute-done | bytes 262176 | tf_op jit(solution)/shard_map/ppermute | solution.py:87
  17.7 3.1 %collective-permute-done.2 = f32[128,512]{1,0:T(8,128)S(1)} collective-permute-done((f32[128,512]{1,0:T(8,128)S(1)}, f32[128,512]{1,0:T(8,128)S(1)}, u32[]{:S(2)}, u32[]{:S(2)}) %collective-permute-start.2) | collective-permute-done | bytes 262176 | tf_op jit(solution)/shard_map/ppermute | solution.py:87
  20.9 1.7 %collective-permute-start.3 = (f32[64,512]{1,0:T(8,128)S(1)}, f32[64,512]{1,0:T(8,128)S(1)}, u32[]{:S(2)}, u32[]{:S(2)}) collective-permute-start(f32[64,512]{1,0:T(8,128)S(1)} %get-tuple-element.41), channel_id=1, source_target_pairs={{0,16},{1,17},{2,18},{3,19},{4,12},{5,13},{6,14},{7,15},{8,24},{9,... | collective-permute-start | bytes 393224 | tf_op jit(solution)/shard_map/ppermute | solution.py:87
  22.5 1.6 %collective-permute-start.21 = (f32[32,512]{1,0:T(8,128)S(1)}, f32[32,512]{1,0:T(8,128)S(1)}, u32[]{:S(2)}, u32[]{:S(2)}) collective-permute-start(f32[32,512]{1,0:T(8,128)S(1)} %get-tuple-element.43), channel_id=1, source_target_pairs={{0,1},{1,0},{2,3},{3,2},{4,5},{5,4},{6,7},{7,6},{8,9},{9,8},{10,11... | collective-permute-start | bytes 196616 | tf_op jit(solution)/shard_map/ppermute | solution.py:87
  25.9 1.7 %collective-permute-start.4 = (f32[32,512]{1,0:T(8,128)S(1)}, f32[32,512]{1,0:T(8,128)S(1)}, u32[]{:S(2)}, u32[]{:S(2)}) collective-permute-start(f32[32,512]{1,0:T(8,128)S(1)} %get-tuple-element.47), channel_id=1, source_target_pairs={{0,1},{1,0},{2,3},{3,2},{4,5},{5,4},{6,7},{7,6},{8,9},{9,8},{10,11... | collective-permute-start | bytes 196616 | tf_op jit(solution)/shard_map/ppermute | solution.py:87
  27.6 2.7 %collective-permute-start.22 = (f32[16,512]{1,0:T(8,128)S(1)}, f32[16,512]{1,0:T(8,128)S(1)}, u32[]{:S(2)}, u32[]{:S(2)}) collective-permute-start(f32[16,512]{1,0:T(8,128)S(1)} %slice_add_fusion.12), channel_id=1, source_target_pairs={{0,2},{1,3},{2,0},{3,1},{4,6},{5,7},{6,4},{7,5},{8,10},{9,11},{10,... | collective-permute-start | bytes 98312 | tf_op jit(solution)/shard_map/ppermute | solution.py:87
  31.8 1.6 %collective-permute-start.5 = (f32[16,512]{1,0:T(8,128)S(1)}, f32[16,512]{1,0:T(8,128)S(1)}, u32[]{:S(2)}, u32[]{:S(2)}) collective-permute-start(f32[16,512]{1,0:T(8,128)S(1)} %slice_add_fusion.16), channel_id=1, source_target_pairs={{0,2},{1,3},{2,0},{3,1},{4,6},{5,7},{6,4},{7,5},{8,10},{9,11},{10,... | collective-permute-start | bytes 98312 | tf_op jit(solution)/shard_map/ppermute | solution.py:87
  33.5 1.9 %collective-permute-start.23 = (f32[16,512]{1,0:T(8,128)S(1)}, f32[16,512]{1,0:T(8,128)S(1)}, u32[]{:S(2)}, u32[]{:S(2)}) collective-permute-start(f32[16,512]{1,0:T(8,128)S(1)} %get-tuple-element.28), channel_id=1, source_target_pairs={{0,2},{1,3},{2,0},{3,1},{4,6},{5,7},{6,4},{7,5},{8,10},{9,11},{10,... | collective-permute-start | bytes 98312 | tf_op jit(solution)/shard_map/ppermute | solution.py:87
  37.1 2.2 %collective-permute-start.6 = (f32[16,512]{1,0:T(8,128)S(1)}, f32[16,512]{1,0:T(8,128)S(1)}, u32[]{:S(2)}, u32[]{:S(2)}) collective-permute-start(f32[16,512]{1,0:T(8,128)S(1)} %get-tuple-element.32), channel_id=1, source_target_pairs={{0,2},{1,3},{2,0},{3,1},{4,6},{5,7},{6,4},{7,5},{8,10},{9,11},{10,... | collective-permute-start | bytes 98312 | tf_op jit(solution)/shard_map/ppermute | solution.py:87
  47.6 2.5 %collective-permute-done.25 = f32[64,512]{1,0:T(8,128)S(1)} collective-permute-done((f32[64,512]{1,0:T(8,128)S(1)}, f32[64,512]{1,0:T(8,128)S(1)}, u32[]{:S(2)}, u32[]{:S(2)}) %collective-permute-start.25) | collective-permute-done | bytes 131104 | tf_op jit(solution)/shard_map/ppermute | solution.py:87
  50.1 1.8 %collective-permute-start.26 = (f32[128,512]{1,0:T(8,128)S(1)}, f32[128,512]{1,0:T(8,128)S(1)}, u32[]{:S(2)}, u32[]{:S(2)}) collective-permute-start(f32[128,512]{1,0:T(8,128)S(1)} %pad_maximum_fusion.3), channel_id=1, source_target_pairs={{0,8},{1,9},{2,10},{3,11},{4,20},{5,21},{6,22},{7,23},{8,0},{9,1},... | collective-permute-start | bytes 786440 | tf_op jit(solution)/shard_map/ppermute | solution.py:87
  52.9 1.8 %collective-permute-start.18 = (f32[128,512]{1,0:T(8,128)S(1)}, f32[128,512]{1,0:T(8,128)S(1)}, u32[]{:S(2)}, u32[]{:S(2)}) collective-permute-start(f32[128,512]{1,0:T(8,128)S(1)} %pad_maximum_fusion.2), channel_id=1, source_target_pairs={{0,8},{1,9},{2,10},{3,11},{4,20},{5,21},{6,22},{7,23},{8,0},{9,1},... | collective-permute-start | bytes 786440 | tf_op jit(solution)/shard_map/ppermute | solution.py:87
  55.7 1.8 %collective-permute-start.9 = (f32[128,512]{1,0:T(8,128)S(1)}, f32[128,512]{1,0:T(8,128)S(1)}, u32[]{:S(2)}, u32[]{:S(2)}) collective-permute-start(f32[128,512]{1,0:T(8,128)S(1)} %pad_maximum_fusion.1), channel_id=1, source_target_pairs={{0,8},{1,9},{2,10},{3,11},{4,20},{5,21},{6,22},{7,23},{8,0},{9,1},... | collective-permute-start | bytes 786440 | tf_op jit(solution)/shard_map/ppermute | solution.py:87
  60.0 2.2 %collective-permute-done.9 = f32[128,512]{1,0:T(8,128)S(1)} collective-permute-done((f32[128,512]{1,0:T(8,128)S(1)}, f32[128,512]{1,0:T(8,128)S(1)}, u32[]{:S(2)}, u32[]{:S(2)}) %collective-permute-start.9) | collective-permute-done | bytes 262176 | tf_op jit(solution)/shard_map/ppermute | solution.py:87
  72.1 2.2 %collective-permute-done.30 = f32[160,128]{1,0:T(8,128)S(1)} collective-permute-done((f32[160,128]{1,0:T(8,128)S(1)}, f32[160,128]{1,0:T(8,128)S(1)}, u32[]{:S(2)}, u32[]{:S(2)}) %collective-permute-start.30) | collective-permute-done | bytes 81952 | tf_op jit(solution)/shard_map/ppermute | solution.py:87
  74.3 1.7 %collective-permute-start.31 = (f32[160,128]{1,0:T(8,128)S(1)}, f32[160,128]{1,0:T(8,128)S(1)}, u32[]{:S(2)}, u32[]{:S(2)}) collective-permute-start(f32[160,128]{1,0:T(8,128)S(1)} %add_add_fusion.1), channel_id=1, source_target_pairs={{0,2},{1,3},{2,0},{3,1},{4,6},{5,7},{6,4},{7,5},{8,10},{9,11},{10,... | collective-permute-start | bytes 245768 | tf_op jit(solution)/shard_map/ppermute | solution.py:87
  78.8 3.3 %collective-permute-done.31 = f32[160,128]{1,0:T(8,128)S(1)} collective-permute-done((f32[160,128]{1,0:T(8,128)S(1)}, f32[160,128]{1,0:T(8,128)S(1)}, u32[]{:S(2)}, u32[]{:S(2)}) %collective-permute-start.31) | collective-permute-done | bytes 81952 | tf_op jit(solution)/shard_map/ppermute | solution.py:87
  83.6 1.8 %collective-permute-start.34 = (f32[160,128]{1,0:T(8,128)S(1)}, f32[160,128]{1,0:T(8,128)S(1)}, u32[]{:S(2)}, u32[]{:S(2)}) collective-permute-start(f32[160,128]{1,0:T(8,128)S(1)} %add_add_fusion), channel_id=1, source_target_pairs={{0,16},{1,17},{2,18},{3,19},{4,12},{5,13},{6,14},{7,15},{8,24},{9,... | collective-permute-start | bytes 245768 | tf_op jit(solution)/shard_map/ppermute | solution.py:87
  87.1 1.8 %collective-permute-done.34 = f32[160,128]{1,0:T(8,128)S(1)} collective-permute-done((f32[160,128]{1,0:T(8,128)S(1)}, f32[160,128]{1,0:T(8,128)S(1)}, u32[]{:S(2)}, u32[]{:S(2)}) %collective-permute-start.34) | collective-permute-done | bytes 81952 | tf_op jit(solution)/shard_map/ppermute | solution.py:87
  91.2 1.6 %collective-permute-done.37.other_ref = f32[640,128]{1,0:T(8,128)S(1)} collective-permute-done((f32[640,128]{1,0:T(8,128)S(1)}, f32[640,128]{1,0:T(8,128)S(1)}, u32[]{:S(2)}, u32[]{:S(2)}) %collective-permute-start.37) | collective-permute-done | bytes 327712 | tf_op jit(solution)/shard_map/ppermute | solution.py:87
  92.8 14.3 %solve.1 = f32[512,128]{1,0:T(8,128)} custom-call(s32[3]{0:T(128)S(1)} %pad_add_fusion.where, f32[640,128]{1,0:T(8,128)S(1)} %pad_maximum_fusion.mine_ref, f32[640,128]{1,0:T(8,128)S(1)} %collective-permute-done.37.other_ref, f32[512,128]{1,0:T(8,128)S(1)} %get-tuple-element.26.p_ref), custom_call_target="tpu_custom_call" | custom-call | tf_op jit(solution)/shard_map/solve/pallas_call | solution.py:269
  (101 shorter events, 44.4 us)
Async XLA Ops:
  1.7 5.9 %collective-permute-start.10 = (f32[512,128]{1,0:T(8,128)S(1)}, f32[512,128]{1,0:T(8,128)S(1)}, u32[]{:S(2)}, u32[]{:S(2)}) collective-permute-start(f32[512,128]{1,0:T(8,128)S(1)} %get-tuple-element.33.own_ref), channel_id=1, source_target_pairs={{0,4},{1,5},{2,6},{3,7},{4,0},{5,1},{6,2},{7,3},{8,12},{9,13},{10,... | collective-permute-start | bytes 786440 | tf_op jit(solution)/shard_map/ppermute | solution.py:87
  1.8 7.0 %collective-permute-start.1 = (f32[512,128]{1,0:T(8,128)S(1)}, f32[512,128]{1,0:T(8,128)S(1)}, u32[]{:S(2)}, u32[]{:S(2)}) collective-permute-start(f32[512,128]{1,0:T(8,128)S(1)} %get-tuple-element.35.own_ref), channel_id=1, source_target_pairs={{0,4},{1,5},{2,6},{3,7},{4,0},{5,1},{6,2},{7,3},{8,12},{9,13},{10,... | collective-permute-start | bytes 786440 | tf_op jit(solution)/shard_map/ppermute | solution.py:87
  4.7 7.4 %collective-permute-start.19 = (f32[128,512]{1,0:T(8,128)S(1)}, f32[128,512]{1,0:T(8,128)S(1)}, u32[]{:S(2)}, u32[]{:S(2)}) collective-permute-start(f32[128,512]{1,0:T(8,128)S(1)} %get-tuple-element.21), channel_id=1, source_target_pairs={{0,8},{1,9},{2,10},{3,11},{4,20},{5,21},{6,22},{7,23},{8,0},{9,1},... | collective-permute-start | bytes 786440 | tf_op jit(solution)/shard_map/ppermute | solution.py:87
  8.8 7.4 %collective-permute-start.11 = (f32[128,512]{1,0:T(8,128)S(1)}, f32[128,512]{1,0:T(8,128)S(1)}, u32[]{:S(2)}, u32[]{:S(2)}) collective-permute-start(f32[128,512]{1,0:T(8,128)S(1)} %get-tuple-element.19), channel_id=1, source_target_pairs={{0,8},{1,9},{2,10},{3,11},{4,20},{5,21},{6,22},{7,23},{8,0},{9,1},... | collective-permute-start | bytes 786440 | tf_op jit(solution)/shard_map/ppermute | solution.py:87
  10.0 10.8 %collective-permute-start.2 = (f32[128,512]{1,0:T(8,128)S(1)}, f32[128,512]{1,0:T(8,128)S(1)}, u32[]{:S(2)}, u32[]{:S(2)}) collective-permute-start(f32[128,512]{1,0:T(8,128)S(1)} %get-tuple-element.17), channel_id=1, source_target_pairs={{0,8},{1,9},{2,10},{3,11},{4,20},{5,21},{6,22},{7,23},{8,0},{9,1},... | collective-permute-start | bytes 786440 | tf_op jit(solution)/shard_map/ppermute | solution.py:87
  12.1 10.4 %collective-permute-start.20 = (f32[64,512]{1,0:T(8,128)S(1)}, f32[64,512]{1,0:T(8,128)S(1)}, u32[]{:S(2)}, u32[]{:S(2)}) collective-permute-start(f32[64,512]{1,0:T(8,128)S(1)} %get-tuple-element.37), channel_id=1, source_target_pairs={{0,16},{1,17},{2,18},{3,19},{4,12},{5,13},{6,14},{7,15},{8,24},{9,... | collective-permute-start | bytes 393224 | tf_op jit(solution)/shard_map/ppermute | solution.py:87
  16.2 8.0 %collective-permute-start.12 = (f32[64,512]{1,0:T(8,128)S(1)}, f32[64,512]{1,0:T(8,128)S(1)}, u32[]{:S(2)}, u32[]{:S(2)}) collective-permute-start(f32[64,512]{1,0:T(8,128)S(1)} %get-tuple-element.39), channel_id=1, source_target_pairs={{0,16},{1,17},{2,18},{3,19},{4,12},{5,13},{6,14},{7,15},{8,24},{9,... | collective-permute-start | bytes 393224 | tf_op jit(solution)/shard_map/ppermute | solution.py:87
  24.2 6.1 %collective-permute-start.13 = (f32[32,512]{1,0:T(8,128)S(1)}, f32[32,512]{1,0:T(8,128)S(1)}, u32[]{:S(2)}, u32[]{:S(2)}) collective-permute-start(f32[32,512]{1,0:T(8,128)S(1)} %get-tuple-element.45), channel_id=1, source_target_pairs={{0,1},{1,0},{2,3},{3,2},{4,5},{5,4},{6,7},{7,6},{8,9},{9,8},{10,11... | collective-permute-start | bytes 196616 | tf_op jit(solution)/shard_map/ppermute | solution.py:87
  25.9 5.9 %collective-permute-start.4 = (f32[32,512]{1,0:T(8,128)S(1)}, f32[32,512]{1,0:T(8,128)S(1)}, u32[]{:S(2)}, u32[]{:S(2)}) collective-permute-start(f32[32,512]{1,0:T(8,128)S(1)} %get-tuple-element.47), channel_id=1, source_target_pairs={{0,1},{1,0},{2,3},{3,2},{4,5},{5,4},{6,7},{7,6},{8,9},{9,8},{10,11... | collective-permute-start | bytes 196616 | tf_op jit(solution)/shard_map/ppermute | solution.py:87
  27.6 5.8 %collective-permute-start.22 = (f32[16,512]{1,0:T(8,128)S(1)}, f32[16,512]{1,0:T(8,128)S(1)}, u32[]{:S(2)}, u32[]{:S(2)}) collective-permute-start(f32[16,512]{1,0:T(8,128)S(1)} %slice_add_fusion.12), channel_id=1, source_target_pairs={{0,2},{1,3},{2,0},{3,1},{4,6},{5,7},{6,4},{7,5},{8,10},{9,11},{10,... | collective-permute-start | bytes 98312 | tf_op jit(solution)/shard_map/ppermute | solution.py:87
  30.3 5.9 %collective-permute-start.14 = (f32[16,512]{1,0:T(8,128)S(1)}, f32[16,512]{1,0:T(8,128)S(1)}, u32[]{:S(2)}, u32[]{:S(2)}) collective-permute-start(f32[16,512]{1,0:T(8,128)S(1)} %slice_add_fusion.14), channel_id=1, source_target_pairs={{0,2},{1,3},{2,0},{3,1},{4,6},{5,7},{6,4},{7,5},{8,10},{9,11},{10,... | collective-permute-start | bytes 98312 | tf_op jit(solution)/shard_map/ppermute | solution.py:87
  33.5 5.8 %collective-permute-start.23 = (f32[16,512]{1,0:T(8,128)S(1)}, f32[16,512]{1,0:T(8,128)S(1)}, u32[]{:S(2)}, u32[]{:S(2)}) collective-permute-start(f32[16,512]{1,0:T(8,128)S(1)} %get-tuple-element.28), channel_id=1, source_target_pairs={{0,2},{1,3},{2,0},{3,1},{4,6},{5,7},{6,4},{7,5},{8,10},{9,11},{10,... | collective-permute-start | bytes 98312 | tf_op jit(solution)/shard_map/ppermute | solution.py:87
  43.6 6.4 %collective-permute-start.25 = (f32[64,512]{1,0:T(8,128)S(1)}, f32[64,512]{1,0:T(8,128)S(1)}, u32[]{:S(2)}, u32[]{:S(2)}) collective-permute-start(f32[64,512]{1,0:T(8,128)S(1)} %pad_maximum_fusion.6), channel_id=1, source_target_pairs={{0,16},{1,17},{2,18},{3,19},{4,12},{5,13},{6,14},{7,15},{8,24},{9,... | collective-permute-start | bytes 393224 | tf_op jit(solution)/shard_map/ppermute | solution.py:87
  45.4 7.5 %collective-permute-start.17 = (f32[64,512]{1,0:T(8,128)S(1)}, f32[64,512]{1,0:T(8,128)S(1)}, u32[]{:S(2)}, u32[]{:S(2)}) collective-permute-start(f32[64,512]{1,0:T(8,128)S(1)} %pad_maximum_fusion.5), channel_id=1, source_target_pairs={{0,16},{1,17},{2,18},{3,19},{4,12},{5,13},{6,14},{7,15},{8,24},{9,... | collective-permute-start | bytes 393224 | tf_op jit(solution)/shard_map/ppermute | solution.py:87
  46.7 9.0 %collective-permute-start.8 = (f32[64,512]{1,0:T(8,128)S(1)}, f32[64,512]{1,0:T(8,128)S(1)}, u32[]{:S(2)}, u32[]{:S(2)}) collective-permute-start(f32[64,512]{1,0:T(8,128)S(1)} %pad_maximum_fusion.4), channel_id=1, source_target_pairs={{0,16},{1,17},{2,18},{3,19},{4,12},{5,13},{6,14},{7,15},{8,24},{9,... | collective-permute-start | bytes 393224 | tf_op jit(solution)/shard_map/ppermute | solution.py:87
  50.1 7.5 %collective-permute-start.26 = (f32[128,512]{1,0:T(8,128)S(1)}, f32[128,512]{1,0:T(8,128)S(1)}, u32[]{:S(2)}, u32[]{:S(2)}) collective-permute-start(f32[128,512]{1,0:T(8,128)S(1)} %pad_maximum_fusion.3), channel_id=1, source_target_pairs={{0,8},{1,9},{2,10},{3,11},{4,20},{5,21},{6,22},{7,23},{8,0},{9,1},... | collective-permute-start | bytes 786440 | tf_op jit(solution)/shard_map/ppermute | solution.py:87
  52.9 6.4 %collective-permute-start.18 = (f32[128,512]{1,0:T(8,128)S(1)}, f32[128,512]{1,0:T(8,128)S(1)}, u32[]{:S(2)}, u32[]{:S(2)}) collective-permute-start(f32[128,512]{1,0:T(8,128)S(1)} %pad_maximum_fusion.2), channel_id=1, source_target_pairs={{0,8},{1,9},{2,10},{3,11},{4,20},{5,21},{6,22},{7,23},{8,0},{9,1},... | collective-permute-start | bytes 786440 | tf_op jit(solution)/shard_map/ppermute | solution.py:87
  55.7 6.4 %collective-permute-start.9 = (f32[128,512]{1,0:T(8,128)S(1)}, f32[128,512]{1,0:T(8,128)S(1)}, u32[]{:S(2)}, u32[]{:S(2)}) collective-permute-start(f32[128,512]{1,0:T(8,128)S(1)} %pad_maximum_fusion.1), channel_id=1, source_target_pairs={{0,8},{1,9},{2,10},{3,11},{4,20},{5,21},{6,22},{7,23},{8,0},{9,1},... | collective-permute-start | bytes 786440 | tf_op jit(solution)/shard_map/ppermute | solution.py:87
  69.0 5.3 %collective-permute-start.30 = (f32[160,128]{1,0:T(8,128)S(1)}, f32[160,128]{1,0:T(8,128)S(1)}, u32[]{:S(2)}, u32[]{:S(2)}) collective-permute-start(f32[160,128]{1,0:T(8,128)S(1)} %get-tuple-element.25), channel_id=1, source_target_pairs={{0,24},{1,25},{2,26},{3,27},{4,28},{5,29},{6,30},{7,31},{8,16},{9,... | collective-permute-start | bytes 245768 | tf_op jit(solution)/shard_map/ppermute | solution.py:87
  74.3 7.7 %collective-permute-start.31 = (f32[160,128]{1,0:T(8,128)S(1)}, f32[160,128]{1,0:T(8,128)S(1)}, u32[]{:S(2)}, u32[]{:S(2)}) collective-permute-start(f32[160,128]{1,0:T(8,128)S(1)} %add_add_fusion.1), channel_id=1, source_target_pairs={{0,2},{1,3},{2,0},{3,1},{4,6},{5,7},{6,4},{7,5},{8,10},{9,11},{10,... | collective-permute-start | bytes 245768 | tf_op jit(solution)/shard_map/ppermute | solution.py:87
  76.0 6.0 %collective-permute-start.32 = (f32[160,128]{1,0:T(8,128)S(1)}, f32[160,128]{1,0:T(8,128)S(1)}, u32[]{:S(2)}, u32[]{:S(2)}) collective-permute-start(f32[160,128]{1,0:T(8,128)S(1)} %add_add_fusion.1), channel_id=1, source_target_pairs={{0,1},{1,0},{2,3},{3,2},{4,5},{5,4},{6,7},{7,6},{8,9},{9,8},{10,11... | collective-permute-start | bytes 245768 | tf_op jit(solution)/shard_map/ppermute | solution.py:87
  77.3 6.2 %collective-permute-start.33 = (f32[160,128]{1,0:T(8,128)S(1)}, f32[160,128]{1,0:T(8,128)S(1)}, u32[]{:S(2)}, u32[]{:S(2)}) collective-permute-start(f32[160,128]{1,0:T(8,128)S(1)} %add_add_fusion.1), channel_id=1, source_target_pairs={{0,3},{1,2},{2,1},{3,0},{4,7},{5,6},{6,5},{7,4},{8,11},{9,10},{10,... | collective-permute-start | bytes 245768 | tf_op jit(solution)/shard_map/ppermute | solution.py:87
  83.6 5.4 %collective-permute-start.34 = (f32[160,128]{1,0:T(8,128)S(1)}, f32[160,128]{1,0:T(8,128)S(1)}, u32[]{:S(2)}, u32[]{:S(2)}) collective-permute-start(f32[160,128]{1,0:T(8,128)S(1)} %add_add_fusion), channel_id=1, source_target_pairs={{0,16},{1,17},{2,18},{3,19},{4,12},{5,13},{6,14},{7,15},{8,24},{9,... | collective-permute-start | bytes 245768 | tf_op jit(solution)/shard_map/ppermute | solution.py:87
  85.8 5.3 %collective-permute-start.36 = (f32[160,128]{1,0:T(8,128)S(1)}, f32[160,128]{1,0:T(8,128)S(1)}, u32[]{:S(2)}, u32[]{:S(2)}) collective-permute-start(f32[160,128]{1,0:T(8,128)S(1)} %add_add_fusion), channel_id=1, source_target_pairs={{0,24},{1,25},{2,26},{3,27},{4,28},{5,29},{6,30},{7,31},{8,16},{9,... | collective-permute-start | bytes 245768 | tf_op jit(solution)/shard_map/ppermute | solution.py:87
  (14 other events, 57.2 us)

commit v4 on v3

--- a/solution.py
+++ b/solution.py
@@ -12,6 +12,7 @@
 TILE = 128
 PANEL = 32
 GROUP = 16
+CHUNKS = 2
 VMEM_LIMIT = 16 << 20
 AXES = ("row", "col")
 NT = (((1,), (1,)), ((), ()))
@@ -131,19 +132,35 @@
     out_ref[...] = stacked(left[...], axis=1)[0]
 
 
-def project_kernel(left_ref, own_ref, peer_ref, keep_ref, send_ref):
-    half = keep_ref.shape[0]
-    right = stacked(jnp.concatenate([own_ref[...], peer_ref[...]], axis=1), axis=1)[1]
-    keep_ref[...] = bf16_dot(left_ref[:half, :], right, NT)
-    send_ref[...] = bf16_dot(left_ref[half:, :], right, NT)
-
-
-def predict_kernel(scale, m_ref, own_ref, peer_ref, *refs):
-    out_ref = refs[-1]
-    left = stacked(m_ref[...], axis=1)[0]
-    right = stacked(jnp.concatenate([own_ref[...], peer_ref[...]], axis=1), axis=0)[1]
-    term = bf16_dot(left, right, NN) * scale
-    out_ref[...] = term + refs[0][...] if len(refs) > 1 else term
+def project_kernel(pieces, left_ref, *refs):
+    ins, (keep_ref, send_ref) = refs[:-2], refs[-2:]
+    half, at = keep_ref.shape[0], 0
+    for n, (low, high) in enumerate(pieces):
+        x = jnp.concatenate([ins[2 * n][low:high, :], ins[2 * n + 1][low:high, :]], axis=1)
+        right = stacked(x, axis=1)[1]
+        keep_ref[:, at : at + high - low] = bf16_dot(left_ref[:half, :], right, NT)
+        send_ref[:, at : at + high - low] = bf16_dot(left_ref[half:, :], right, NT)
+        at += high - low
+
+
+def predict_kernel(pieces, scales, m_ref, *refs):
+    out_ref, at = refs[-1], 0
+    for n, (low, high) in enumerate(pieces):
+        x = jnp.concatenate([refs[2 * n][low:high, :], refs[2 * n + 1][low:high, :]], axis=1)
+        left, right = stacked(m_ref[:, at : at + high - low], axis=1)[0], stacked(x, axis=0)[1]
+        term = bf16_dot(left, right, NN) * scales[n]
+        total = term if n == 0 else total + term
+        at += high - low
+    out_ref[...] = total + refs[2 * len(pieces)][...] if len(refs) > 2 * len(pieces) + 1 else total
+
+
+def chunked(terms, rows, chunks):
+    edges = [terms * rows * c // chunks // TILE * TILE for c in range(chunks)] + [terms * rows]
+    result = []
+    for first, last in zip(edges, edges[1:]):
+        inside = [(j, max(first - j * rows, 0), min(last - j * rows, rows)) for j in range(terms)]
+        result.append([piece for piece in inside if piece[1] < piece[2]])
+    return result
 
 
 def core_blocks(count):
@@ -302,14 +319,29 @@
         [own[0], peer[0]],
         where_m,
     )
-    m = []
-    for j in range(terms):
-        keep, send = call(project_kernel, "project", [f32(half // 2, norb)] * 2, [], [left, own[j], peer[j]])
+    chunks = chunked(terms, norb, CHUNKS)
+    m, mine = [], []
+    for chunk in chunks:
+        rows_of = tuple(piece[1:] for piece in chunk)
+        sides = [x for piece in chunk for x in (own[piece[0]], peer[piece[0]])]
+        columns = sum(high - low for low, high in rows_of)
+        keep, send = call(
+            functools.partial(project_kernel, rows_of), "project", [f32(half // 2, columns)] * 2, [], [left] + sides
+        )
         m.append(all_reduce(route, keep, send, scatter, levels))
-    mine = []
-    for j in range(terms):
-        scale = WEIGHTS[j] / total
-        mine = [call(functools.partial(predict_kernel, scale), "predict", f32(half, 2 * width), [], [m[j], own[j], peer[j]] + mine)]
+    for chunk, product in zip(chunks, m):
+        rows_of = tuple(piece[1:] for piece in chunk)
+        sides = [x for piece in chunk for x in (own[piece[0]], peer[piece[0]])]
+        scales = tuple(WEIGHTS[piece[0]] / total for piece in chunk)
+        mine = [
+            call(
+                functools.partial(predict_kernel, rows_of, scales),
+                "predict",
+                f32(half, 2 * width),
+                [],
+                [product] + sides + mine,
+            )
+        ]
     mine = call(functools.partial(restore_kernel, blocks), "restore", f32(half, 2 * width), [], mine, where_m)
     other = swap(mine, route.core_perm())
 

time: 107 us -> 110 us (1.028)
  waiting for transfers between devices: 33.1 us -> 43.7 us
  starting transfers between devices: 49.8 us -> 42.7 us
    ppermute x38 -> x30, waiting for transfers between devices: 33.1 us -> 43.7 us  [swap(): return lax.ppermute(x, AXES, perm)]
    ppermute x38 -> x30, starting transfers between devices: 49.8 us -> 42.7 us  [swap(): return lax.ppermute(x, AXES, perm)]
    pallas_call x10 -> x8, Pallas kernels: 22.1 us -> 21.8 us  [call(): pl.pallas_call(kernel, name=name, out_shape=out_shape, in_specs=([] if sc...]
  transfers between devices with their start and end apart: 38 -> 30, of which waited for: 24 -> 26; matrix products, arithmetic and copies ran while one was open for 1% -> 0% of each run, Pallas kernels for 5% -> 4%
where the time goes in v4:
time: 110 us
  waiting for transfers between devices  43.7 us (40%)
  starting transfers between devices  42.7 us (39%)
  Pallas kernels  21.8 us (20%)
  local copies, waits for them, and re-layouts  1.27 us (1%)
    ppermute x30, waiting for transfers between devices, swap(): return lax.ppermute(x, AXES, perm)  43.7 us
    ppermute x30, starting transfers between devices, swap(): return lax.ppermute(x, AXES, perm)  42.7 us
    pallas_call x8, Pallas kernels, call(): pl.pallas_call(kernel, name=name, out_shape=out_shape, in_specs=([] if sc...  21.8 us
  transfers between devices with their start and end apart: 30, of which 26 were waited for; matrix products, arithmetic and copies ran while one was open for 0% of the time, Pallas kernels for 4%

profile of v4, /device:TPU:0, one launch (start us, length us, event | category | flops | bytes accessed | tf_op | source)
XLA Modules:
  0.0 110.2 jit_solution(759752723307982275)
XLA Ops:
  5.2 2.9 %collective-permute-start.11 = (f32[128,768]{1,0:T(8,128)S(1)}, f32[128,768]{1,0:T(8,128)S(1)}, u32[]{:S(2)}, u32[]{:S(2)}) collective-permute-start(f32[128,768]{1,0:T(8,128)S(1)} %get-tuple-element.17), channel_id=1, source_target_pairs={{0,8},{1,9},{2,10},{3,11},{4,20},{5,21},{6,22},{7,23},{8,0},{9,1},... | collective-permute-start | bytes 1179656 | tf_op jit(solution)/shard_map/ppermute | solution.py:88
  9.8 4.0 %collective-permute-done.11 = f32[128,768]{1,0:T(8,128)S(1)} collective-permute-done((f32[128,768]{1,0:T(8,128)S(1)}, f32[128,768]{1,0:T(8,128)S(1)}, u32[]{:S(2)}, u32[]{:S(2)}) %collective-permute-start.11) | collective-permute-done | bytes 393248 | tf_op jit(solution)/shard_map/ppermute | solution.py:88
  13.9 2.1 %collective-permute-start.12 = (f32[64,768]{1,0:T(8,128)S(1)}, f32[64,768]{1,0:T(8,128)S(1)}, u32[]{:S(2)}, u32[]{:S(2)}) collective-permute-start(f32[64,768]{1,0:T(8,128)S(1)} %get-tuple-element.28), channel_id=1, source_target_pairs={{0,16},{1,17},{2,18},{3,19},{4,12},{5,13},{6,14},{7,15},{8,24},{9,... | collective-permute-start | bytes 589832 | tf_op jit(solution)/shard_map/ppermute | solution.py:88
  16.0 4.0 %collective-permute-done.3 = f32[128,768]{1,0:T(8,128)S(1)} collective-permute-done((f32[128,768]{1,0:T(8,128)S(1)}, f32[128,768]{1,0:T(8,128)S(1)}, u32[]{:S(2)}, u32[]{:S(2)}) %collective-permute-start.3) | collective-permute-done | bytes 393248 | tf_op jit(solution)/shard_map/ppermute | solution.py:88
  20.0 2.4 %collective-permute-start.4 = (f32[64,768]{1,0:T(8,128)S(1)}, f32[64,768]{1,0:T(8,128)S(1)}, u32[]{:S(2)}, u32[]{:S(2)}) collective-permute-start(f32[64,768]{1,0:T(8,128)S(1)} %get-tuple-element.30), channel_id=1, source_target_pairs={{0,16},{1,17},{2,18},{3,19},{4,12},{5,13},{6,14},{7,15},{8,24},{9,... | collective-permute-start | bytes 589832 | tf_op jit(solution)/shard_map/ppermute | solution.py:88
  24.1 2.0 %collective-permute-done.4 = f32[64,768]{1,0:T(8,128)S(1)} collective-permute-done((f32[64,768]{1,0:T(8,128)S(1)}, f32[64,768]{1,0:T(8,128)S(1)}, u32[]{:S(2)}, u32[]{:S(2)}) %collective-permute-start.4) | collective-permute-done | bytes 196640 | tf_op jit(solution)/shard_map/ppermute | solution.py:88
  26.1 2.1 %collective-permute-start.5 = (f32[32,768]{1,0:T(8,128)S(1)}, f32[32,768]{1,0:T(8,128)S(1)}, u32[]{:S(2)}, u32[]{:S(2)}) collective-permute-start(f32[32,768]{1,0:T(8,128)S(1)} %get-tuple-element.37), channel_id=1, source_target_pairs={{0,1},{1,0},{2,3},{3,2},{4,5},{5,4},{6,7},{7,6},{8,9},{9,8},{10,11... | collective-permute-start | bytes 294920 | tf_op jit(solution)/shard_map/ppermute | solution.py:88
  28.3 2.7 %collective-permute-start.14 = (f32[16,768]{1,0:T(8,128)S(1)}, f32[16,768]{1,0:T(8,128)S(1)}, u32[]{:S(2)}, u32[]{:S(2)}) collective-permute-start(f32[16,768]{1,0:T(8,128)S(1)} %slice_add_fusion.8), channel_id=1, source_target_pairs={{0,2},{1,3},{2,0},{3,1},{4,6},{5,7},{6,4},{7,5},{8,10},{9,11},{10,... | collective-permute-start | bytes 147464 | tf_op jit(solution)/shard_map/ppermute | solution.py:88
  31.4 2.6 %collective-permute-start.6 = (f32[16,768]{1,0:T(8,128)S(1)}, f32[16,768]{1,0:T(8,128)S(1)}, u32[]{:S(2)}, u32[]{:S(2)}) collective-permute-start(f32[16,768]{1,0:T(8,128)S(1)} %slice_add_fusion.10), channel_id=1, source_target_pairs={{0,2},{1,3},{2,0},{3,1},{4,6},{5,7},{6,4},{7,5},{8,10},{9,11},{10,... | collective-permute-start | bytes 147464 | tf_op jit(solution)/shard_map/ppermute | solution.py:88
  36.8 2.4 %collective-permute-start.7 = (f32[16,768]{1,0:T(8,128)S(1)}, f32[16,768]{1,0:T(8,128)S(1)}, u32[]{:S(2)}, u32[]{:S(2)}) collective-permute-start(f32[16,768]{1,0:T(8,128)S(1)} %get-tuple-element.26), channel_id=1, source_target_pairs={{0,2},{1,3},{2,0},{3,1},{4,6},{5,7},{6,4},{7,5},{8,10},{9,11},{10,... | collective-permute-start | bytes 147464 | tf_op jit(solution)/shard_map/ppermute | solution.py:88
  41.9 1.7 %collective-permute-start.8 = (f32[32,768]{1,0:T(8,128)S(1)}, f32[32,768]{1,0:T(8,128)S(1)}, u32[]{:S(2)}, u32[]{:S(2)}) collective-permute-start(f32[32,768]{1,0:T(8,128)S(1)} %pad_maximum_fusion.5), channel_id=1, source_target_pairs={{0,1},{1,0},{2,3},{3,2},{4,5},{5,4},{6,7},{7,6},{8,9},{9,8},{10,11... | collective-permute-start | bytes 294920 | tf_op jit(solution)/shard_map/ppermute | solution.py:88
  46.6 1.9 %collective-permute-start.9 = (f32[64,768]{1,0:T(8,128)S(1)}, f32[64,768]{1,0:T(8,128)S(1)}, u32[]{:S(2)}, u32[]{:S(2)}) collective-permute-start(f32[64,768]{1,0:T(8,128)S(1)} %pad_maximum_fusion.3), channel_id=1, source_target_pairs={{0,16},{1,17},{2,18},{3,19},{4,12},{5,13},{6,14},{7,15},{8,24},{9,... | collective-permute-start | bytes 589832 | tf_op jit(solution)/shard_map/ppermute | solution.py:88
  48.5 4.1 %collective-permute-done.17 = f32[64,768]{1,0:T(8,128)S(1)} collective-permute-done((f32[64,768]{1,0:T(8,128)S(1)}, f32[64,768]{1,0:T(8,128)S(1)}, u32[]{:S(2)}, u32[]{:S(2)}) %collective-permute-start.17) | collective-permute-done | bytes 196640 | tf_op jit(solution)/shard_map/ppermute | solution.py:88
  54.2 2.6 %collective-permute-done.9 = f32[64,768]{1,0:T(8,128)S(1)} collective-permute-done((f32[64,768]{1,0:T(8,128)S(1)}, f32[64,768]{1,0:T(8,128)S(1)}, u32[]{:S(2)}, u32[]{:S(2)}) %collective-permute-start.9) | collective-permute-done | bytes 196640 | tf_op jit(solution)/shard_map/ppermute | solution.py:88
  58.5 2.0 %collective-permute-done.18 = f32[128,768]{1,0:T(8,128)S(1)} collective-permute-done((f32[128,768]{1,0:T(8,128)S(1)}, f32[128,768]{1,0:T(8,128)S(1)}, u32[]{:S(2)}, u32[]{:S(2)}) %collective-permute-start.18) | collective-permute-done | bytes 393248 | tf_op jit(solution)/shard_map/ppermute | solution.py:88
  61.4 3.3 %collective-permute-done.10 = f32[128,768]{1,0:T(8,128)S(1)} collective-permute-done((f32[128,768]{1,0:T(8,128)S(1)}, f32[128,768]{1,0:T(8,128)S(1)}, u32[]{:S(2)}, u32[]{:S(2)}) %collective-permute-start.10) | collective-permute-done | bytes 393248 | tf_op jit(solution)/shard_map/ppermute | solution.py:88
  75.5 1.8 %collective-permute-done.22 = f32[160,128]{1,0:T(8,128)S(1)} collective-permute-done((f32[160,128]{1,0:T(8,128)S(1)}, f32[160,128]{1,0:T(8,128)S(1)}, u32[]{:S(2)}, u32[]{:S(2)}) %collective-permute-start.22) | collective-permute-done | bytes 81952 | tf_op jit(solution)/shard_map/ppermute | solution.py:88
  77.3 2.7 %collective-permute-start.25 = (f32[160,128]{1,0:T(8,128)S(1)}, f32[160,128]{1,0:T(8,128)S(1)}, u32[]{:S(2)}, u32[]{:S(2)}) collective-permute-start(f32[160,128]{1,0:T(8,128)S(1)} %add_add_fusion.1), channel_id=1, source_target_pairs={{0,3},{1,2},{2,1},{3,0},{4,7},{5,6},{6,5},{7,4},{8,11},{9,10},{10,... | collective-permute-start | bytes 245768 | tf_op jit(solution)/shard_map/ppermute | solution.py:88
  80.0 1.7 %collective-permute-start.23 = (f32[160,128]{1,0:T(8,128)S(1)}, f32[160,128]{1,0:T(8,128)S(1)}, u32[]{:S(2)}, u32[]{:S(2)}) collective-permute-start(f32[160,128]{1,0:T(8,128)S(1)} %add_add_fusion.1), channel_id=1, source_target_pairs={{0,2},{1,3},{2,0},{3,1},{4,6},{5,7},{6,4},{7,5},{8,10},{9,11},{10,... | collective-permute-start | bytes 245768 | tf_op jit(solution)/shard_map/ppermute | solution.py:88
  81.7 2.5 %collective-permute-done.25 = f32[160,128]{1,0:T(8,128)S(1)} collective-permute-done((f32[160,128]{1,0:T(8,128)S(1)}, f32[160,128]{1,0:T(8,128)S(1)}, u32[]{:S(2)}, u32[]{:S(2)}) %collective-permute-start.25) | collective-permute-done | bytes 81952 | tf_op jit(solution)/shard_map/ppermute | solution.py:88
  85.1 2.0 %collective-permute-done.23 = f32[160,128]{1,0:T(8,128)S(1)} collective-permute-done((f32[160,128]{1,0:T(8,128)S(1)}, f32[160,128]{1,0:T(8,128)S(1)}, u32[]{:S(2)}, u32[]{:S(2)}) %collective-permute-start.23) | collective-permute-done | bytes 81952 | tf_op jit(solution)/shard_map/ppermute | solution.py:88
  87.3 2.4 %collective-permute-start.27 = (f32[160,128]{1,0:T(8,128)S(1)}, f32[160,128]{1,0:T(8,128)S(1)}, u32[]{:S(2)}, u32[]{:S(2)}) collective-permute-start(f32[160,128]{1,0:T(8,128)S(1)} %add_add_fusion), channel_id=1, source_target_pairs={{0,8},{1,9},{2,10},{3,11},{4,20},{5,21},{6,22},{7,23},{8,0},{9,1},... | collective-permute-start | bytes 245768 | tf_op jit(solution)/shard_map/ppermute | solution.py:88
  90.7 1.9 %collective-permute-done.28 = f32[160,128]{1,0:T(8,128)S(1)} collective-permute-done((f32[160,128]{1,0:T(8,128)S(1)}, f32[160,128]{1,0:T(8,128)S(1)}, u32[]{:S(2)}, u32[]{:S(2)}) %collective-permute-start.28) | collective-permute-done | bytes 81952 | tf_op jit(solution)/shard_map/ppermute | solution.py:88
  95.8 14.4 %solve.1 = f32[512,128]{1,0:T(8,128)} custom-call(s32[3]{0:T(128)S(1)} %pad_add_fusion.where, f32[640,128]{1,0:T(8,128)S(1)} %pad_maximum_fusion.2.mine_ref, f32[640,128]{1,0:T(8,128)S(1)} %collective-permute-done.29.other_ref, f32[512,128]{1,0:T(8,128)S(1)} %get-tuple-element.22.p_ref), custom_call_target="tpu_custom_call" | custom-call | tf_op jit(solution)/shard_map/solve/pallas_call | solution.py:286
  (72 shorter events, 37.6 us)
Async XLA Ops:
  1.8 6.3 %collective-permute-start.2 = (f32[512,128]{1,0:T(8,128)S(1)}, f32[512,128]{1,0:T(8,128)S(1)}, u32[]{:S(2)}, u32[]{:S(2)}) collective-permute-start(f32[512,128]{1,0:T(8,128)S(1)} %get-tuple-element.31.refs_2_), channel_id=1, source_target_pairs={{0,4},{1,5},{2,6},{3,7},{4,0},{5,1},{6,2},{7,3},{8,12},{9,13},{10,... | collective-permute-start | bytes 786440 | tf_op jit(solution)/shard_map/ppermute | solution.py:88
  5.2 8.7 %collective-permute-start.11 = (f32[128,768]{1,0:T(8,128)S(1)}, f32[128,768]{1,0:T(8,128)S(1)}, u32[]{:S(2)}, u32[]{:S(2)}) collective-permute-start(f32[128,768]{1,0:T(8,128)S(1)} %get-tuple-element.17), channel_id=1, source_target_pairs={{0,8},{1,9},{2,10},{3,11},{4,20},{5,21},{6,22},{7,23},{8,0},{9,1},... | collective-permute-start | bytes 1179656 | tf_op jit(solution)/shard_map/ppermute | solution.py:88
  9.7 10.2 %collective-permute-start.3 = (f32[128,768]{1,0:T(8,128)S(1)}, f32[128,768]{1,0:T(8,128)S(1)}, u32[]{:S(2)}, u32[]{:S(2)}) collective-permute-start(f32[128,768]{1,0:T(8,128)S(1)} %get-tuple-element.15), channel_id=1, source_target_pairs={{0,8},{1,9},{2,10},{3,11},{4,20},{5,21},{6,22},{7,23},{8,0},{9,1},... | collective-permute-start | bytes 1179656 | tf_op jit(solution)/shard_map/ppermute | solution.py:88
  13.9 8.6 %collective-permute-start.12 = (f32[64,768]{1,0:T(8,128)S(1)}, f32[64,768]{1,0:T(8,128)S(1)}, u32[]{:S(2)}, u32[]{:S(2)}) collective-permute-start(f32[64,768]{1,0:T(8,128)S(1)} %get-tuple-element.28), channel_id=1, source_target_pairs={{0,16},{1,17},{2,18},{3,19},{4,12},{5,13},{6,14},{7,15},{8,24},{9,... | collective-permute-start | bytes 589832 | tf_op jit(solution)/shard_map/ppermute | solution.py:88
  20.0 6.1 %collective-permute-start.4 = (f32[64,768]{1,0:T(8,128)S(1)}, f32[64,768]{1,0:T(8,128)S(1)}, u32[]{:S(2)}, u32[]{:S(2)}) collective-permute-start(f32[64,768]{1,0:T(8,128)S(1)} %get-tuple-element.30), channel_id=1, source_target_pairs={{0,16},{1,17},{2,18},{3,19},{4,12},{5,13},{6,14},{7,15},{8,24},{9,... | collective-permute-start | bytes 589832 | tf_op jit(solution)/shard_map/ppermute | solution.py:88
  22.5 5.8 %collective-permute-start.13 = (f32[32,768]{1,0:T(8,128)S(1)}, f32[32,768]{1,0:T(8,128)S(1)}, u32[]{:S(2)}, u32[]{:S(2)}) collective-permute-start(f32[32,768]{1,0:T(8,128)S(1)} %get-tuple-element.35), channel_id=1, source_target_pairs={{0,1},{1,0},{2,3},{3,2},{4,5},{5,4},{6,7},{7,6},{8,9},{9,8},{10,11... | collective-permute-start | bytes 294920 | tf_op jit(solution)/shard_map/ppermute | solution.py:88
  26.1 5.3 %collective-permute-start.5 = (f32[32,768]{1,0:T(8,128)S(1)}, f32[32,768]{1,0:T(8,128)S(1)}, u32[]{:S(2)}, u32[]{:S(2)}) collective-permute-start(f32[32,768]{1,0:T(8,128)S(1)} %get-tuple-element.37), channel_id=1, source_target_pairs={{0,1},{1,0},{2,3},{3,2},{4,5},{5,4},{6,7},{7,6},{8,9},{9,8},{10,11... | collective-permute-start | bytes 294920 | tf_op jit(solution)/shard_map/ppermute | solution.py:88
  28.3 6.6 %collective-permute-start.14 = (f32[16,768]{1,0:T(8,128)S(1)}, f32[16,768]{1,0:T(8,128)S(1)}, u32[]{:S(2)}, u32[]{:S(2)}) collective-permute-start(f32[16,768]{1,0:T(8,128)S(1)} %slice_add_fusion.8), channel_id=1, source_target_pairs={{0,2},{1,3},{2,0},{3,1},{4,6},{5,7},{6,4},{7,5},{8,10},{9,11},{10,... | collective-permute-start | bytes 147464 | tf_op jit(solution)/shard_map/ppermute | solution.py:88
  31.4 5.4 %collective-permute-start.6 = (f32[16,768]{1,0:T(8,128)S(1)}, f32[16,768]{1,0:T(8,128)S(1)}, u32[]{:S(2)}, u32[]{:S(2)}) collective-permute-start(f32[16,768]{1,0:T(8,128)S(1)} %slice_add_fusion.10), channel_id=1, source_target_pairs={{0,2},{1,3},{2,0},{3,1},{4,6},{5,7},{6,4},{7,5},{8,10},{9,11},{10,... | collective-permute-start | bytes 147464 | tf_op jit(solution)/shard_map/ppermute | solution.py:88
  34.9 5.2 %collective-permute-start.15 = (f32[16,768]{1,0:T(8,128)S(1)}, f32[16,768]{1,0:T(8,128)S(1)}, u32[]{:S(2)}, u32[]{:S(2)}) collective-permute-start(f32[16,768]{1,0:T(8,128)S(1)} %get-tuple-element.24), channel_id=1, source_target_pairs={{0,2},{1,3},{2,0},{3,1},{4,6},{5,7},{6,4},{7,5},{8,10},{9,11},{10,... | collective-permute-start | bytes 147464 | tf_op jit(solution)/shard_map/ppermute | solution.py:88
  36.8 5.1 %collective-permute-start.7 = (f32[16,768]{1,0:T(8,128)S(1)}, f32[16,768]{1,0:T(8,128)S(1)}, u32[]{:S(2)}, u32[]{:S(2)}) collective-permute-start(f32[16,768]{1,0:T(8,128)S(1)} %get-tuple-element.26), channel_id=1, source_target_pairs={{0,2},{1,3},{2,0},{3,1},{4,6},{5,7},{6,4},{7,5},{8,10},{9,11},{10,... | collective-permute-start | bytes 147464 | tf_op jit(solution)/shard_map/ppermute | solution.py:88
  41.9 4.7 %collective-permute-start.8 = (f32[32,768]{1,0:T(8,128)S(1)}, f32[32,768]{1,0:T(8,128)S(1)}, u32[]{:S(2)}, u32[]{:S(2)}) collective-permute-start(f32[32,768]{1,0:T(8,128)S(1)} %pad_maximum_fusion.5), channel_id=1, source_target_pairs={{0,1},{1,0},{2,3},{3,2},{4,5},{5,4},{6,7},{7,6},{8,9},{9,8},{10,11... | collective-permute-start | bytes 294920 | tf_op jit(solution)/shard_map/ppermute | solution.py:88
  44.8 7.8 %collective-permute-start.17 = (f32[64,768]{1,0:T(8,128)S(1)}, f32[64,768]{1,0:T(8,128)S(1)}, u32[]{:S(2)}, u32[]{:S(2)}) collective-permute-start(f32[64,768]{1,0:T(8,128)S(1)} %pad_maximum_fusion.4), channel_id=1, source_target_pairs={{0,16},{1,17},{2,18},{3,19},{4,12},{5,13},{6,14},{7,15},{8,24},{9,... | collective-permute-start | bytes 589832 | tf_op jit(solution)/shard_map/ppermute | solution.py:88
  46.6 10.2 %collective-permute-start.9 = (f32[64,768]{1,0:T(8,128)S(1)}, f32[64,768]{1,0:T(8,128)S(1)}, u32[]{:S(2)}, u32[]{:S(2)}) collective-permute-start(f32[64,768]{1,0:T(8,128)S(1)} %pad_maximum_fusion.3), channel_id=1, source_target_pairs={{0,16},{1,17},{2,18},{3,19},{4,12},{5,13},{6,14},{7,15},{8,24},{9,... | collective-permute-start | bytes 589832 | tf_op jit(solution)/shard_map/ppermute | solution.py:88
  52.7 7.8 %collective-permute-start.18 = (f32[128,768]{1,0:T(8,128)S(1)}, f32[128,768]{1,0:T(8,128)S(1)}, u32[]{:S(2)}, u32[]{:S(2)}) collective-permute-start(f32[128,768]{1,0:T(8,128)S(1)} %pad_maximum_fusion.1), channel_id=1, source_target_pairs={{0,8},{1,9},{2,10},{3,11},{4,20},{5,21},{6,22},{7,23},{8,0},{9,1},... | collective-permute-start | bytes 1179656 | tf_op jit(solution)/shard_map/ppermute | solution.py:88
  56.9 7.8 %collective-permute-start.10 = (f32[128,768]{1,0:T(8,128)S(1)}, f32[128,768]{1,0:T(8,128)S(1)}, u32[]{:S(2)}, u32[]{:S(2)}) collective-permute-start(f32[128,768]{1,0:T(8,128)S(1)} %pad_maximum_fusion), channel_id=1, source_target_pairs={{0,8},{1,9},{2,10},{3,11},{4,20},{5,21},{6,22},{7,23},{8,0},{9,1},... | collective-permute-start | bytes 1179656 | tf_op jit(solution)/shard_map/ppermute | solution.py:88
  69.1 5.0 %collective-permute-start.20 = (f32[160,128]{1,0:T(8,128)S(1)}, f32[160,128]{1,0:T(8,128)S(1)}, u32[]{:S(2)}, u32[]{:S(2)}) collective-permute-start(f32[160,128]{1,0:T(8,128)S(1)} %get-tuple-element.19), channel_id=1, source_target_pairs={{0,16},{1,17},{2,18},{3,19},{4,12},{5,13},{6,14},{7,15},{8,24},{9,... | collective-permute-start | bytes 245768 | tf_op jit(solution)/shard_map/ppermute | solution.py:88
  70.4 5.0 %collective-permute-start.21 = (f32[160,128]{1,0:T(8,128)S(1)}, f32[160,128]{1,0:T(8,128)S(1)}, u32[]{:S(2)}, u32[]{:S(2)}) collective-permute-start(f32[160,128]{1,0:T(8,128)S(1)} %get-tuple-element.20), channel_id=1, source_target_pairs={{0,8},{1,9},{2,10},{3,11},{4,20},{5,21},{6,22},{7,23},{8,0},{9,1},... | collective-permute-start | bytes 245768 | tf_op jit(solution)/shard_map/ppermute | solution.py:88
  71.9 5.3 %collective-permute-start.22 = (f32[160,128]{1,0:T(8,128)S(1)}, f32[160,128]{1,0:T(8,128)S(1)}, u32[]{:S(2)}, u32[]{:S(2)}) collective-permute-start(f32[160,128]{1,0:T(8,128)S(1)} %get-tuple-element.21), channel_id=1, source_target_pairs={{0,24},{1,25},{2,26},{3,27},{4,28},{5,29},{6,30},{7,31},{8,16},{9,... | collective-permute-start | bytes 245768 | tf_op jit(solution)/shard_map/ppermute | solution.py:88
  77.3 7.0 %collective-permute-start.25 = (f32[160,128]{1,0:T(8,128)S(1)}, f32[160,128]{1,0:T(8,128)S(1)}, u32[]{:S(2)}, u32[]{:S(2)}) collective-permute-start(f32[160,128]{1,0:T(8,128)S(1)} %add_add_fusion.1), channel_id=1, source_target_pairs={{0,3},{1,2},{2,1},{3,0},{4,7},{5,6},{6,5},{7,4},{8,11},{9,10},{10,... | collective-permute-start | bytes 245768 | tf_op jit(solution)/shard_map/ppermute | solution.py:88
  80.0 5.0 %collective-permute-start.24 = (f32[160,128]{1,0:T(8,128)S(1)}, f32[160,128]{1,0:T(8,128)S(1)}, u32[]{:S(2)}, u32[]{:S(2)}) collective-permute-start(f32[160,128]{1,0:T(8,128)S(1)} %add_add_fusion.1), channel_id=1, source_target_pairs={{0,1},{1,0},{2,3},{3,2},{4,5},{5,4},{6,7},{7,6},{8,9},{9,8},{10,11... | collective-permute-start | bytes 245768 | tf_op jit(solution)/shard_map/ppermute | solution.py:88
  80.0 7.0 %collective-permute-start.23 = (f32[160,128]{1,0:T(8,128)S(1)}, f32[160,128]{1,0:T(8,128)S(1)}, u32[]{:S(2)}, u32[]{:S(2)}) collective-permute-start(f32[160,128]{1,0:T(8,128)S(1)} %add_add_fusion.1), channel_id=1, source_target_pairs={{0,2},{1,3},{2,0},{3,1},{4,6},{5,7},{6,4},{7,5},{8,10},{9,11},{10,... | collective-permute-start | bytes 245768 | tf_op jit(solution)/shard_map/ppermute | solution.py:88
  87.1 5.4 %collective-permute-start.28 = (f32[160,128]{1,0:T(8,128)S(1)}, f32[160,128]{1,0:T(8,128)S(1)}, u32[]{:S(2)}, u32[]{:S(2)}) collective-permute-start(f32[160,128]{1,0:T(8,128)S(1)} %add_add_fusion), channel_id=1, source_target_pairs={{0,24},{1,25},{2,26},{3,27},{4,28},{5,29},{6,30},{7,31},{8,16},{9,... | collective-permute-start | bytes 245768 | tf_op jit(solution)/shard_map/ppermute | solution.py:88
  87.3 5.7 %collective-permute-start.27 = (f32[160,128]{1,0:T(8,128)S(1)}, f32[160,128]{1,0:T(8,128)S(1)}, u32[]{:S(2)}, u32[]{:S(2)}) collective-permute-start(f32[160,128]{1,0:T(8,128)S(1)} %add_add_fusion), channel_id=1, source_target_pairs={{0,8},{1,9},{2,10},{3,11},{4,20},{5,21},{6,22},{7,23},{8,0},{9,1},... | collective-permute-start | bytes 245768 | tf_op jit(solution)/shard_map/ppermute | solution.py:88
  (6 other events, 15.9 us)

commit v5 on v3

--- a/solution.py
+++ b/solution.py
@@ -12,6 +12,7 @@
 TILE = 128
 PANEL = 32
 GROUP = 16
+AHEAD = 4
 VMEM_LIMIT = 16 << 20
 AXES = ("row", "col")
 NT = (((1,), (1,)), ((), ()))
@@ -120,42 +121,51 @@
     return keep
 
 
-def arrange_kernel(blocks, where, own_ref, peer_ref, out_ref, left):
-    rows, width = left.shape[0], own_ref.shape[1]
+def fetch_kernel(in_ref, out_ref):
+    pltpu.sync_copy(in_ref, out_ref)
+
+
+def project_kernel(j, left_ref, own_ref, peer_ref, keep_ref, send_ref):
+    half = keep_ref.shape[0]
+    right = stacked(jnp.concatenate([own_ref[j], peer_ref[j]], axis=1), axis=1)[1]
+    keep_ref[...] = bf16_dot(left_ref[:half, :], right, NT)
+    send_ref[...] = bf16_dot(left_ref[half:, :], right, NT)
+
+
+def first_project_kernel(blocks, where, own_ref, peer_ref, keep_ref, send_ref, left_ref, left):
+    rows, width = left.shape[0], own_ref.shape[2]
     core, place = where[0], where[1]
     size = rows // blocks
     for k in range(blocks):
         at = pl.multiple_of(core * rows + (place ^ k) * size, size)
-        left[k * size : (k + 1) * size, :width] = own_ref[pl.ds(at, size), :]
-        left[k * size : (k + 1) * size, width:] = peer_ref[pl.ds(at, size), :]
-    out_ref[...] = stacked(left[...], axis=1)[0]
-
-
-def project_kernel(left_ref, own_ref, peer_ref, keep_ref, send_ref):
-    half = keep_ref.shape[0]
-    right = stacked(jnp.concatenate([own_ref[...], peer_ref[...]], axis=1), axis=1)[1]
-    keep_ref[...] = bf16_dot(left_ref[:half, :], right, NT)
-    send_ref[...] = bf16_dot(left_ref[half:, :], right, NT)
-
-
-def predict_kernel(scale, m_ref, own_ref, peer_ref, *refs):
-    out_ref = refs[-1]
+        left[k * size : (k + 1) * size, :width] = own_ref[0, pl.ds(at, size), :]
+        left[k * size : (k + 1) * size, width:] = peer_ref[0, pl.ds(at, size), :]
+    left_ref[...] = stacked(left[...], axis=1)[0]
+    project_kernel(0, left_ref, own_ref, peer_ref, keep_ref, send_ref)
+
+
+def term(j, scale, m_ref, own_ref, peer_ref):
     left = stacked(m_ref[...], axis=1)[0]
-    right = stacked(jnp.concatenate([own_ref[...], peer_ref[...]], axis=1), axis=0)[1]
-    term = bf16_dot(left, right, NN) * scale
-    out_ref[...] = term + refs[0][...] if len(refs) > 1 else term
+    right = stacked(jnp.concatenate([own_ref[j], peer_ref[j]], axis=1), axis=0)[1]
+    return bf16_dot(left, right, NN) * scale
+
+
+def predict_kernel(j, scale, m_ref, own_ref, peer_ref, *refs):
+    value = term(j, scale, m_ref, own_ref, peer_ref)
+    refs[-1][...] = value + refs[0][...] if len(refs) > 1 else value
+
+
+def last_predict_kernel(j, scale, blocks, where, m_ref, own_ref, peer_ref, sum_ref, out_ref, total):
+    total[...] = term(j, scale, m_ref, own_ref, peer_ref) + sum_ref[...]
+    size = total.shape[0] // blocks
+    for k in range(blocks):
+        out_ref[pl.ds(pl.multiple_of((where[1] ^ k) * size, size), size), :] = total[k * size : (k + 1) * size, :]
 
 
 def core_blocks(count):
     blocks = [(i, j) for i in range(count) for j in range(i, count)]
     half = (len(blocks) + 1) // 2
     return blocks[:half], blocks[half:]
-
-
-def restore_kernel(blocks, where, in_ref, out_ref):
-    size = in_ref.shape[0] // blocks
-    for k in range(blocks):
-        out_ref[pl.ds(pl.multiple_of((where[1] ^ k) * size, size), size), :] = in_ref[k * size : (k + 1) * size, :]
 
 
 def gram_kernel(parts, scale, where, mine_ref, other_ref, *refs):
@@ -209,14 +219,11 @@
         scale = [jnp.zeros((8, tile), jnp.float32)] * per_panel
         cols = {}
         for j in range(PANEL):
-            if j % GROUP == 0:
-                cols = {
-                    k: {
-                        i: jnp.broadcast_to(r[i][0][:, PANEL * s + k : PANEL * s + k + 1], (8, tile))
-                        for i in range(k // 8, per_panel)
-                    }
-                    for k in range(j, j + GROUP)
-                }
+            start = 0 if j == 0 else j + AHEAD
+            if start % GROUP == 0 and start < PANEL:
+                for k in range(start, start + GROUP):
+                    at = PANEL * s + k
+                    cols[k] = {i: jnp.broadcast_to(r[i][0][:, at : at + 1], (8, tile)) for i in range(k // 8, per_panel)}
             jb, js = j // 8, j % 8
             col = cols[j]
             pivot = jnp.broadcast_to(col[jb][js : js + 1, :], (8, tile))
@@ -225,7 +232,7 @@
             mult = {i: col[i] * inverse for i in range(jb, per_panel)}
             mult[jb] = jnp.where(sub > js, mult[jb], 0.0)
             first = jb if js < 7 else jb + 1
-            for k in range(j + 1, (j // GROUP + 1) * GROUP):
+            for k in range(j + 1, len(cols)):
                 row = jnp.broadcast_to(col[k // 8][k % 8 : k % 8 + 1, :], (8, tile))
                 for i in range(k // 8, per_panel):
                     cols[k][i] = cols[k][i] - mult[i] * row
@@ -246,9 +253,13 @@
                 break
             left, right = stacked(u, axis=0)
             if s < panels - 1:
-                low = PANEL * (s + 1)
-                update = bf16_dot(left[:, :tile], right, TN)
-                work[start + low : start + tile, start:] -= update[low:, :]
+                flipped = jnp.transpose(left[:, :tile])
+                low, high, near = PANEL * (s + 1), PANEL * (s + 2), min(start + 2 * tile, width)
+                for rows, columns in (((low, high), (start, near)), ((low, high), (near, width)), ((high, tile), (start, width))):
+                    if rows[0] < rows[1] and columns[0] < columns[1]:
+                        work[start + rows[0] : start + rows[1], columns[0] : columns[1]] -= bf16_dot(
+                            flipped[rows[0] : rows[1], :], right[:, columns[0] - start : columns[1] - start], NN
+                        )
             if b < count - 1:
                 stack_a[deep * s : deep * (s + 1), start:n] = left[:, : n - start]
                 stack_b[deep * s : deep * (s + 1), start:] = right
@@ -292,25 +303,34 @@
     parts = 1 << parts_levels
     where_g = jnp.stack([core, route.place(core, parts_levels), route.place(1 - core, parts_levels)])
 
-    own = [history[j] for j in range(terms)]
-    peer = [swap(h, route.core_perm()) for h in own]
-    left = call(
-        functools.partial(arrange_kernel, blocks),
-        "arrange",
-        jax.ShapeDtypeStruct((half, 12 * width), jnp.bfloat16),
+    peer = swap(history, route.core_perm())
+    own = pl.pallas_call(
+        fetch_kernel,
+        name="fetch",
+        out_shape=f32(*history.shape),
+        in_specs=[pl.BlockSpec(memory_space=pl.ANY)],
+        out_specs=VMEM,
+        compiler_params=pltpu.CompilerParams(vmem_limit_bytes=VMEM_LIMIT),
+    )(history)
+    out = [f32(half // 2, norb)] * 2
+    keep, send, left = call(
+        functools.partial(first_project_kernel, blocks),
+        "project",
+        out + [jax.ShapeDtypeStruct((half, 12 * width), jnp.bfloat16)],
         [f32(half, 2 * width)],
-        [own[0], peer[0]],
+        [own, peer],
         where_m,
     )
-    m = []
-    for j in range(terms):
-        keep, send = call(project_kernel, "project", [f32(half // 2, norb)] * 2, [], [left, own[j], peer[j]])
-        m.append(all_reduce(route, keep, send, scatter, levels))
-    mine = []
-    for j in range(terms):
-        scale = WEIGHTS[j] / total
-        mine = [call(functools.partial(predict_kernel, scale), "predict", f32(half, 2 * width), [], [m[j], own[j], peer[j]] + mine)]
-    mine = call(functools.partial(restore_kernel, blocks), "restore", f32(half, 2 * width), [], mine, where_m)
+    products = [(keep, send)]
+    for j in range(1, terms):
+        products.append(call(functools.partial(project_kernel, j), "project", out, [], [left, own, peer]))
+    m = [all_reduce(route, keep, send, scatter, levels) for keep, send in products]
+    out, mine = f32(half, 2 * width), []
+    for j in range(terms - 1):
+        kernel = functools.partial(predict_kernel, j, WEIGHTS[j] / total)
+        mine = [call(kernel, "predict", out, [], [m[j], own, peer] + mine)]
+    kernel = functools.partial(last_predict_kernel, terms - 1, WEIGHTS[terms - 1] / total, blocks)
+    mine = call(kernel, "predict", out, [out], [m[-1], own, peer] + mine, where_m)
     other = swap(mine, route.core_perm())
 
     shares = (norb // TILE) * (norb // TILE + 1) // 2

time: 107 us -> 108 us (level)
  waiting for transfers between devices: 33.1 us -> 37.9 us
  starting transfers between devices: 49.8 us -> 46.8 us
  Pallas kernels: 22.1 us -> 20.9 us
    ppermute x38 -> x36, waiting for transfers between devices: 33.1 us -> 37.9 us  [swap(): return lax.ppermute(x, AXES, perm)]
    ppermute x38 -> x36, starting transfers between devices: 49.8 us -> 46.8 us  [swap(): return lax.ppermute(x, AXES, perm)]
    pallas_call x10 -> x8, Pallas kernels: 22.1 us -> 20.9 us  [call(): pl.pallas_call(kernel, name=name, out_shape=out_shape, in_specs=([] if sc...]
    squeeze x1 -> x0, local copies, waits for them, and re-layouts: 1.16 us -> none  [on_device(): own = [history[j] for j in range(terms)]]
    unnamed x9 -> x11, local copies, waits for them, and re-layouts: 0.06 us -> 1.2 us
  transfers between devices with their start and end apart: 38 -> 36, of which waited for: 24 -> 26; matrix products, arithmetic and copies ran while one was open for 1% -> 1% of each run, Pallas kernels for 5% -> 3%
where the time goes in v5:
time: 108 us
  starting transfers between devices  46.8 us (43%)
  waiting for transfers between devices  37.9 us (35%)
  Pallas kernels  20.9 us (19%)
  local copies, waits for them, and re-layouts  1.25 us (1%)
    ppermute x36, starting transfers between devices, swap(): return lax.ppermute(x, AXES, perm)  46.8 us
    ppermute x36, waiting for transfers between devices, swap(): return lax.ppermute(x, AXES, perm)  37.9 us
    pallas_call x8, Pallas kernels, call(): pl.pallas_call(kernel, name=name, out_shape=out_shape, in_specs=([] if sc...  20.9 us
  transfers between devices with their start and end apart: 36, of which 26 were waited for; matrix products, arithmetic and copies ran while one was open for 1% of the time, Pallas kernels for 3%

profile of v5, /device:TPU:0, one launch (start us, length us, event | category | flops | bytes accessed | tf_op | source)
XLA Modules:
  0.0 107.7 jit_solution(13573793685315444615)
XLA Ops:
  2.6 1.7 %project.3 = (f32[128,512]{1,0:T(8,128)S(1)}, f32[128,512]{1,0:T(8,128)S(1)}, bf16[256,1536]{1,0:T(8,128)(2,1)S(1)}) custom-call(s32[2]{0:T(128)S(1)} %pad_add_fusion.1.where, f32[3,512,128]{2,1,0:T(8,128)S(1)} %fetch.1.own_ref, f32[3,512,128]{2,1,0:T(8,128)S(1)} %collective-permute-done.peer_ref), custom_call_target="tpu_custom_call" | custom-call | tf_op jit(solution)/shard_map/project/pallas_call | solution.py:280
  4.3 2.9 %collective-permute-start.17 = (f32[128,512]{1,0:T(8,128)S(1)}, f32[128,512]{1,0:T(8,128)S(1)}, u32[]{:S(2)}, u32[]{:S(2)}) collective-permute-start(f32[128,512]{1,0:T(8,128)S(1)} %get-tuple-element.23), channel_id=1, source_target_pairs={{0,8},{1,9},{2,10},{3,11},{4,20},{5,21},{6,22},{7,23},{8,0},{9,1},... | collective-permute-start | bytes 786440 | tf_op jit(solution)/shard_map/ppermute | solution.py:88
  9.6 2.1 %collective-permute-start.1 = (f32[128,512]{1,0:T(8,128)S(1)}, f32[128,512]{1,0:T(8,128)S(1)}, u32[]{:S(2)}, u32[]{:S(2)}) collective-permute-start(f32[128,512]{1,0:T(8,128)S(1)} %get-tuple-element.19), channel_id=1, source_target_pairs={{0,8},{1,9},{2,10},{3,11},{4,20},{5,21},{6,22},{7,23},{8,0},{9,1},... | collective-permute-start | bytes 786440 | tf_op jit(solution)/shard_map/ppermute | solution.py:88
  11.7 2.0 %collective-permute-start.18 = (f32[64,512]{1,0:T(8,128)S(1)}, f32[64,512]{1,0:T(8,128)S(1)}, u32[]{:S(2)}, u32[]{:S(2)}) collective-permute-start(f32[64,512]{1,0:T(8,128)S(1)} %get-tuple-element.36), channel_id=1, source_target_pairs={{0,16},{1,17},{2,18},{3,19},{4,12},{5,13},{6,14},{7,15},{8,24},{9,... | collective-permute-start | bytes 393224 | tf_op jit(solution)/shard_map/ppermute | solution.py:88
  13.7 2.0 %collective-permute-done.9 = f32[128,512]{1,0:T(8,128)S(1)} collective-permute-done((f32[128,512]{1,0:T(8,128)S(1)}, f32[128,512]{1,0:T(8,128)S(1)}, u32[]{:S(2)}, u32[]{:S(2)}) %collective-permute-start.9) | collective-permute-done | bytes 262176 | tf_op jit(solution)/shard_map/ppermute | solution.py:88
  17.4 3.1 %collective-permute-done.1 = f32[128,512]{1,0:T(8,128)S(1)} collective-permute-done((f32[128,512]{1,0:T(8,128)S(1)}, f32[128,512]{1,0:T(8,128)S(1)}, u32[]{:S(2)}, u32[]{:S(2)}) %collective-permute-start.1) | collective-permute-done | bytes 262176 | tf_op jit(solution)/shard_map/ppermute | solution.py:88
  20.5 1.7 %collective-permute-start.2 = (f32[64,512]{1,0:T(8,128)S(1)}, f32[64,512]{1,0:T(8,128)S(1)}, u32[]{:S(2)}, u32[]{:S(2)}) collective-permute-start(f32[64,512]{1,0:T(8,128)S(1)} %get-tuple-element.40), channel_id=1, source_target_pairs={{0,16},{1,17},{2,18},{3,19},{4,12},{5,13},{6,14},{7,15},{8,24},{9,... | collective-permute-start | bytes 393224 | tf_op jit(solution)/shard_map/ppermute | solution.py:88
  22.2 1.6 %collective-permute-start.19 = (f32[32,512]{1,0:T(8,128)S(1)}, f32[32,512]{1,0:T(8,128)S(1)}, u32[]{:S(2)}, u32[]{:S(2)}) collective-permute-start(f32[32,512]{1,0:T(8,128)S(1)} %get-tuple-element.42), channel_id=1, source_target_pairs={{0,1},{1,0},{2,3},{3,2},{4,5},{5,4},{6,7},{7,6},{8,9},{9,8},{10,11... | collective-permute-start | bytes 196616 | tf_op jit(solution)/shard_map/ppermute | solution.py:88
  25.5 1.7 %collective-permute-start.3 = (f32[32,512]{1,0:T(8,128)S(1)}, f32[32,512]{1,0:T(8,128)S(1)}, u32[]{:S(2)}, u32[]{:S(2)}) collective-permute-start(f32[32,512]{1,0:T(8,128)S(1)} %get-tuple-element.46), channel_id=1, source_target_pairs={{0,1},{1,0},{2,3},{3,2},{4,5},{5,4},{6,7},{7,6},{8,9},{9,8},{10,11... | collective-permute-start | bytes 196616 | tf_op jit(solution)/shard_map/ppermute | solution.py:88
  27.3 2.7 %collective-permute-start.20 = (f32[16,512]{1,0:T(8,128)S(1)}, f32[16,512]{1,0:T(8,128)S(1)}, u32[]{:S(2)}, u32[]{:S(2)}) collective-permute-start(f32[16,512]{1,0:T(8,128)S(1)} %slice_add_fusion.12), channel_id=1, source_target_pairs={{0,2},{1,3},{2,0},{3,1},{4,6},{5,7},{6,4},{7,5},{8,10},{9,11},{10,... | collective-permute-start | bytes 98312 | tf_op jit(solution)/shard_map/ppermute | solution.py:88
  33.1 1.8 %collective-permute-start.21 = (f32[16,512]{1,0:T(8,128)S(1)}, f32[16,512]{1,0:T(8,128)S(1)}, u32[]{:S(2)}, u32[]{:S(2)}) collective-permute-start(f32[16,512]{1,0:T(8,128)S(1)} %get-tuple-element.30), channel_id=1, source_target_pairs={{0,2},{1,3},{2,0},{3,1},{4,6},{5,7},{6,4},{7,5},{8,10},{9,11},{10,... | collective-permute-start | bytes 98312 | tf_op jit(solution)/shard_map/ppermute | solution.py:88
  34.9 2.4 %collective-permute-done.4 = f32[16,512]{1,0:T(8,128)S(1)} collective-permute-done((f32[16,512]{1,0:T(8,128)S(1)}, f32[16,512]{1,0:T(8,128)S(1)}, u32[]{:S(2)}, u32[]{:S(2)}) %collective-permute-start.4) | collective-permute-done | bytes 32800 | tf_op jit(solution)/shard_map/ppermute | solution.py:88
  38.3 2.1 %collective-permute-start.13 = (f32[16,512]{1,0:T(8,128)S(1)}, f32[16,512]{1,0:T(8,128)S(1)}, u32[]{:S(2)}, u32[]{:S(2)}) collective-permute-start(f32[16,512]{1,0:T(8,128)S(1)} %get-tuple-element.32), channel_id=1, source_target_pairs={{0,2},{1,3},{2,0},{3,1},{4,6},{5,7},{6,4},{7,5},{8,10},{9,11},{10,... | collective-permute-start | bytes 98312 | tf_op jit(solution)/shard_map/ppermute | solution.py:88
  40.5 1.7 %collective-permute-done.5 = f32[16,512]{1,0:T(8,128)S(1)} collective-permute-done((f32[16,512]{1,0:T(8,128)S(1)}, f32[16,512]{1,0:T(8,128)S(1)}, u32[]{:S(2)}, u32[]{:S(2)}) %collective-permute-start.5) | collective-permute-done | bytes 32800 | tf_op jit(solution)/shard_map/ppermute | solution.py:88
  44.8 1.8 %collective-permute-start.23 = (f32[64,512]{1,0:T(8,128)S(1)}, f32[64,512]{1,0:T(8,128)S(1)}, u32[]{:S(2)}, u32[]{:S(2)}) collective-permute-start(f32[64,512]{1,0:T(8,128)S(1)} %pad_maximum_fusion.6), channel_id=1, source_target_pairs={{0,16},{1,17},{2,18},{3,19},{4,12},{5,13},{6,14},{7,15},{8,24},{9,... | collective-permute-start | bytes 393224 | tf_op jit(solution)/shard_map/ppermute | solution.py:88
  48.8 2.4 %collective-permute-done.23 = f32[64,512]{1,0:T(8,128)S(1)} collective-permute-done((f32[64,512]{1,0:T(8,128)S(1)}, f32[64,512]{1,0:T(8,128)S(1)}, u32[]{:S(2)}, u32[]{:S(2)}) %collective-permute-start.23) | collective-permute-done | bytes 131104 | tf_op jit(solution)/shard_map/ppermute | solution.py:88
  60.5 2.8 %collective-permute-done.16 = f32[128,512]{1,0:T(8,128)S(1)} collective-permute-done((f32[128,512]{1,0:T(8,128)S(1)}, f32[128,512]{1,0:T(8,128)S(1)}, u32[]{:S(2)}, u32[]{:S(2)}) %collective-permute-start.16) | collective-permute-done | bytes 262176 | tf_op jit(solution)/shard_map/ppermute | solution.py:88
  67.9 1.8 %collective-permute-start.26 = (f32[160,128]{1,0:T(8,128)S(1)}, f32[160,128]{1,0:T(8,128)S(1)}, u32[]{:S(2)}, u32[]{:S(2)}) collective-permute-start(f32[160,128]{1,0:T(8,128)S(1)} %get-tuple-element.25), channel_id=1, source_target_pairs={{0,16},{1,17},{2,18},{3,19},{4,12},{5,13},{6,14},{7,15},{8,24},{9,... | collective-permute-start | bytes 245768 | tf_op jit(solution)/shard_map/ppermute | solution.py:88
  72.9 1.9 %collective-permute-done.27 = f32[160,128]{1,0:T(8,128)S(1)} collective-permute-done((f32[160,128]{1,0:T(8,128)S(1)}, f32[160,128]{1,0:T(8,128)S(1)}, u32[]{:S(2)}, u32[]{:S(2)}) %collective-permute-start.27) | collective-permute-done | bytes 81952 | tf_op jit(solution)/shard_map/ppermute | solution.py:88
  76.3 1.9 %collective-permute-start.31 = (f32[160,128]{1,0:T(8,128)S(1)}, f32[160,128]{1,0:T(8,128)S(1)}, u32[]{:S(2)}, u32[]{:S(2)}) collective-permute-start(f32[160,128]{1,0:T(8,128)S(1)} %add_add_fusion.1), channel_id=1, source_target_pairs={{0,3},{1,2},{2,1},{3,0},{4,7},{5,6},{6,5},{7,4},{8,11},{9,10},{10,... | collective-permute-start | bytes 245768 | tf_op jit(solution)/shard_map/ppermute | solution.py:88
  78.2 2.5 %collective-permute-start.29 = (f32[160,128]{1,0:T(8,128)S(1)}, f32[160,128]{1,0:T(8,128)S(1)}, u32[]{:S(2)}, u32[]{:S(2)}) collective-permute-start(f32[160,128]{1,0:T(8,128)S(1)} %add_add_fusion.1), channel_id=1, source_target_pairs={{0,2},{1,3},{2,0},{3,1},{4,6},{5,7},{6,4},{7,5},{8,10},{9,11},{10,... | collective-permute-start | bytes 245768 | tf_op jit(solution)/shard_map/ppermute | solution.py:88
  80.8 2.3 %collective-permute-done.31 = f32[160,128]{1,0:T(8,128)S(1)} collective-permute-done((f32[160,128]{1,0:T(8,128)S(1)}, f32[160,128]{1,0:T(8,128)S(1)}, u32[]{:S(2)}, u32[]{:S(2)}) %collective-permute-start.31) | collective-permute-done | bytes 81952 | tf_op jit(solution)/shard_map/ppermute | solution.py:88
  88.9 1.9 %collective-permute-done.34 = f32[160,128]{1,0:T(8,128)S(1)} collective-permute-done((f32[160,128]{1,0:T(8,128)S(1)}, f32[160,128]{1,0:T(8,128)S(1)}, u32[]{:S(2)}, u32[]{:S(2)}) %collective-permute-start.34) | collective-permute-done | bytes 81952 | tf_op jit(solution)/shard_map/ppermute | solution.py:88
  94.4 13.3 %solve.1 = f32[512,128]{1,0:T(8,128)} custom-call(s32[3]{0:T(128)S(1)} %pad_add_fusion.where, f32[640,128]{1,0:T(8,128)S(1)} %pad_maximum_fusion.mine_ref, f32[640,128]{1,0:T(8,128)S(1)} %collective-permute-done.35.other_ref, f32[512,128]{1,0:T(8,128)S(1)} %get-tuple-element.28.p_ref), custom_call_target="tpu_custom_call" | custom-call | tf_op jit(solution)/shard_map/solve/pallas_call | solution.py:280
  (97 shorter events, 45.4 us)
Async XLA Ops:
  4.3 7.4 %collective-permute-start.17 = (f32[128,512]{1,0:T(8,128)S(1)}, f32[128,512]{1,0:T(8,128)S(1)}, u32[]{:S(2)}, u32[]{:S(2)}) collective-permute-start(f32[128,512]{1,0:T(8,128)S(1)} %get-tuple-element.23), channel_id=1, source_target_pairs={{0,8},{1,9},{2,10},{3,11},{4,20},{5,21},{6,22},{7,23},{8,0},{9,1},... | collective-permute-start | bytes 786440 | tf_op jit(solution)/shard_map/ppermute | solution.py:88
  8.4 7.4 %collective-permute-start.9 = (f32[128,512]{1,0:T(8,128)S(1)}, f32[128,512]{1,0:T(8,128)S(1)}, u32[]{:S(2)}, u32[]{:S(2)}) collective-permute-start(f32[128,512]{1,0:T(8,128)S(1)} %get-tuple-element.21), channel_id=1, source_target_pairs={{0,8},{1,9},{2,10},{3,11},{4,20},{5,21},{6,22},{7,23},{8,0},{9,1},... | collective-permute-start | bytes 786440 | tf_op jit(solution)/shard_map/ppermute | solution.py:88
  9.6 10.8 %collective-permute-start.1 = (f32[128,512]{1,0:T(8,128)S(1)}, f32[128,512]{1,0:T(8,128)S(1)}, u32[]{:S(2)}, u32[]{:S(2)}) collective-permute-start(f32[128,512]{1,0:T(8,128)S(1)} %get-tuple-element.19), channel_id=1, source_target_pairs={{0,8},{1,9},{2,10},{3,11},{4,20},{5,21},{6,22},{7,23},{8,0},{9,1},... | collective-permute-start | bytes 786440 | tf_op jit(solution)/shard_map/ppermute | solution.py:88
  11.7 10.4 %collective-permute-start.18 = (f32[64,512]{1,0:T(8,128)S(1)}, f32[64,512]{1,0:T(8,128)S(1)}, u32[]{:S(2)}, u32[]{:S(2)}) collective-permute-start(f32[64,512]{1,0:T(8,128)S(1)} %get-tuple-element.36), channel_id=1, source_target_pairs={{0,16},{1,17},{2,18},{3,19},{4,12},{5,13},{6,14},{7,15},{8,24},{9,... | collective-permute-start | bytes 393224 | tf_op jit(solution)/shard_map/ppermute | solution.py:88
  15.8 8.1 %collective-permute-start.10 = (f32[64,512]{1,0:T(8,128)S(1)}, f32[64,512]{1,0:T(8,128)S(1)}, u32[]{:S(2)}, u32[]{:S(2)}) collective-permute-start(f32[64,512]{1,0:T(8,128)S(1)} %get-tuple-element.38), channel_id=1, source_target_pairs={{0,16},{1,17},{2,18},{3,19},{4,12},{5,13},{6,14},{7,15},{8,24},{9,... | collective-permute-start | bytes 393224 | tf_op jit(solution)/shard_map/ppermute | solution.py:88
  22.2 5.1 %collective-permute-start.19 = (f32[32,512]{1,0:T(8,128)S(1)}, f32[32,512]{1,0:T(8,128)S(1)}, u32[]{:S(2)}, u32[]{:S(2)}) collective-permute-start(f32[32,512]{1,0:T(8,128)S(1)} %get-tuple-element.42), channel_id=1, source_target_pairs={{0,1},{1,0},{2,3},{3,2},{4,5},{5,4},{6,7},{7,6},{8,9},{9,8},{10,11... | collective-permute-start | bytes 196616 | tf_op jit(solution)/shard_map/ppermute | solution.py:88
  23.9 6.1 %collective-permute-start.11 = (f32[32,512]{1,0:T(8,128)S(1)}, f32[32,512]{1,0:T(8,128)S(1)}, u32[]{:S(2)}, u32[]{:S(2)}) collective-permute-start(f32[32,512]{1,0:T(8,128)S(1)} %get-tuple-element.44), channel_id=1, source_target_pairs={{0,1},{1,0},{2,3},{3,2},{4,5},{5,4},{6,7},{7,6},{8,9},{9,8},{10,11... | collective-permute-start | bytes 196616 | tf_op jit(solution)/shard_map/ppermute | solution.py:88
  25.5 5.9 %collective-permute-start.3 = (f32[32,512]{1,0:T(8,128)S(1)}, f32[32,512]{1,0:T(8,128)S(1)}, u32[]{:S(2)}, u32[]{:S(2)}) collective-permute-start(f32[32,512]{1,0:T(8,128)S(1)} %get-tuple-element.46), channel_id=1, source_target_pairs={{0,1},{1,0},{2,3},{3,2},{4,5},{5,4},{6,7},{7,6},{8,9},{9,8},{10,11... | collective-permute-start | bytes 196616 | tf_op jit(solution)/shard_map/ppermute | solution.py:88
  27.3 5.8 %collective-permute-start.20 = (f32[16,512]{1,0:T(8,128)S(1)}, f32[16,512]{1,0:T(8,128)S(1)}, u32[]{:S(2)}, u32[]{:S(2)}) collective-permute-start(f32[16,512]{1,0:T(8,128)S(1)} %slice_add_fusion.12), channel_id=1, source_target_pairs={{0,2},{1,3},{2,0},{3,1},{4,6},{5,7},{6,4},{7,5},{8,10},{9,11},{10,... | collective-permute-start | bytes 98312 | tf_op jit(solution)/shard_map/ppermute | solution.py:88
  30.0 8.3 %collective-permute-start.12 = (f32[16,512]{1,0:T(8,128)S(1)}, f32[16,512]{1,0:T(8,128)S(1)}, u32[]{:S(2)}, u32[]{:S(2)}) collective-permute-start(f32[16,512]{1,0:T(8,128)S(1)} %slice_add_fusion.14), channel_id=1, source_target_pairs={{0,2},{1,3},{2,0},{3,1},{4,6},{5,7},{6,4},{7,5},{8,10},{9,11},{10,... | collective-permute-start | bytes 98312 | tf_op jit(solution)/shard_map/ppermute | solution.py:88
  31.5 5.8 %collective-permute-start.4 = (f32[16,512]{1,0:T(8,128)S(1)}, f32[16,512]{1,0:T(8,128)S(1)}, u32[]{:S(2)}, u32[]{:S(2)}) collective-permute-start(f32[16,512]{1,0:T(8,128)S(1)} %slice_add_fusion.16), channel_id=1, source_target_pairs={{0,2},{1,3},{2,0},{3,1},{4,6},{5,7},{6,4},{7,5},{8,10},{9,11},{10,... | collective-permute-start | bytes 98312 | tf_op jit(solution)/shard_map/ppermute | solution.py:88
  33.1 7.3 %collective-permute-start.21 = (f32[16,512]{1,0:T(8,128)S(1)}, f32[16,512]{1,0:T(8,128)S(1)}, u32[]{:S(2)}, u32[]{:S(2)}) collective-permute-start(f32[16,512]{1,0:T(8,128)S(1)} %get-tuple-element.30), channel_id=1, source_target_pairs={{0,2},{1,3},{2,0},{3,1},{4,6},{5,7},{6,4},{7,5},{8,10},{9,11},{10,... | collective-permute-start | bytes 98312 | tf_op jit(solution)/shard_map/ppermute | solution.py:88
  44.8 6.4 %collective-permute-start.23 = (f32[64,512]{1,0:T(8,128)S(1)}, f32[64,512]{1,0:T(8,128)S(1)}, u32[]{:S(2)}, u32[]{:S(2)}) collective-permute-start(f32[64,512]{1,0:T(8,128)S(1)} %pad_maximum_fusion.6), channel_id=1, source_target_pairs={{0,16},{1,17},{2,18},{3,19},{4,12},{5,13},{6,14},{7,15},{8,24},{9,... | collective-permute-start | bytes 393224 | tf_op jit(solution)/shard_map/ppermute | solution.py:88
  46.5 7.5 %collective-permute-start.7 = (f32[64,512]{1,0:T(8,128)S(1)}, f32[64,512]{1,0:T(8,128)S(1)}, u32[]{:S(2)}, u32[]{:S(2)}) collective-permute-start(f32[64,512]{1,0:T(8,128)S(1)} %pad_maximum_fusion.4), channel_id=1, source_target_pairs={{0,16},{1,17},{2,18},{3,19},{4,12},{5,13},{6,14},{7,15},{8,24},{9,... | collective-permute-start | bytes 393224 | tf_op jit(solution)/shard_map/ppermute | solution.py:88
  47.4 9.3 %collective-permute-start.15 = (f32[64,512]{1,0:T(8,128)S(1)}, f32[64,512]{1,0:T(8,128)S(1)}, u32[]{:S(2)}, u32[]{:S(2)}) collective-permute-start(f32[64,512]{1,0:T(8,128)S(1)} %pad_maximum_fusion.5), channel_id=1, source_target_pairs={{0,16},{1,17},{2,18},{3,19},{4,12},{5,13},{6,14},{7,15},{8,24},{9,... | collective-permute-start | bytes 393224 | tf_op jit(solution)/shard_map/ppermute | solution.py:88
  51.2 7.2 %collective-permute-start.24 = (f32[128,512]{1,0:T(8,128)S(1)}, f32[128,512]{1,0:T(8,128)S(1)}, u32[]{:S(2)}, u32[]{:S(2)}) collective-permute-start(f32[128,512]{1,0:T(8,128)S(1)} %pad_maximum_fusion.3), channel_id=1, source_target_pairs={{0,8},{1,9},{2,10},{3,11},{4,20},{5,21},{6,22},{7,23},{8,0},{9,1},... | collective-permute-start | bytes 786440 | tf_op jit(solution)/shard_map/ppermute | solution.py:88
  54.0 6.4 %collective-permute-start.8 = (f32[128,512]{1,0:T(8,128)S(1)}, f32[128,512]{1,0:T(8,128)S(1)}, u32[]{:S(2)}, u32[]{:S(2)}) collective-permute-start(f32[128,512]{1,0:T(8,128)S(1)} %pad_maximum_fusion.1), channel_id=1, source_target_pairs={{0,8},{1,9},{2,10},{3,11},{4,20},{5,21},{6,22},{7,23},{8,0},{9,1},... | collective-permute-start | bytes 786440 | tf_op jit(solution)/shard_map/ppermute | solution.py:88
  56.8 6.5 %collective-permute-start.16 = (f32[128,512]{1,0:T(8,128)S(1)}, f32[128,512]{1,0:T(8,128)S(1)}, u32[]{:S(2)}, u32[]{:S(2)}) collective-permute-start(f32[128,512]{1,0:T(8,128)S(1)} %pad_maximum_fusion.2), channel_id=1, source_target_pairs={{0,8},{1,9},{2,10},{3,11},{4,20},{5,21},{6,22},{7,23},{8,0},{9,1},... | collective-permute-start | bytes 786440 | tf_op jit(solution)/shard_map/ppermute | solution.py:88
  69.7 5.2 %collective-permute-start.27 = (f32[160,128]{1,0:T(8,128)S(1)}, f32[160,128]{1,0:T(8,128)S(1)}, u32[]{:S(2)}, u32[]{:S(2)}) collective-permute-start(f32[160,128]{1,0:T(8,128)S(1)} %get-tuple-element.26), channel_id=1, source_target_pairs={{0,8},{1,9},{2,10},{3,11},{4,20},{5,21},{6,22},{7,23},{8,0},{9,1},... | collective-permute-start | bytes 245768 | tf_op jit(solution)/shard_map/ppermute | solution.py:88
  70.9 5.3 %collective-permute-start.28 = (f32[160,128]{1,0:T(8,128)S(1)}, f32[160,128]{1,0:T(8,128)S(1)}, u32[]{:S(2)}, u32[]{:S(2)}) collective-permute-start(f32[160,128]{1,0:T(8,128)S(1)} %get-tuple-element.27), channel_id=1, source_target_pairs={{0,24},{1,25},{2,26},{3,27},{4,28},{5,29},{6,30},{7,31},{8,16},{9,... | collective-permute-start | bytes 245768 | tf_op jit(solution)/shard_map/ppermute | solution.py:88
  76.3 6.7 %collective-permute-start.31 = (f32[160,128]{1,0:T(8,128)S(1)}, f32[160,128]{1,0:T(8,128)S(1)}, u32[]{:S(2)}, u32[]{:S(2)}) collective-permute-start(f32[160,128]{1,0:T(8,128)S(1)} %add_add_fusion.1), channel_id=1, source_target_pairs={{0,3},{1,2},{2,1},{3,0},{4,7},{5,6},{6,5},{7,4},{8,11},{9,10},{10,... | collective-permute-start | bytes 245768 | tf_op jit(solution)/shard_map/ppermute | solution.py:88
  78.2 6.3 %collective-permute-start.30 = (f32[160,128]{1,0:T(8,128)S(1)}, f32[160,128]{1,0:T(8,128)S(1)}, u32[]{:S(2)}, u32[]{:S(2)}) collective-permute-start(f32[160,128]{1,0:T(8,128)S(1)} %add_add_fusion.1), channel_id=1, source_target_pairs={{0,1},{1,0},{2,3},{3,2},{4,5},{5,4},{6,7},{7,6},{8,9},{9,8},{10,11... | collective-permute-start | bytes 245768 | tf_op jit(solution)/shard_map/ppermute | solution.py:88
  78.2 7.1 %collective-permute-start.29 = (f32[160,128]{1,0:T(8,128)S(1)}, f32[160,128]{1,0:T(8,128)S(1)}, u32[]{:S(2)}, u32[]{:S(2)}) collective-permute-start(f32[160,128]{1,0:T(8,128)S(1)} %add_add_fusion.1), channel_id=1, source_target_pairs={{0,2},{1,3},{2,0},{3,1},{4,6},{5,7},{6,4},{7,5},{8,10},{9,11},{10,... | collective-permute-start | bytes 245768 | tf_op jit(solution)/shard_map/ppermute | solution.py:88
  85.4 5.4 %collective-permute-start.34 = (f32[160,128]{1,0:T(8,128)S(1)}, f32[160,128]{1,0:T(8,128)S(1)}, u32[]{:S(2)}, u32[]{:S(2)}) collective-permute-start(f32[160,128]{1,0:T(8,128)S(1)} %add_add_fusion), channel_id=1, source_target_pairs={{0,24},{1,25},{2,26},{3,27},{4,28},{5,29},{6,30},{7,31},{8,16},{9,... | collective-permute-start | bytes 245768 | tf_op jit(solution)/shard_map/ppermute | solution.py:88
  (13 other events, 49.2 us)

commit v6 on v5

--- a/solution.py
+++ b/solution.py
@@ -52,6 +52,9 @@
             [("row", b) for b in order] + [("col", b) for b in col_bits] for order in orders
         )
         self.levels = len(self.orders[0])
+
+    def core(self):
+        return lax.axis_index("row") & 1
 
     def core_perm(self):
         c = self.cols
@@ -132,9 +135,10 @@
     send_ref[...] = bf16_dot(left_ref[half:, :], right, NT)
 
 
-def first_project_kernel(blocks, where, own_ref, peer_ref, keep_ref, send_ref, left_ref, left):
-    rows, width = left.shape[0], own_ref.shape[2]
-    core, place = where[0], where[1]
+def first_project_kernel(route, scatter, own_ref, peer_ref, keep_ref, send_ref, left_ref, left):
+    rows, width, blocks = left.shape[0], own_ref.shape[2], 1 << scatter
+    core = route.core()
+    place = route.place(core, scatter)
     size = rows // blocks
     for k in range(blocks):
         at = pl.multiple_of(core * rows + (place ^ k) * size, size)
@@ -155,11 +159,12 @@
     refs[-1][...] = value + refs[0][...] if len(refs) > 1 else value
 
 
-def last_predict_kernel(j, scale, blocks, where, m_ref, own_ref, peer_ref, sum_ref, out_ref, total):
+def last_predict_kernel(j, scale, route, scatter, m_ref, own_ref, peer_ref, sum_ref, out_ref, total):
     total[...] = term(j, scale, m_ref, own_ref, peer_ref) + sum_ref[...]
+    place, blocks = route.place(route.core(), scatter), 1 << scatter
     size = total.shape[0] // blocks
     for k in range(blocks):
-        out_ref[pl.ds(pl.multiple_of((where[1] ^ k) * size, size), size), :] = total[k * size : (k + 1) * size, :]
+        out_ref[pl.ds(pl.multiple_of((place ^ k) * size, size), size), :] = total[k * size : (k + 1) * size, :]
 
 
 def core_blocks(count):
@@ -168,12 +173,13 @@
     return blocks[:half], blocks[half:]
 
 
-def gram_kernel(parts, scale, where, mine_ref, other_ref, *refs):
+def gram_kernel(route, scale, mine_ref, other_ref, *refs):
     outs, own_ref, p, acc = refs[:-3], refs[-3], refs[-2], refs[-1]
     half, width = mine_ref.shape[0], own_ref.shape[1]
     count = 2 * half // TILE
     lists = core_blocks(count)
-    core, place = where[0], where[1]
+    parts, core = 1 << route.row_levels, route.core()
+    place = route.place(core, route.row_levels)
     here = pl.ds(pl.multiple_of(core * half, half), half)
     there = pl.ds(pl.multiple_of((1 - core) * half, half), half)
     p[here, :] = mine_ref[...]
@@ -194,12 +200,14 @@
         outs[k // each][k % each * size : (k % each + 1) * size, :] = acc[pl.ds(pl.multiple_of((place ^ k) * size, 8), size), :]
 
 
-def solve_kernel(parts, where, mine_ref, other_ref, p_ref, out_ref, natural, work, stack_a, stack_b):
+def solve_kernel(route, mine_ref, other_ref, p_ref, out_ref, natural, work, stack_a, stack_b):
     n, tile = p_ref.shape[0], TILE
     width = n + p_ref.shape[1]
     count, groups, per_panel, panels = n // tile, width // tile, PANEL // 8, tile // PANEL
-    core, size = where[0], mine_ref.shape[0] // parts
-    for ref, number, place in ((mine_ref, core, where[1]), (other_ref, 1 - core, where[2])):
+    parts, core = 1 << route.row_levels, route.core()
+    size = mine_ref.shape[0] // parts
+    for ref, number in ((mine_ref, core), (other_ref, 1 - core)):
+        place = route.place(number, route.row_levels)
         for k in range(parts):
             at = pl.multiple_of((place ^ k) * size, 8)
             natural[number, pl.ds(at, size), :] = ref[k * size : (k + 1) * size, :]
@@ -269,23 +277,22 @@
 
 
 VMEM = pl.BlockSpec(memory_space=pltpu.VMEM)
-SMEM = pl.BlockSpec(memory_space=pltpu.SMEM)
 
 
 def f32(*shape):
     return jax.ShapeDtypeStruct(shape, jnp.float32)
 
 
-def call(kernel, name, out_shape, scratch, args, scalars=None):
+def call(kernel, name, out_shape, scratch, args):
     return pl.pallas_call(
         kernel,
         name=name,
         out_shape=out_shape,
-        in_specs=([] if scalars is None else [SMEM]) + [VMEM] * len(args),
+        in_specs=[VMEM] * len(args),
         out_specs=jax.tree.map(lambda _: VMEM, out_shape),
         scratch_shapes=[pltpu.VMEM(s.shape, s.dtype) for s in scratch],
         compiler_params=pltpu.CompilerParams(vmem_limit_bytes=VMEM_LIMIT),
-    )(*([] if scalars is None else [scalars]), *args)
+    )(*args)
 
 
 def on_device(rows, cols, history):
@@ -293,15 +300,9 @@
     terms, norb, width = history.shape
     total = width * rows * cols
     half = norb // 2
-    core = lax.axis_index("row") & 1
 
     levels = route.levels
     scatter = min(levels, (half // 8).bit_length() - 1)
-    blocks = 1 << scatter
-    where_m = jnp.stack([core, route.place(core, scatter)])
-    parts_levels = route.row_levels
-    parts = 1 << parts_levels
-    where_g = jnp.stack([core, route.place(core, parts_levels), route.place(1 - core, parts_levels)])
 
     peer = swap(history, route.core_perm())
     own = pl.pallas_call(
@@ -314,12 +315,11 @@
     )(history)
     out = [f32(half // 2, norb)] * 2
     keep, send, left = call(
-        functools.partial(first_project_kernel, blocks),
+        functools.partial(first_project_kernel, route, scatter),
         "project",
         out + [jax.ShapeDtypeStruct((half, 12 * width), jnp.bfloat16)],
         [f32(half, 2 * width)],
         [own, peer],
-        where_m,
     )
     products = [(keep, send)]
     for j in range(1, terms):
@@ -329,25 +329,24 @@
     for j in range(terms - 1):
         kernel = functools.partial(predict_kernel, j, WEIGHTS[j] / total)
         mine = [call(kernel, "predict", out, [], [m[j], own, peer] + mine)]
-    kernel = functools.partial(last_predict_kernel, terms - 1, WEIGHTS[terms - 1] / total, blocks)
-    mine = call(kernel, "predict", out, [out], [m[-1], own, peer] + mine, where_m)
+    kernel = functools.partial(last_predict_kernel, terms - 1, WEIGHTS[terms - 1] / total, route, scatter)
+    mine = call(kernel, "predict", out, [out], [m[-1], own, peer] + mine)
     other = swap(mine, route.core_perm())
 
     shares = (norb // TILE) * (norb // TILE + 1) // 2
     share = (shares + 1) // 2 * TILE
-    ways = 1 << min(2, parts_levels)
+    ways = 1 << min(2, route.row_levels)
     *pieces, predicted = call(
-        functools.partial(gram_kernel, parts, 1.0 / total),
+        functools.partial(gram_kernel, route, 1.0 / total),
         "gram",
         [f32(share // ways, TILE)] * ways + [f32(norb, width)],
         [f32(norb, 2 * width), f32(share, TILE)],
         [mine, other],
-        where_g,
     )
-    gram = direct_all_reduce(route, pieces, parts_levels, levels)
+    gram = direct_all_reduce(route, pieces, route.row_levels, levels)
     gram_other = swap(gram, route.core_perm())
     return call(
-        functools.partial(solve_kernel, parts),
+        functools.partial(solve_kernel, route),
         "solve",
         f32(norb, width),
         [
@@ -357,7 +356,6 @@
             jax.ShapeDtypeStruct((6 * TILE, norb + width), jnp.bfloat16),
         ],
         [gram, gram_other, predicted],
-        where_g,
     )
 
 

time: 108 us -> 106 us (0.981)
  Pallas kernels: 20.9 us -> 18.8 us
    pallas_call x8, Pallas kernels: 20.9 us -> 18.7 us  [call(): pl.pallas_call(kernel, name=name, out_shape=out_shape, in_specs=[VMEM] *...]
  transfers between devices with their start and end apart: 36 -> 36, of which waited for: 26 -> 26; matrix products, arithmetic and copies ran while one was open for 1% -> 0% of each run, Pallas kernels for 3% -> 3%
where the time goes in v6:
time: 106 us; the launch traced here: 105 us
  starting transfers between devices  46.9 us (44%)
  waiting for transfers between devices  37.9 us (36%)
  Pallas kernels  18.8 us (18%)
  local copies, waits for them, and re-layouts  1.25 us (1%)
    ppermute x36, starting transfers between devices, swap(): return lax.ppermute(x, AXES, perm)  46.9 us
    ppermute x36, waiting for transfers between devices, swap(): return lax.ppermute(x, AXES, perm)  37.9 us
    pallas_call x8, Pallas kernels, call(): pl.pallas_call(kernel, name=name, out_shape=out_shape, in_specs=[VMEM] *...  18.7 us
  transfers between devices with their start and end apart: 36, of which 26 were waited for; matrix products, arithmetic and copies ran while one was open for 0% of the time, Pallas kernels for 3%

profile of v6, /device:TPU:0, one launch (start us, length us, event | category | flops | bytes accessed | tf_op | source)
XLA Modules:
  0.0 105.5 jit_solution(10976172583667986341)
XLA Ops:
  3.8 2.9 %collective-permute-start.17 = (f32[128,512]{1,0:T(8,128)S(1)}, f32[128,512]{1,0:T(8,128)S(1)}, u32[]{:S(2)}, u32[]{:S(2)}) collective-permute-start(f32[128,512]{1,0:T(8,128)S(1)} %get-tuple-element.23), channel_id=1, source_target_pairs={{0,8},{1,9},{2,10},{3,11},{4,20},{5,21},{6,22},{7,23},{8,0},{9,1},... | collective-permute-start | bytes 786440 | tf_op jit(solution)/shard_map/ppermute | solution.py:91
  9.1 2.1 %collective-permute-start.1 = (f32[128,512]{1,0:T(8,128)S(1)}, f32[128,512]{1,0:T(8,128)S(1)}, u32[]{:S(2)}, u32[]{:S(2)}) collective-permute-start(f32[128,512]{1,0:T(8,128)S(1)} %get-tuple-element.19), channel_id=1, source_target_pairs={{0,8},{1,9},{2,10},{3,11},{4,20},{5,21},{6,22},{7,23},{8,0},{9,1},... | collective-permute-start | bytes 786440 | tf_op jit(solution)/shard_map/ppermute | solution.py:91
  11.2 2.0 %collective-permute-start.18 = (f32[64,512]{1,0:T(8,128)S(1)}, f32[64,512]{1,0:T(8,128)S(1)}, u32[]{:S(2)}, u32[]{:S(2)}) collective-permute-start(f32[64,512]{1,0:T(8,128)S(1)} %get-tuple-element.36), channel_id=1, source_target_pairs={{0,16},{1,17},{2,18},{3,19},{4,12},{5,13},{6,14},{7,15},{8,24},{9,... | collective-permute-start | bytes 393224 | tf_op jit(solution)/shard_map/ppermute | solution.py:91
  13.2 2.0 %collective-permute-done.9 = f32[128,512]{1,0:T(8,128)S(1)} collective-permute-done((f32[128,512]{1,0:T(8,128)S(1)}, f32[128,512]{1,0:T(8,128)S(1)}, u32[]{:S(2)}, u32[]{:S(2)}) %collective-permute-start.9) | collective-permute-done | bytes 262176 | tf_op jit(solution)/shard_map/ppermute | solution.py:91
  16.8 3.1 %collective-permute-done.1 = f32[128,512]{1,0:T(8,128)S(1)} collective-permute-done((f32[128,512]{1,0:T(8,128)S(1)}, f32[128,512]{1,0:T(8,128)S(1)}, u32[]{:S(2)}, u32[]{:S(2)}) %collective-permute-start.1) | collective-permute-done | bytes 262176 | tf_op jit(solution)/shard_map/ppermute | solution.py:91
  19.9 1.7 %collective-permute-start.2 = (f32[64,512]{1,0:T(8,128)S(1)}, f32[64,512]{1,0:T(8,128)S(1)}, u32[]{:S(2)}, u32[]{:S(2)}) collective-permute-start(f32[64,512]{1,0:T(8,128)S(1)} %get-tuple-element.40), channel_id=1, source_target_pairs={{0,16},{1,17},{2,18},{3,19},{4,12},{5,13},{6,14},{7,15},{8,24},{9,... | collective-permute-start | bytes 393224 | tf_op jit(solution)/shard_map/ppermute | solution.py:91
  21.7 1.6 %collective-permute-start.19 = (f32[32,512]{1,0:T(8,128)S(1)}, f32[32,512]{1,0:T(8,128)S(1)}, u32[]{:S(2)}, u32[]{:S(2)}) collective-permute-start(f32[32,512]{1,0:T(8,128)S(1)} %get-tuple-element.42), channel_id=1, source_target_pairs={{0,1},{1,0},{2,3},{3,2},{4,5},{5,4},{6,7},{7,6},{8,9},{9,8},{10,11... | collective-permute-start | bytes 196616 | tf_op jit(solution)/shard_map/ppermute | solution.py:91
  25.0 1.7 %collective-permute-start.3 = (f32[32,512]{1,0:T(8,128)S(1)}, f32[32,512]{1,0:T(8,128)S(1)}, u32[]{:S(2)}, u32[]{:S(2)}) collective-permute-start(f32[32,512]{1,0:T(8,128)S(1)} %get-tuple-element.46), channel_id=1, source_target_pairs={{0,1},{1,0},{2,3},{3,2},{4,5},{5,4},{6,7},{7,6},{8,9},{9,8},{10,11... | collective-permute-start | bytes 196616 | tf_op jit(solution)/shard_map/ppermute | solution.py:91
  26.8 2.7 %collective-permute-start.20 = (f32[16,512]{1,0:T(8,128)S(1)}, f32[16,512]{1,0:T(8,128)S(1)}, u32[]{:S(2)}, u32[]{:S(2)}) collective-permute-start(f32[16,512]{1,0:T(8,128)S(1)} %slice_add_fusion.12), channel_id=1, source_target_pairs={{0,2},{1,3},{2,0},{3,1},{4,6},{5,7},{6,4},{7,5},{8,10},{9,11},{10,... | collective-permute-start | bytes 98312 | tf_op jit(solution)/shard_map/ppermute | solution.py:91
  32.6 1.8 %collective-permute-start.21 = (f32[16,512]{1,0:T(8,128)S(1)}, f32[16,512]{1,0:T(8,128)S(1)}, u32[]{:S(2)}, u32[]{:S(2)}) collective-permute-start(f32[16,512]{1,0:T(8,128)S(1)} %get-tuple-element.30), channel_id=1, source_target_pairs={{0,2},{1,3},{2,0},{3,1},{4,6},{5,7},{6,4},{7,5},{8,10},{9,11},{10,... | collective-permute-start | bytes 98312 | tf_op jit(solution)/shard_map/ppermute | solution.py:91
  34.4 2.4 %collective-permute-done.4 = f32[16,512]{1,0:T(8,128)S(1)} collective-permute-done((f32[16,512]{1,0:T(8,128)S(1)}, f32[16,512]{1,0:T(8,128)S(1)}, u32[]{:S(2)}, u32[]{:S(2)}) %collective-permute-start.4) | collective-permute-done | bytes 32800 | tf_op jit(solution)/shard_map/ppermute | solution.py:91
  37.7 2.1 %collective-permute-start.13 = (f32[16,512]{1,0:T(8,128)S(1)}, f32[16,512]{1,0:T(8,128)S(1)}, u32[]{:S(2)}, u32[]{:S(2)}) collective-permute-start(f32[16,512]{1,0:T(8,128)S(1)} %get-tuple-element.32), channel_id=1, source_target_pairs={{0,2},{1,3},{2,0},{3,1},{4,6},{5,7},{6,4},{7,5},{8,10},{9,11},{10,... | collective-permute-start | bytes 98312 | tf_op jit(solution)/shard_map/ppermute | solution.py:91
  40.0 1.7 %collective-permute-done.5 = f32[16,512]{1,0:T(8,128)S(1)} collective-permute-done((f32[16,512]{1,0:T(8,128)S(1)}, f32[16,512]{1,0:T(8,128)S(1)}, u32[]{:S(2)}, u32[]{:S(2)}) %collective-permute-start.5) | collective-permute-done | bytes 32800 | tf_op jit(solution)/shard_map/ppermute | solution.py:91
  44.2 1.8 %collective-permute-start.23 = (f32[64,512]{1,0:T(8,128)S(1)}, f32[64,512]{1,0:T(8,128)S(1)}, u32[]{:S(2)}, u32[]{:S(2)}) collective-permute-start(f32[64,512]{1,0:T(8,128)S(1)} %pad_maximum_fusion.6), channel_id=1, source_target_pairs={{0,16},{1,17},{2,18},{3,19},{4,12},{5,13},{6,14},{7,15},{8,24},{9,... | collective-permute-start | bytes 393224 | tf_op jit(solution)/shard_map/ppermute | solution.py:91
  48.2 2.4 %collective-permute-done.23 = f32[64,512]{1,0:T(8,128)S(1)} collective-permute-done((f32[64,512]{1,0:T(8,128)S(1)}, f32[64,512]{1,0:T(8,128)S(1)}, u32[]{:S(2)}, u32[]{:S(2)}) %collective-permute-start.23) | collective-permute-done | bytes 131104 | tf_op jit(solution)/shard_map/ppermute | solution.py:91
  60.0 2.8 %collective-permute-done.16 = f32[128,512]{1,0:T(8,128)S(1)} collective-permute-done((f32[128,512]{1,0:T(8,128)S(1)}, f32[128,512]{1,0:T(8,128)S(1)}, u32[]{:S(2)}, u32[]{:S(2)}) %collective-permute-start.16) | collective-permute-done | bytes 262176 | tf_op jit(solution)/shard_map/ppermute | solution.py:91
  66.3 1.8 %collective-permute-start.26 = (f32[160,128]{1,0:T(8,128)S(1)}, f32[160,128]{1,0:T(8,128)S(1)}, u32[]{:S(2)}, u32[]{:S(2)}) collective-permute-start(f32[160,128]{1,0:T(8,128)S(1)} %get-tuple-element.25), channel_id=1, source_target_pairs={{0,16},{1,17},{2,18},{3,19},{4,12},{5,13},{6,14},{7,15},{8,24},{9,... | collective-permute-start | bytes 245768 | tf_op jit(solution)/shard_map/ppermute | solution.py:91
  71.4 1.9 %collective-permute-done.27 = f32[160,128]{1,0:T(8,128)S(1)} collective-permute-done((f32[160,128]{1,0:T(8,128)S(1)}, f32[160,128]{1,0:T(8,128)S(1)}, u32[]{:S(2)}, u32[]{:S(2)}) %collective-permute-start.27) | collective-permute-done | bytes 81952 | tf_op jit(solution)/shard_map/ppermute | solution.py:91
  74.7 1.9 %collective-permute-start.31 = (f32[160,128]{1,0:T(8,128)S(1)}, f32[160,128]{1,0:T(8,128)S(1)}, u32[]{:S(2)}, u32[]{:S(2)}) collective-permute-start(f32[160,128]{1,0:T(8,128)S(1)} %add_add_fusion.1), channel_id=1, source_target_pairs={{0,3},{1,2},{2,1},{3,0},{4,7},{5,6},{6,5},{7,4},{8,11},{9,10},{10,... | collective-permute-start | bytes 245768 | tf_op jit(solution)/shard_map/ppermute | solution.py:91
  76.6 2.5 %collective-permute-start.29 = (f32[160,128]{1,0:T(8,128)S(1)}, f32[160,128]{1,0:T(8,128)S(1)}, u32[]{:S(2)}, u32[]{:S(2)}) collective-permute-start(f32[160,128]{1,0:T(8,128)S(1)} %add_add_fusion.1), channel_id=1, source_target_pairs={{0,2},{1,3},{2,0},{3,1},{4,6},{5,7},{6,4},{7,5},{8,10},{9,11},{10,... | collective-permute-start | bytes 245768 | tf_op jit(solution)/shard_map/ppermute | solution.py:91
  79.2 2.2 %collective-permute-done.31 = f32[160,128]{1,0:T(8,128)S(1)} collective-permute-done((f32[160,128]{1,0:T(8,128)S(1)}, f32[160,128]{1,0:T(8,128)S(1)}, u32[]{:S(2)}, u32[]{:S(2)}) %collective-permute-start.31) | collective-permute-done | bytes 81952 | tf_op jit(solution)/shard_map/ppermute | solution.py:91
  87.3 1.9 %collective-permute-done.34 = f32[160,128]{1,0:T(8,128)S(1)} collective-permute-done((f32[160,128]{1,0:T(8,128)S(1)}, f32[160,128]{1,0:T(8,128)S(1)}, u32[]{:S(2)}, u32[]{:S(2)}) %collective-permute-start.34) | collective-permute-done | bytes 81952 | tf_op jit(solution)/shard_map/ppermute | solution.py:91
  91.1 1.6 %collective-permute-done.35.other_ref = f32[640,128]{1,0:T(8,128)S(1)} collective-permute-done((f32[640,128]{1,0:T(8,128)S(1)}, f32[640,128]{1,0:T(8,128)S(1)}, u32[]{:S(2)}, u32[]{:S(2)}) %collective-permute-start.35) | collective-permute-done | bytes 327712 | tf_op jit(solution)/shard_map/ppermute | solution.py:91
  92.7 12.8 %solve.1 = f32[512,128]{1,0:T(8,128)} custom-call(f32[640,128]{1,0:T(8,128)S(1)} %pad_maximum_fusion.mine_ref, f32[640,128]{1,0:T(8,128)S(1)} %collective-permute-done.35.other_ref, f32[512,128]{1,0:T(8,128)S(1)} %get-tuple-element.28.p_ref), custom_call_target="tpu_custom_call" | custom-call | tf_op jit(solution)/shard_map/solve/pallas_call | solution.py:287
  (95 shorter events, 43.8 us)
Async XLA Ops:
  3.8 7.4 %collective-permute-start.17 = (f32[128,512]{1,0:T(8,128)S(1)}, f32[128,512]{1,0:T(8,128)S(1)}, u32[]{:S(2)}, u32[]{:S(2)}) collective-permute-start(f32[128,512]{1,0:T(8,128)S(1)} %get-tuple-element.23), channel_id=1, source_target_pairs={{0,8},{1,9},{2,10},{3,11},{4,20},{5,21},{6,22},{7,23},{8,0},{9,1},... | collective-permute-start | bytes 786440 | tf_op jit(solution)/shard_map/ppermute | solution.py:91
  7.8 7.4 %collective-permute-start.9 = (f32[128,512]{1,0:T(8,128)S(1)}, f32[128,512]{1,0:T(8,128)S(1)}, u32[]{:S(2)}, u32[]{:S(2)}) collective-permute-start(f32[128,512]{1,0:T(8,128)S(1)} %get-tuple-element.21), channel_id=1, source_target_pairs={{0,8},{1,9},{2,10},{3,11},{4,20},{5,21},{6,22},{7,23},{8,0},{9,1},... | collective-permute-start | bytes 786440 | tf_op jit(solution)/shard_map/ppermute | solution.py:91
  9.1 10.8 %collective-permute-start.1 = (f32[128,512]{1,0:T(8,128)S(1)}, f32[128,512]{1,0:T(8,128)S(1)}, u32[]{:S(2)}, u32[]{:S(2)}) collective-permute-start(f32[128,512]{1,0:T(8,128)S(1)} %get-tuple-element.19), channel_id=1, source_target_pairs={{0,8},{1,9},{2,10},{3,11},{4,20},{5,21},{6,22},{7,23},{8,0},{9,1},... | collective-permute-start | bytes 786440 | tf_op jit(solution)/shard_map/ppermute | solution.py:91
  11.2 10.4 %collective-permute-start.18 = (f32[64,512]{1,0:T(8,128)S(1)}, f32[64,512]{1,0:T(8,128)S(1)}, u32[]{:S(2)}, u32[]{:S(2)}) collective-permute-start(f32[64,512]{1,0:T(8,128)S(1)} %get-tuple-element.36), channel_id=1, source_target_pairs={{0,16},{1,17},{2,18},{3,19},{4,12},{5,13},{6,14},{7,15},{8,24},{9,... | collective-permute-start | bytes 393224 | tf_op jit(solution)/shard_map/ppermute | solution.py:91
  15.3 8.0 %collective-permute-start.10 = (f32[64,512]{1,0:T(8,128)S(1)}, f32[64,512]{1,0:T(8,128)S(1)}, u32[]{:S(2)}, u32[]{:S(2)}) collective-permute-start(f32[64,512]{1,0:T(8,128)S(1)} %get-tuple-element.38), channel_id=1, source_target_pairs={{0,16},{1,17},{2,18},{3,19},{4,12},{5,13},{6,14},{7,15},{8,24},{9,... | collective-permute-start | bytes 393224 | tf_op jit(solution)/shard_map/ppermute | solution.py:91
  21.7 5.1 %collective-permute-start.19 = (f32[32,512]{1,0:T(8,128)S(1)}, f32[32,512]{1,0:T(8,128)S(1)}, u32[]{:S(2)}, u32[]{:S(2)}) collective-permute-start(f32[32,512]{1,0:T(8,128)S(1)} %get-tuple-element.42), channel_id=1, source_target_pairs={{0,1},{1,0},{2,3},{3,2},{4,5},{5,4},{6,7},{7,6},{8,9},{9,8},{10,11... | collective-permute-start | bytes 196616 | tf_op jit(solution)/shard_map/ppermute | solution.py:91
  23.3 6.1 %collective-permute-start.11 = (f32[32,512]{1,0:T(8,128)S(1)}, f32[32,512]{1,0:T(8,128)S(1)}, u32[]{:S(2)}, u32[]{:S(2)}) collective-permute-start(f32[32,512]{1,0:T(8,128)S(1)} %get-tuple-element.44), channel_id=1, source_target_pairs={{0,1},{1,0},{2,3},{3,2},{4,5},{5,4},{6,7},{7,6},{8,9},{9,8},{10,11... | collective-permute-start | bytes 196616 | tf_op jit(solution)/shard_map/ppermute | solution.py:91
  25.0 5.9 %collective-permute-start.3 = (f32[32,512]{1,0:T(8,128)S(1)}, f32[32,512]{1,0:T(8,128)S(1)}, u32[]{:S(2)}, u32[]{:S(2)}) collective-permute-start(f32[32,512]{1,0:T(8,128)S(1)} %get-tuple-element.46), channel_id=1, source_target_pairs={{0,1},{1,0},{2,3},{3,2},{4,5},{5,4},{6,7},{7,6},{8,9},{9,8},{10,11... | collective-permute-start | bytes 196616 | tf_op jit(solution)/shard_map/ppermute | solution.py:91
  26.8 5.8 %collective-permute-start.20 = (f32[16,512]{1,0:T(8,128)S(1)}, f32[16,512]{1,0:T(8,128)S(1)}, u32[]{:S(2)}, u32[]{:S(2)}) collective-permute-start(f32[16,512]{1,0:T(8,128)S(1)} %slice_add_fusion.12), channel_id=1, source_target_pairs={{0,2},{1,3},{2,0},{3,1},{4,6},{5,7},{6,4},{7,5},{8,10},{9,11},{10,... | collective-permute-start | bytes 98312 | tf_op jit(solution)/shard_map/ppermute | solution.py:91
  29.4 8.3 %collective-permute-start.12 = (f32[16,512]{1,0:T(8,128)S(1)}, f32[16,512]{1,0:T(8,128)S(1)}, u32[]{:S(2)}, u32[]{:S(2)}) collective-permute-start(f32[16,512]{1,0:T(8,128)S(1)} %slice_add_fusion.14), channel_id=1, source_target_pairs={{0,2},{1,3},{2,0},{3,1},{4,6},{5,7},{6,4},{7,5},{8,10},{9,11},{10,... | collective-permute-start | bytes 98312 | tf_op jit(solution)/shard_map/ppermute | solution.py:91
  30.9 5.8 %collective-permute-start.4 = (f32[16,512]{1,0:T(8,128)S(1)}, f32[16,512]{1,0:T(8,128)S(1)}, u32[]{:S(2)}, u32[]{:S(2)}) collective-permute-start(f32[16,512]{1,0:T(8,128)S(1)} %slice_add_fusion.16), channel_id=1, source_target_pairs={{0,2},{1,3},{2,0},{3,1},{4,6},{5,7},{6,4},{7,5},{8,10},{9,11},{10,... | collective-permute-start | bytes 98312 | tf_op jit(solution)/shard_map/ppermute | solution.py:91
  32.6 7.3 %collective-permute-start.21 = (f32[16,512]{1,0:T(8,128)S(1)}, f32[16,512]{1,0:T(8,128)S(1)}, u32[]{:S(2)}, u32[]{:S(2)}) collective-permute-start(f32[16,512]{1,0:T(8,128)S(1)} %get-tuple-element.30), channel_id=1, source_target_pairs={{0,2},{1,3},{2,0},{3,1},{4,6},{5,7},{6,4},{7,5},{8,10},{9,11},{10,... | collective-permute-start | bytes 98312 | tf_op jit(solution)/shard_map/ppermute | solution.py:91
  44.2 6.4 %collective-permute-start.23 = (f32[64,512]{1,0:T(8,128)S(1)}, f32[64,512]{1,0:T(8,128)S(1)}, u32[]{:S(2)}, u32[]{:S(2)}) collective-permute-start(f32[64,512]{1,0:T(8,128)S(1)} %pad_maximum_fusion.6), channel_id=1, source_target_pairs={{0,16},{1,17},{2,18},{3,19},{4,12},{5,13},{6,14},{7,15},{8,24},{9,... | collective-permute-start | bytes 393224 | tf_op jit(solution)/shard_map/ppermute | solution.py:91
  46.0 7.5 %collective-permute-start.7 = (f32[64,512]{1,0:T(8,128)S(1)}, f32[64,512]{1,0:T(8,128)S(1)}, u32[]{:S(2)}, u32[]{:S(2)}) collective-permute-start(f32[64,512]{1,0:T(8,128)S(1)} %pad_maximum_fusion.4), channel_id=1, source_target_pairs={{0,16},{1,17},{2,18},{3,19},{4,12},{5,13},{6,14},{7,15},{8,24},{9,... | collective-permute-start | bytes 393224 | tf_op jit(solution)/shard_map/ppermute | solution.py:91
  46.9 9.3 %collective-permute-start.15 = (f32[64,512]{1,0:T(8,128)S(1)}, f32[64,512]{1,0:T(8,128)S(1)}, u32[]{:S(2)}, u32[]{:S(2)}) collective-permute-start(f32[64,512]{1,0:T(8,128)S(1)} %pad_maximum_fusion.5), channel_id=1, source_target_pairs={{0,16},{1,17},{2,18},{3,19},{4,12},{5,13},{6,14},{7,15},{8,24},{9,... | collective-permute-start | bytes 393224 | tf_op jit(solution)/shard_map/ppermute | solution.py:91
  50.7 7.2 %collective-permute-start.24 = (f32[128,512]{1,0:T(8,128)S(1)}, f32[128,512]{1,0:T(8,128)S(1)}, u32[]{:S(2)}, u32[]{:S(2)}) collective-permute-start(f32[128,512]{1,0:T(8,128)S(1)} %pad_maximum_fusion.3), channel_id=1, source_target_pairs={{0,8},{1,9},{2,10},{3,11},{4,20},{5,21},{6,22},{7,23},{8,0},{9,1},... | collective-permute-start | bytes 786440 | tf_op jit(solution)/shard_map/ppermute | solution.py:91
  53.5 6.4 %collective-permute-start.8 = (f32[128,512]{1,0:T(8,128)S(1)}, f32[128,512]{1,0:T(8,128)S(1)}, u32[]{:S(2)}, u32[]{:S(2)}) collective-permute-start(f32[128,512]{1,0:T(8,128)S(1)} %pad_maximum_fusion.1), channel_id=1, source_target_pairs={{0,8},{1,9},{2,10},{3,11},{4,20},{5,21},{6,22},{7,23},{8,0},{9,1},... | collective-permute-start | bytes 786440 | tf_op jit(solution)/shard_map/ppermute | solution.py:91
  56.2 6.5 %collective-permute-start.16 = (f32[128,512]{1,0:T(8,128)S(1)}, f32[128,512]{1,0:T(8,128)S(1)}, u32[]{:S(2)}, u32[]{:S(2)}) collective-permute-start(f32[128,512]{1,0:T(8,128)S(1)} %pad_maximum_fusion.2), channel_id=1, source_target_pairs={{0,8},{1,9},{2,10},{3,11},{4,20},{5,21},{6,22},{7,23},{8,0},{9,1},... | collective-permute-start | bytes 786440 | tf_op jit(solution)/shard_map/ppermute | solution.py:91
  68.1 5.2 %collective-permute-start.27 = (f32[160,128]{1,0:T(8,128)S(1)}, f32[160,128]{1,0:T(8,128)S(1)}, u32[]{:S(2)}, u32[]{:S(2)}) collective-permute-start(f32[160,128]{1,0:T(8,128)S(1)} %get-tuple-element.26), channel_id=1, source_target_pairs={{0,8},{1,9},{2,10},{3,11},{4,20},{5,21},{6,22},{7,23},{8,0},{9,1},... | collective-permute-start | bytes 245768 | tf_op jit(solution)/shard_map/ppermute | solution.py:91
  69.4 5.3 %collective-permute-start.28 = (f32[160,128]{1,0:T(8,128)S(1)}, f32[160,128]{1,0:T(8,128)S(1)}, u32[]{:S(2)}, u32[]{:S(2)}) collective-permute-start(f32[160,128]{1,0:T(8,128)S(1)} %get-tuple-element.27), channel_id=1, source_target_pairs={{0,24},{1,25},{2,26},{3,27},{4,28},{5,29},{6,30},{7,31},{8,16},{9,... | collective-permute-start | bytes 245768 | tf_op jit(solution)/shard_map/ppermute | solution.py:91
  74.7 6.7 %collective-permute-start.31 = (f32[160,128]{1,0:T(8,128)S(1)}, f32[160,128]{1,0:T(8,128)S(1)}, u32[]{:S(2)}, u32[]{:S(2)}) collective-permute-start(f32[160,128]{1,0:T(8,128)S(1)} %add_add_fusion.1), channel_id=1, source_target_pairs={{0,3},{1,2},{2,1},{3,0},{4,7},{5,6},{6,5},{7,4},{8,11},{9,10},{10,... | collective-permute-start | bytes 245768 | tf_op jit(solution)/shard_map/ppermute | solution.py:91
  76.6 6.3 %collective-permute-start.30 = (f32[160,128]{1,0:T(8,128)S(1)}, f32[160,128]{1,0:T(8,128)S(1)}, u32[]{:S(2)}, u32[]{:S(2)}) collective-permute-start(f32[160,128]{1,0:T(8,128)S(1)} %add_add_fusion.1), channel_id=1, source_target_pairs={{0,1},{1,0},{2,3},{3,2},{4,5},{5,4},{6,7},{7,6},{8,9},{9,8},{10,11... | collective-permute-start | bytes 245768 | tf_op jit(solution)/shard_map/ppermute | solution.py:91
  76.6 7.1 %collective-permute-start.29 = (f32[160,128]{1,0:T(8,128)S(1)}, f32[160,128]{1,0:T(8,128)S(1)}, u32[]{:S(2)}, u32[]{:S(2)}) collective-permute-start(f32[160,128]{1,0:T(8,128)S(1)} %add_add_fusion.1), channel_id=1, source_target_pairs={{0,2},{1,3},{2,0},{3,1},{4,6},{5,7},{6,4},{7,5},{8,10},{9,11},{10,... | collective-permute-start | bytes 245768 | tf_op jit(solution)/shard_map/ppermute | solution.py:91
  83.8 5.4 %collective-permute-start.34 = (f32[160,128]{1,0:T(8,128)S(1)}, f32[160,128]{1,0:T(8,128)S(1)}, u32[]{:S(2)}, u32[]{:S(2)}) collective-permute-start(f32[160,128]{1,0:T(8,128)S(1)} %add_add_fusion), channel_id=1, source_target_pairs={{0,24},{1,25},{2,26},{3,27},{4,28},{5,29},{6,30},{7,31},{8,16},{9,... | collective-permute-start | bytes 245768 | tf_op jit(solution)/shard_map/ppermute | solution.py:91
  (13 other events, 49.1 us)

commit v7 on v6

--- a/solution.py
+++ b/solution.py
@@ -6,6 +6,7 @@
 from jax.experimental import pallas as pl
 from jax.experimental.pallas import tpu as pltpu
 from jax.sharding import PartitionSpec as P
+
 
 HIGHEST = lax.Precision.HIGHEST
 WEIGHTS = (2.5, -2.0, 0.5)
@@ -53,6 +54,9 @@
         )
         self.levels = len(self.orders[0])
 
+    def scatter(self, norb):
+        return min(self.levels, (norb // 16).bit_length() - 1)
+
     def core(self):
         return lax.axis_index("row") & 1
 
@@ -92,17 +96,20 @@
 
 
 def all_reduce(route, keep, send, scatter, levels):
+    def step(x, level):
+        return swap(x, route.perm(level))
+
     for level in range(scatter):
-        got = swap(send, route.perm(level))
+        got = step(send, level)
         if level < scatter - 1:
             half = keep.shape[0] // 2
             keep, send = keep[:half] + got[:half], keep[half:] + got[half:]
         else:
             keep = keep + got
     for level in range(scatter, levels):
-        keep = keep + swap(keep, route.perm(level))
+        keep = keep + step(keep, level)
     for level in reversed(range(scatter)):
-        keep = jnp.concatenate([keep, swap(keep, route.perm(level))], axis=0)
+        keep = jnp.concatenate([keep, step(keep, level)], axis=0)
     return keep
 
 
@@ -283,10 +290,9 @@
     return jax.ShapeDtypeStruct(shape, jnp.float32)
 
 
-def call(kernel, name, out_shape, scratch, args):
+def call(kernel, out_shape, scratch, args):
     return pl.pallas_call(
         kernel,
-        name=name,
         out_shape=out_shape,
         in_specs=[VMEM] * len(args),
         out_specs=jax.tree.map(lambda _: VMEM, out_shape),
@@ -296,13 +302,16 @@
 
 
 def on_device(rows, cols, history):
+    return orbitals(rows, cols, history)
+
+
+def orbitals(rows, cols, history):
     route = Route(rows, cols)
     terms, norb, width = history.shape
     total = width * rows * cols
     half = norb // 2
 
-    levels = route.levels
-    scatter = min(levels, (half // 8).bit_length() - 1)
+    levels, scatter = route.levels, route.scatter(norb)
 
     peer = swap(history, route.core_perm())
     own = pl.pallas_call(
@@ -316,21 +325,20 @@
     out = [f32(half // 2, norb)] * 2
     keep, send, left = call(
         functools.partial(first_project_kernel, route, scatter),
-        "project",
         out + [jax.ShapeDtypeStruct((half, 12 * width), jnp.bfloat16)],
         [f32(half, 2 * width)],
         [own, peer],
     )
     products = [(keep, send)]
     for j in range(1, terms):
-        products.append(call(functools.partial(project_kernel, j), "project", out, [], [left, own, peer]))
+        products.append(call(functools.partial(project_kernel, j), out, [], [left, own, peer]))
     m = [all_reduce(route, keep, send, scatter, levels) for keep, send in products]
     out, mine = f32(half, 2 * width), []
     for j in range(terms - 1):
         kernel = functools.partial(predict_kernel, j, WEIGHTS[j] / total)
-        mine = [call(kernel, "predict", out, [], [m[j], own, peer] + mine)]
+        mine = [call(kernel, out, [], [m[j], own, peer] + mine)]
     kernel = functools.partial(last_predict_kernel, terms - 1, WEIGHTS[terms - 1] / total, route, scatter)
-    mine = call(kernel, "predict", out, [out], [m[-1], own, peer] + mine)
+    mine = call(kernel, out, [out], [m[-1], own, peer] + mine)
     other = swap(mine, route.core_perm())
 
     shares = (norb // TILE) * (norb // TILE + 1) // 2
@@ -338,7 +346,6 @@
     ways = 1 << min(2, route.row_levels)
     *pieces, predicted = call(
         functools.partial(gram_kernel, route, 1.0 / total),
-        "gram",
         [f32(share // ways, TILE)] * ways + [f32(norb, width)],
         [f32(norb, 2 * width), f32(share, TILE)],
         [mine, other],
@@ -347,7 +354,6 @@
     gram_other = swap(gram, route.core_perm())
     return call(
         functools.partial(solve_kernel, route),
-        "solve",
         f32(norb, width),
         [
             f32(2, share, TILE),
@@ -360,10 +366,16 @@
 
 
 def solution(mesh):
-    return jax.shard_map(
-        functools.partial(on_device, mesh.shape["row"], mesh.shape["col"]),
-        mesh=mesh,
-        in_specs=(P(None, None, ("row", "col")),),
-        out_specs=P(None, ("row", "col")),
-        check_vma=False,
-    )
+    rows, cols = mesh.shape["row"], mesh.shape["col"]
+
+    def program(history):
+        step = jax.shard_map(
+            functools.partial(on_device, rows, cols),
+            mesh=mesh,
+            in_specs=(P(None, None, AXES),),
+            out_specs=P(None, AXES),
+            check_vma=False,
+        )
+        return step(history)
+
+    return program

time: 106 us -> 106 us (level)
  no operation moved by 1% of the time
where the time goes in v7:
time: 106 us; the launch traced here: 105 us
  starting transfers between devices  46.9 us (44%)
  waiting for transfers between devices  37.9 us (36%)
  Pallas kernels  18.8 us (18%)
  local copies, waits for them, and re-layouts  1.25 us (1%)
    ppermute x36, starting transfers between devices, swap(): return lax.ppermute(x, AXES, perm)  46.9 us
    ppermute x36, waiting for transfers between devices, swap(): return lax.ppermute(x, AXES, perm)  37.9 us
    pallas_call x8, Pallas kernels, call(): pl.pallas_call(kernel, out_shape=out_shape, in_specs=[VMEM] * len(args),...  18.7 us
  transfers between devices with their start and end apart: 36, of which 26 were waited for; matrix products, arithmetic and copies ran while one was open for 0% of the time, Pallas kernels for 3%

profile of v7, /device:TPU:0, one launch (start us, length us, event | category | flops | bytes accessed | tf_op | source)
XLA Modules:
  0.0 105.5 jit_solution(10976172583667986341)
XLA Ops:
  3.8 2.9 %collective-permute-start.17 = (f32[128,512]{1,0:T(8,128)S(1)}, f32[128,512]{1,0:T(8,128)S(1)}, u32[]{:S(2)}, u32[]{:S(2)}) collective-permute-start(f32[128,512]{1,0:T(8,128)S(1)} %get-tuple-element.23), channel_id=1, source_target_pairs={{0,8},{1,9},{2,10},{3,11},{4,20},{5,21},{6,22},{7,23},{8,0},{9,1},... | collective-permute-start | bytes 786440 | tf_op jit(solution)/shard_map/ppermute | solution.py:95
  9.1 2.1 %collective-permute-start.1 = (f32[128,512]{1,0:T(8,128)S(1)}, f32[128,512]{1,0:T(8,128)S(1)}, u32[]{:S(2)}, u32[]{:S(2)}) collective-permute-start(f32[128,512]{1,0:T(8,128)S(1)} %get-tuple-element.19), channel_id=1, source_target_pairs={{0,8},{1,9},{2,10},{3,11},{4,20},{5,21},{6,22},{7,23},{8,0},{9,1},... | collective-permute-start | bytes 786440 | tf_op jit(solution)/shard_map/ppermute | solution.py:95
  11.2 2.0 %collective-permute-start.18 = (f32[64,512]{1,0:T(8,128)S(1)}, f32[64,512]{1,0:T(8,128)S(1)}, u32[]{:S(2)}, u32[]{:S(2)}) collective-permute-start(f32[64,512]{1,0:T(8,128)S(1)} %get-tuple-element.36), channel_id=1, source_target_pairs={{0,16},{1,17},{2,18},{3,19},{4,12},{5,13},{6,14},{7,15},{8,24},{9,... | collective-permute-start | bytes 393224 | tf_op jit(solution)/shard_map/ppermute | solution.py:95
  13.2 2.0 %collective-permute-done.9 = f32[128,512]{1,0:T(8,128)S(1)} collective-permute-done((f32[128,512]{1,0:T(8,128)S(1)}, f32[128,512]{1,0:T(8,128)S(1)}, u32[]{:S(2)}, u32[]{:S(2)}) %collective-permute-start.9) | collective-permute-done | bytes 262176 | tf_op jit(solution)/shard_map/ppermute | solution.py:95
  16.8 3.1 %collective-permute-done.1 = f32[128,512]{1,0:T(8,128)S(1)} collective-permute-done((f32[128,512]{1,0:T(8,128)S(1)}, f32[128,512]{1,0:T(8,128)S(1)}, u32[]{:S(2)}, u32[]{:S(2)}) %collective-permute-start.1) | collective-permute-done | bytes 262176 | tf_op jit(solution)/shard_map/ppermute | solution.py:95
  19.9 1.7 %collective-permute-start.2 = (f32[64,512]{1,0:T(8,128)S(1)}, f32[64,512]{1,0:T(8,128)S(1)}, u32[]{:S(2)}, u32[]{:S(2)}) collective-permute-start(f32[64,512]{1,0:T(8,128)S(1)} %get-tuple-element.40), channel_id=1, source_target_pairs={{0,16},{1,17},{2,18},{3,19},{4,12},{5,13},{6,14},{7,15},{8,24},{9,... | collective-permute-start | bytes 393224 | tf_op jit(solution)/shard_map/ppermute | solution.py:95
  21.7 1.6 %collective-permute-start.19 = (f32[32,512]{1,0:T(8,128)S(1)}, f32[32,512]{1,0:T(8,128)S(1)}, u32[]{:S(2)}, u32[]{:S(2)}) collective-permute-start(f32[32,512]{1,0:T(8,128)S(1)} %get-tuple-element.42), channel_id=1, source_target_pairs={{0,1},{1,0},{2,3},{3,2},{4,5},{5,4},{6,7},{7,6},{8,9},{9,8},{10,11... | collective-permute-start | bytes 196616 | tf_op jit(solution)/shard_map/ppermute | solution.py:95
  25.0 1.7 %collective-permute-start.3 = (f32[32,512]{1,0:T(8,128)S(1)}, f32[32,512]{1,0:T(8,128)S(1)}, u32[]{:S(2)}, u32[]{:S(2)}) collective-permute-start(f32[32,512]{1,0:T(8,128)S(1)} %get-tuple-element.46), channel_id=1, source_target_pairs={{0,1},{1,0},{2,3},{3,2},{4,5},{5,4},{6,7},{7,6},{8,9},{9,8},{10,11... | collective-permute-start | bytes 196616 | tf_op jit(solution)/shard_map/ppermute | solution.py:95
  26.8 2.7 %collective-permute-start.20 = (f32[16,512]{1,0:T(8,128)S(1)}, f32[16,512]{1,0:T(8,128)S(1)}, u32[]{:S(2)}, u32[]{:S(2)}) collective-permute-start(f32[16,512]{1,0:T(8,128)S(1)} %slice_add_fusion.12), channel_id=1, source_target_pairs={{0,2},{1,3},{2,0},{3,1},{4,6},{5,7},{6,4},{7,5},{8,10},{9,11},{10,... | collective-permute-start | bytes 98312 | tf_op jit(solution)/shard_map/ppermute | solution.py:95
  32.6 1.8 %collective-permute-start.21 = (f32[16,512]{1,0:T(8,128)S(1)}, f32[16,512]{1,0:T(8,128)S(1)}, u32[]{:S(2)}, u32[]{:S(2)}) collective-permute-start(f32[16,512]{1,0:T(8,128)S(1)} %get-tuple-element.30), channel_id=1, source_target_pairs={{0,2},{1,3},{2,0},{3,1},{4,6},{5,7},{6,4},{7,5},{8,10},{9,11},{10,... | collective-permute-start | bytes 98312 | tf_op jit(solution)/shard_map/ppermute | solution.py:95
  34.4 2.4 %collective-permute-done.4 = f32[16,512]{1,0:T(8,128)S(1)} collective-permute-done((f32[16,512]{1,0:T(8,128)S(1)}, f32[16,512]{1,0:T(8,128)S(1)}, u32[]{:S(2)}, u32[]{:S(2)}) %collective-permute-start.4) | collective-permute-done | bytes 32800 | tf_op jit(solution)/shard_map/ppermute | solution.py:95
  37.7 2.1 %collective-permute-start.13 = (f32[16,512]{1,0:T(8,128)S(1)}, f32[16,512]{1,0:T(8,128)S(1)}, u32[]{:S(2)}, u32[]{:S(2)}) collective-permute-start(f32[16,512]{1,0:T(8,128)S(1)} %get-tuple-element.32), channel_id=1, source_target_pairs={{0,2},{1,3},{2,0},{3,1},{4,6},{5,7},{6,4},{7,5},{8,10},{9,11},{10,... | collective-permute-start | bytes 98312 | tf_op jit(solution)/shard_map/ppermute | solution.py:95
  40.0 1.7 %collective-permute-done.5 = f32[16,512]{1,0:T(8,128)S(1)} collective-permute-done((f32[16,512]{1,0:T(8,128)S(1)}, f32[16,512]{1,0:T(8,128)S(1)}, u32[]{:S(2)}, u32[]{:S(2)}) %collective-permute-start.5) | collective-permute-done | bytes 32800 | tf_op jit(solution)/shard_map/ppermute | solution.py:95
  44.2 1.8 %collective-permute-start.23 = (f32[64,512]{1,0:T(8,128)S(1)}, f32[64,512]{1,0:T(8,128)S(1)}, u32[]{:S(2)}, u32[]{:S(2)}) collective-permute-start(f32[64,512]{1,0:T(8,128)S(1)} %pad_maximum_fusion.6), channel_id=1, source_target_pairs={{0,16},{1,17},{2,18},{3,19},{4,12},{5,13},{6,14},{7,15},{8,24},{9,... | collective-permute-start | bytes 393224 | tf_op jit(solution)/shard_map/ppermute | solution.py:95
  48.2 2.4 %collective-permute-done.23 = f32[64,512]{1,0:T(8,128)S(1)} collective-permute-done((f32[64,512]{1,0:T(8,128)S(1)}, f32[64,512]{1,0:T(8,128)S(1)}, u32[]{:S(2)}, u32[]{:S(2)}) %collective-permute-start.23) | collective-permute-done | bytes 131104 | tf_op jit(solution)/shard_map/ppermute | solution.py:95
  60.0 2.8 %collective-permute-done.16 = f32[128,512]{1,0:T(8,128)S(1)} collective-permute-done((f32[128,512]{1,0:T(8,128)S(1)}, f32[128,512]{1,0:T(8,128)S(1)}, u32[]{:S(2)}, u32[]{:S(2)}) %collective-permute-start.16) | collective-permute-done | bytes 262176 | tf_op jit(solution)/shard_map/ppermute | solution.py:95
  66.3 1.8 %collective-permute-start.26 = (f32[160,128]{1,0:T(8,128)S(1)}, f32[160,128]{1,0:T(8,128)S(1)}, u32[]{:S(2)}, u32[]{:S(2)}) collective-permute-start(f32[160,128]{1,0:T(8,128)S(1)} %get-tuple-element.25), channel_id=1, source_target_pairs={{0,16},{1,17},{2,18},{3,19},{4,12},{5,13},{6,14},{7,15},{8,24},{9,... | collective-permute-start | bytes 245768 | tf_op jit(solution)/shard_map/ppermute | solution.py:95
  71.4 1.9 %collective-permute-done.27 = f32[160,128]{1,0:T(8,128)S(1)} collective-permute-done((f32[160,128]{1,0:T(8,128)S(1)}, f32[160,128]{1,0:T(8,128)S(1)}, u32[]{:S(2)}, u32[]{:S(2)}) %collective-permute-start.27) | collective-permute-done | bytes 81952 | tf_op jit(solution)/shard_map/ppermute | solution.py:95
  74.7 1.9 %collective-permute-start.31 = (f32[160,128]{1,0:T(8,128)S(1)}, f32[160,128]{1,0:T(8,128)S(1)}, u32[]{:S(2)}, u32[]{:S(2)}) collective-permute-start(f32[160,128]{1,0:T(8,128)S(1)} %add_add_fusion.1), channel_id=1, source_target_pairs={{0,3},{1,2},{2,1},{3,0},{4,7},{5,6},{6,5},{7,4},{8,11},{9,10},{10,... | collective-permute-start | bytes 245768 | tf_op jit(solution)/shard_map/ppermute | solution.py:95
  76.6 2.5 %collective-permute-start.29 = (f32[160,128]{1,0:T(8,128)S(1)}, f32[160,128]{1,0:T(8,128)S(1)}, u32[]{:S(2)}, u32[]{:S(2)}) collective-permute-start(f32[160,128]{1,0:T(8,128)S(1)} %add_add_fusion.1), channel_id=1, source_target_pairs={{0,2},{1,3},{2,0},{3,1},{4,6},{5,7},{6,4},{7,5},{8,10},{9,11},{10,... | collective-permute-start | bytes 245768 | tf_op jit(solution)/shard_map/ppermute | solution.py:95
  79.2 2.2 %collective-permute-done.31 = f32[160,128]{1,0:T(8,128)S(1)} collective-permute-done((f32[160,128]{1,0:T(8,128)S(1)}, f32[160,128]{1,0:T(8,128)S(1)}, u32[]{:S(2)}, u32[]{:S(2)}) %collective-permute-start.31) | collective-permute-done | bytes 81952 | tf_op jit(solution)/shard_map/ppermute | solution.py:95
  87.3 1.9 %collective-permute-done.34 = f32[160,128]{1,0:T(8,128)S(1)} collective-permute-done((f32[160,128]{1,0:T(8,128)S(1)}, f32[160,128]{1,0:T(8,128)S(1)}, u32[]{:S(2)}, u32[]{:S(2)}) %collective-permute-start.34) | collective-permute-done | bytes 81952 | tf_op jit(solution)/shard_map/ppermute | solution.py:95
  91.1 1.6 %collective-permute-done.35.other_ref = f32[640,128]{1,0:T(8,128)S(1)} collective-permute-done((f32[640,128]{1,0:T(8,128)S(1)}, f32[640,128]{1,0:T(8,128)S(1)}, u32[]{:S(2)}, u32[]{:S(2)}) %collective-permute-start.35) | collective-permute-done | bytes 327712 | tf_op jit(solution)/shard_map/ppermute | solution.py:95
  92.7 12.8 %shard_map.24 = f32[512,128]{1,0:T(8,128)} custom-call(f32[640,128]{1,0:T(8,128)S(1)} %pad_maximum_fusion.mine_ref, f32[640,128]{1,0:T(8,128)S(1)} %collective-permute-done.35.other_ref, f32[512,128]{1,0:T(8,128)S(1)} %get-tuple-element.28.p_ref), custom_call_target="tpu_custom_call" | custom-call | tf_op jit(solution)/shard_map/pallas_call | solution.py:294
  (95 shorter events, 43.8 us)
Async XLA Ops:
  3.8 7.4 %collective-permute-start.17 = (f32[128,512]{1,0:T(8,128)S(1)}, f32[128,512]{1,0:T(8,128)S(1)}, u32[]{:S(2)}, u32[]{:S(2)}) collective-permute-start(f32[128,512]{1,0:T(8,128)S(1)} %get-tuple-element.23), channel_id=1, source_target_pairs={{0,8},{1,9},{2,10},{3,11},{4,20},{5,21},{6,22},{7,23},{8,0},{9,1},... | collective-permute-start | bytes 786440 | tf_op jit(solution)/shard_map/ppermute | solution.py:95
  7.8 7.4 %collective-permute-start.9 = (f32[128,512]{1,0:T(8,128)S(1)}, f32[128,512]{1,0:T(8,128)S(1)}, u32[]{:S(2)}, u32[]{:S(2)}) collective-permute-start(f32[128,512]{1,0:T(8,128)S(1)} %get-tuple-element.21), channel_id=1, source_target_pairs={{0,8},{1,9},{2,10},{3,11},{4,20},{5,21},{6,22},{7,23},{8,0},{9,1},... | collective-permute-start | bytes 786440 | tf_op jit(solution)/shard_map/ppermute | solution.py:95
  9.1 10.8 %collective-permute-start.1 = (f32[128,512]{1,0:T(8,128)S(1)}, f32[128,512]{1,0:T(8,128)S(1)}, u32[]{:S(2)}, u32[]{:S(2)}) collective-permute-start(f32[128,512]{1,0:T(8,128)S(1)} %get-tuple-element.19), channel_id=1, source_target_pairs={{0,8},{1,9},{2,10},{3,11},{4,20},{5,21},{6,22},{7,23},{8,0},{9,1},... | collective-permute-start | bytes 786440 | tf_op jit(solution)/shard_map/ppermute | solution.py:95
  11.2 10.4 %collective-permute-start.18 = (f32[64,512]{1,0:T(8,128)S(1)}, f32[64,512]{1,0:T(8,128)S(1)}, u32[]{:S(2)}, u32[]{:S(2)}) collective-permute-start(f32[64,512]{1,0:T(8,128)S(1)} %get-tuple-element.36), channel_id=1, source_target_pairs={{0,16},{1,17},{2,18},{3,19},{4,12},{5,13},{6,14},{7,15},{8,24},{9,... | collective-permute-start | bytes 393224 | tf_op jit(solution)/shard_map/ppermute | solution.py:95
  15.3 8.0 %collective-permute-start.10 = (f32[64,512]{1,0:T(8,128)S(1)}, f32[64,512]{1,0:T(8,128)S(1)}, u32[]{:S(2)}, u32[]{:S(2)}) collective-permute-start(f32[64,512]{1,0:T(8,128)S(1)} %get-tuple-element.38), channel_id=1, source_target_pairs={{0,16},{1,17},{2,18},{3,19},{4,12},{5,13},{6,14},{7,15},{8,24},{9,... | collective-permute-start | bytes 393224 | tf_op jit(solution)/shard_map/ppermute | solution.py:95
  21.7 5.1 %collective-permute-start.19 = (f32[32,512]{1,0:T(8,128)S(1)}, f32[32,512]{1,0:T(8,128)S(1)}, u32[]{:S(2)}, u32[]{:S(2)}) collective-permute-start(f32[32,512]{1,0:T(8,128)S(1)} %get-tuple-element.42), channel_id=1, source_target_pairs={{0,1},{1,0},{2,3},{3,2},{4,5},{5,4},{6,7},{7,6},{8,9},{9,8},{10,11... | collective-permute-start | bytes 196616 | tf_op jit(solution)/shard_map/ppermute | solution.py:95
  23.3 6.1 %collective-permute-start.11 = (f32[32,512]{1,0:T(8,128)S(1)}, f32[32,512]{1,0:T(8,128)S(1)}, u32[]{:S(2)}, u32[]{:S(2)}) collective-permute-start(f32[32,512]{1,0:T(8,128)S(1)} %get-tuple-element.44), channel_id=1, source_target_pairs={{0,1},{1,0},{2,3},{3,2},{4,5},{5,4},{6,7},{7,6},{8,9},{9,8},{10,11... | collective-permute-start | bytes 196616 | tf_op jit(solution)/shard_map/ppermute | solution.py:95
  25.0 5.9 %collective-permute-start.3 = (f32[32,512]{1,0:T(8,128)S(1)}, f32[32,512]{1,0:T(8,128)S(1)}, u32[]{:S(2)}, u32[]{:S(2)}) collective-permute-start(f32[32,512]{1,0:T(8,128)S(1)} %get-tuple-element.46), channel_id=1, source_target_pairs={{0,1},{1,0},{2,3},{3,2},{4,5},{5,4},{6,7},{7,6},{8,9},{9,8},{10,11... | collective-permute-start | bytes 196616 | tf_op jit(solution)/shard_map/ppermute | solution.py:95
  26.8 5.8 %collective-permute-start.20 = (f32[16,512]{1,0:T(8,128)S(1)}, f32[16,512]{1,0:T(8,128)S(1)}, u32[]{:S(2)}, u32[]{:S(2)}) collective-permute-start(f32[16,512]{1,0:T(8,128)S(1)} %slice_add_fusion.12), channel_id=1, source_target_pairs={{0,2},{1,3},{2,0},{3,1},{4,6},{5,7},{6,4},{7,5},{8,10},{9,11},{10,... | collective-permute-start | bytes 98312 | tf_op jit(solution)/shard_map/ppermute | solution.py:95
  29.4 8.3 %collective-permute-start.12 = (f32[16,512]{1,0:T(8,128)S(1)}, f32[16,512]{1,0:T(8,128)S(1)}, u32[]{:S(2)}, u32[]{:S(2)}) collective-permute-start(f32[16,512]{1,0:T(8,128)S(1)} %slice_add_fusion.14), channel_id=1, source_target_pairs={{0,2},{1,3},{2,0},{3,1},{4,6},{5,7},{6,4},{7,5},{8,10},{9,11},{10,... | collective-permute-start | bytes 98312 | tf_op jit(solution)/shard_map/ppermute | solution.py:95
  30.9 5.8 %collective-permute-start.4 = (f32[16,512]{1,0:T(8,128)S(1)}, f32[16,512]{1,0:T(8,128)S(1)}, u32[]{:S(2)}, u32[]{:S(2)}) collective-permute-start(f32[16,512]{1,0:T(8,128)S(1)} %slice_add_fusion.16), channel_id=1, source_target_pairs={{0,2},{1,3},{2,0},{3,1},{4,6},{5,7},{6,4},{7,5},{8,10},{9,11},{10,... | collective-permute-start | bytes 98312 | tf_op jit(solution)/shard_map/ppermute | solution.py:95
  32.6 7.3 %collective-permute-start.21 = (f32[16,512]{1,0:T(8,128)S(1)}, f32[16,512]{1,0:T(8,128)S(1)}, u32[]{:S(2)}, u32[]{:S(2)}) collective-permute-start(f32[16,512]{1,0:T(8,128)S(1)} %get-tuple-element.30), channel_id=1, source_target_pairs={{0,2},{1,3},{2,0},{3,1},{4,6},{5,7},{6,4},{7,5},{8,10},{9,11},{10,... | collective-permute-start | bytes 98312 | tf_op jit(solution)/shard_map/ppermute | solution.py:95
  44.2 6.4 %collective-permute-start.23 = (f32[64,512]{1,0:T(8,128)S(1)}, f32[64,512]{1,0:T(8,128)S(1)}, u32[]{:S(2)}, u32[]{:S(2)}) collective-permute-start(f32[64,512]{1,0:T(8,128)S(1)} %pad_maximum_fusion.6), channel_id=1, source_target_pairs={{0,16},{1,17},{2,18},{3,19},{4,12},{5,13},{6,14},{7,15},{8,24},{9,... | collective-permute-start | bytes 393224 | tf_op jit(solution)/shard_map/ppermute | solution.py:95
  46.0 7.5 %collective-permute-start.7 = (f32[64,512]{1,0:T(8,128)S(1)}, f32[64,512]{1,0:T(8,128)S(1)}, u32[]{:S(2)}, u32[]{:S(2)}) collective-permute-start(f32[64,512]{1,0:T(8,128)S(1)} %pad_maximum_fusion.4), channel_id=1, source_target_pairs={{0,16},{1,17},{2,18},{3,19},{4,12},{5,13},{6,14},{7,15},{8,24},{9,... | collective-permute-start | bytes 393224 | tf_op jit(solution)/shard_map/ppermute | solution.py:95
  46.9 9.3 %collective-permute-start.15 = (f32[64,512]{1,0:T(8,128)S(1)}, f32[64,512]{1,0:T(8,128)S(1)}, u32[]{:S(2)}, u32[]{:S(2)}) collective-permute-start(f32[64,512]{1,0:T(8,128)S(1)} %pad_maximum_fusion.5), channel_id=1, source_target_pairs={{0,16},{1,17},{2,18},{3,19},{4,12},{5,13},{6,14},{7,15},{8,24},{9,... | collective-permute-start | bytes 393224 | tf_op jit(solution)/shard_map/ppermute | solution.py:95
  50.7 7.2 %collective-permute-start.24 = (f32[128,512]{1,0:T(8,128)S(1)}, f32[128,512]{1,0:T(8,128)S(1)}, u32[]{:S(2)}, u32[]{:S(2)}) collective-permute-start(f32[128,512]{1,0:T(8,128)S(1)} %pad_maximum_fusion.3), channel_id=1, source_target_pairs={{0,8},{1,9},{2,10},{3,11},{4,20},{5,21},{6,22},{7,23},{8,0},{9,1},... | collective-permute-start | bytes 786440 | tf_op jit(solution)/shard_map/ppermute | solution.py:95
  53.5 6.4 %collective-permute-start.8 = (f32[128,512]{1,0:T(8,128)S(1)}, f32[128,512]{1,0:T(8,128)S(1)}, u32[]{:S(2)}, u32[]{:S(2)}) collective-permute-start(f32[128,512]{1,0:T(8,128)S(1)} %pad_maximum_fusion.1), channel_id=1, source_target_pairs={{0,8},{1,9},{2,10},{3,11},{4,20},{5,21},{6,22},{7,23},{8,0},{9,1},... | collective-permute-start | bytes 786440 | tf_op jit(solution)/shard_map/ppermute | solution.py:95
  56.2 6.5 %collective-permute-start.16 = (f32[128,512]{1,0:T(8,128)S(1)}, f32[128,512]{1,0:T(8,128)S(1)}, u32[]{:S(2)}, u32[]{:S(2)}) collective-permute-start(f32[128,512]{1,0:T(8,128)S(1)} %pad_maximum_fusion.2), channel_id=1, source_target_pairs={{0,8},{1,9},{2,10},{3,11},{4,20},{5,21},{6,22},{7,23},{8,0},{9,1},... | collective-permute-start | bytes 786440 | tf_op jit(solution)/shard_map/ppermute | solution.py:95
  68.1 5.2 %collective-permute-start.27 = (f32[160,128]{1,0:T(8,128)S(1)}, f32[160,128]{1,0:T(8,128)S(1)}, u32[]{:S(2)}, u32[]{:S(2)}) collective-permute-start(f32[160,128]{1,0:T(8,128)S(1)} %get-tuple-element.26), channel_id=1, source_target_pairs={{0,8},{1,9},{2,10},{3,11},{4,20},{5,21},{6,22},{7,23},{8,0},{9,1},... | collective-permute-start | bytes 245768 | tf_op jit(solution)/shard_map/ppermute | solution.py:95
  69.4 5.3 %collective-permute-start.28 = (f32[160,128]{1,0:T(8,128)S(1)}, f32[160,128]{1,0:T(8,128)S(1)}, u32[]{:S(2)}, u32[]{:S(2)}) collective-permute-start(f32[160,128]{1,0:T(8,128)S(1)} %get-tuple-element.27), channel_id=1, source_target_pairs={{0,24},{1,25},{2,26},{3,27},{4,28},{5,29},{6,30},{7,31},{8,16},{9,... | collective-permute-start | bytes 245768 | tf_op jit(solution)/shard_map/ppermute | solution.py:95
  74.7 6.7 %collective-permute-start.31 = (f32[160,128]{1,0:T(8,128)S(1)}, f32[160,128]{1,0:T(8,128)S(1)}, u32[]{:S(2)}, u32[]{:S(2)}) collective-permute-start(f32[160,128]{1,0:T(8,128)S(1)} %add_add_fusion.1), channel_id=1, source_target_pairs={{0,3},{1,2},{2,1},{3,0},{4,7},{5,6},{6,5},{7,4},{8,11},{9,10},{10,... | collective-permute-start | bytes 245768 | tf_op jit(solution)/shard_map/ppermute | solution.py:95
  76.6 6.3 %collective-permute-start.30 = (f32[160,128]{1,0:T(8,128)S(1)}, f32[160,128]{1,0:T(8,128)S(1)}, u32[]{:S(2)}, u32[]{:S(2)}) collective-permute-start(f32[160,128]{1,0:T(8,128)S(1)} %add_add_fusion.1), channel_id=1, source_target_pairs={{0,1},{1,0},{2,3},{3,2},{4,5},{5,4},{6,7},{7,6},{8,9},{9,8},{10,11... | collective-permute-start | bytes 245768 | tf_op jit(solution)/shard_map/ppermute | solution.py:95
  76.6 7.1 %collective-permute-start.29 = (f32[160,128]{1,0:T(8,128)S(1)}, f32[160,128]{1,0:T(8,128)S(1)}, u32[]{:S(2)}, u32[]{:S(2)}) collective-permute-start(f32[160,128]{1,0:T(8,128)S(1)} %add_add_fusion.1), channel_id=1, source_target_pairs={{0,2},{1,3},{2,0},{3,1},{4,6},{5,7},{6,4},{7,5},{8,10},{9,11},{10,... | collective-permute-start | bytes 245768 | tf_op jit(solution)/shard_map/ppermute | solution.py:95
  83.8 5.4 %collective-permute-start.34 = (f32[160,128]{1,0:T(8,128)S(1)}, f32[160,128]{1,0:T(8,128)S(1)}, u32[]{:S(2)}, u32[]{:S(2)}) collective-permute-start(f32[160,128]{1,0:T(8,128)S(1)} %add_add_fusion), channel_id=1, source_target_pairs={{0,24},{1,25},{2,26},{3,27},{4,28},{5,29},{6,30},{7,31},{8,16},{9,... | collective-permute-start | bytes 245768 | tf_op jit(solution)/shard_map/ppermute | solution.py:95
  (13 other events, 49.1 us)

commit v8 on v7

--- a/solution.py
+++ b/solution.py
@@ -241,14 +241,16 @@
                     cols[k] = {i: jnp.broadcast_to(r[i][0][:, at : at + 1], (8, tile)) for i in range(k // 8, per_panel)}
             jb, js = j // 8, j % 8
             col = cols[j]
-            pivot = jnp.broadcast_to(col[jb][js : js + 1, :], (8, tile))
+            pivot = jnp.broadcast_to(col[jb][js : js + 1, :], (8, tile)) if j == 0 else following
             scale[jb] = jnp.where(sub == js, lax.rsqrt(pivot), scale[jb])
             inverse = 1.0 / pivot
-            mult = {i: col[i] * inverse for i in range(jb, per_panel)}
-            mult[jb] = jnp.where(sub > js, mult[jb], 0.0)
+            below = {i: col[i] if i > jb else jnp.where(sub > js, col[i], 0.0) for i in range(jb, per_panel)}
+            mult = {i: below[i] * inverse for i in range(jb, per_panel)}
             first = jb if js < 7 else jb + 1
             for k in range(j + 1, len(cols)):
                 row = jnp.broadcast_to(col[k // 8][k % 8 : k % 8 + 1, :], (8, tile))
+                if k == j + 1:
+                    following = jnp.broadcast_to(cols[k][k // 8][k % 8 : k % 8 + 1, :], (8, tile)) - row * row * inverse
                 for i in range(k // 8, per_panel):
                     cols[k][i] = cols[k][i] - mult[i] * row
             for c in range(groups - b):
@@ -290,9 +292,11 @@
     return jax.ShapeDtypeStruct(shape, jnp.float32)
 
 
-def call(kernel, out_shape, scratch, args):
+def call(kernel, out_shape, scratch, args, flops=0):
+    moved = sum(x.size * x.dtype.itemsize for x in list(args) + jax.tree.leaves(out_shape))
     return pl.pallas_call(
         kernel,
+        cost_estimate=pl.CostEstimate(flops=flops, bytes_accessed=moved, transcendentals=0),
         out_shape=out_shape,
         in_specs=[VMEM] * len(args),
         out_specs=jax.tree.map(lambda _: VMEM, out_shape),
@@ -322,23 +326,25 @@
         out_specs=VMEM,
         compiler_params=pltpu.CompilerParams(vmem_limit_bytes=VMEM_LIMIT),
     )(history)
+    flops = 6 * 2 * half * norb * 2 * width
     out = [f32(half // 2, norb)] * 2
     keep, send, left = call(
         functools.partial(first_project_kernel, route, scatter),
         out + [jax.ShapeDtypeStruct((half, 12 * width), jnp.bfloat16)],
         [f32(half, 2 * width)],
         [own, peer],
+        flops=flops,
     )
     products = [(keep, send)]
     for j in range(1, terms):
-        products.append(call(functools.partial(project_kernel, j), out, [], [left, own, peer]))
+        products.append(call(functools.partial(project_kernel, j), out, [], [left, own, peer], flops))
     m = [all_reduce(route, keep, send, scatter, levels) for keep, send in products]
     out, mine = f32(half, 2 * width), []
     for j in range(terms - 1):
         kernel = functools.partial(predict_kernel, j, WEIGHTS[j] / total)
-        mine = [call(kernel, out, [], [m[j], own, peer] + mine)]
+        mine = [call(kernel, out, [], [m[j], own, peer] + mine, flops)]
     kernel = functools.partial(last_predict_kernel, terms - 1, WEIGHTS[terms - 1] / total, route, scatter)
-    mine = call(kernel, out, [out], [m[-1], own, peer] + mine)
+    mine = call(kernel, out, [out], [m[-1], own, peer] + mine, flops)
     other = swap(mine, route.core_perm())
 
     shares = (norb // TILE) * (norb // TILE + 1) // 2

time: 106 us -> 105 us (level)
  no operation moved by 1% of the time
where the time goes in v8:
time: 105 us
  starting transfers between devices  46.9 us (45%)
  waiting for transfers between devices  37.9 us (36%)
  Pallas kernels  18.3 us (17%)
  local copies, waits for them, and re-layouts  1.25 us (1%)
    ppermute x36, starting transfers between devices, swap(): return lax.ppermute(x, AXES, perm)  46.9 us
    ppermute x36, waiting for transfers between devices, swap(): return lax.ppermute(x, AXES, perm)  37.9 us
    pallas_call x8, Pallas kernels, call(): pl.pallas_call(kernel, cost_estimate=pl.CostEstimate(flops=flops, bytes_a...  18.3 us
  transfers between devices with their start and end apart: 36, of which 26 were waited for; matrix products, arithmetic and copies ran while one was open for 0% of the time, Pallas kernels for 3%

profile of v8, /device:TPU:0, one launch (start us, length us, event | category | flops | bytes accessed | tf_op | source)
XLA Modules:
  0.0 105.0 jit_solution(9332269524299278708)
XLA Ops:
  3.8 2.9 %collective-permute-start.17 = (f32[128,512]{1,0:T(8,128)S(1)}, f32[128,512]{1,0:T(8,128)S(1)}, u32[]{:S(2)}, u32[]{:S(2)}) collective-permute-start(f32[128,512]{1,0:T(8,128)S(1)} %get-tuple-element.23), channel_id=1, source_target_pairs={{0,8},{1,9},{2,10},{3,11},{4,20},{5,21},{6,22},{7,23},{8,0},{9,1},... | collective-permute-start | bytes 786440 | tf_op jit(solution)/shard_map/ppermute | solution.py:95
  9.1 2.1 %collective-permute-start.1 = (f32[128,512]{1,0:T(8,128)S(1)}, f32[128,512]{1,0:T(8,128)S(1)}, u32[]{:S(2)}, u32[]{:S(2)}) collective-permute-start(f32[128,512]{1,0:T(8,128)S(1)} %get-tuple-element.19), channel_id=1, source_target_pairs={{0,8},{1,9},{2,10},{3,11},{4,20},{5,21},{6,22},{7,23},{8,0},{9,1},... | collective-permute-start | bytes 786440 | tf_op jit(solution)/shard_map/ppermute | solution.py:95
  11.2 2.0 %collective-permute-start.18 = (f32[64,512]{1,0:T(8,128)S(1)}, f32[64,512]{1,0:T(8,128)S(1)}, u32[]{:S(2)}, u32[]{:S(2)}) collective-permute-start(f32[64,512]{1,0:T(8,128)S(1)} %get-tuple-element.36), channel_id=1, source_target_pairs={{0,16},{1,17},{2,18},{3,19},{4,12},{5,13},{6,14},{7,15},{8,24},{9,... | collective-permute-start | bytes 393224 | tf_op jit(solution)/shard_map/ppermute | solution.py:95
  13.2 2.0 %collective-permute-done.9 = f32[128,512]{1,0:T(8,128)S(1)} collective-permute-done((f32[128,512]{1,0:T(8,128)S(1)}, f32[128,512]{1,0:T(8,128)S(1)}, u32[]{:S(2)}, u32[]{:S(2)}) %collective-permute-start.9) | collective-permute-done | bytes 262176 | tf_op jit(solution)/shard_map/ppermute | solution.py:95
  16.8 3.1 %collective-permute-done.1 = f32[128,512]{1,0:T(8,128)S(1)} collective-permute-done((f32[128,512]{1,0:T(8,128)S(1)}, f32[128,512]{1,0:T(8,128)S(1)}, u32[]{:S(2)}, u32[]{:S(2)}) %collective-permute-start.1) | collective-permute-done | bytes 262176 | tf_op jit(solution)/shard_map/ppermute | solution.py:95
  19.9 1.7 %collective-permute-start.2 = (f32[64,512]{1,0:T(8,128)S(1)}, f32[64,512]{1,0:T(8,128)S(1)}, u32[]{:S(2)}, u32[]{:S(2)}) collective-permute-start(f32[64,512]{1,0:T(8,128)S(1)} %get-tuple-element.40), channel_id=1, source_target_pairs={{0,16},{1,17},{2,18},{3,19},{4,12},{5,13},{6,14},{7,15},{8,24},{9,... | collective-permute-start | bytes 393224 | tf_op jit(solution)/shard_map/ppermute | solution.py:95
  21.7 1.6 %collective-permute-start.19 = (f32[32,512]{1,0:T(8,128)S(1)}, f32[32,512]{1,0:T(8,128)S(1)}, u32[]{:S(2)}, u32[]{:S(2)}) collective-permute-start(f32[32,512]{1,0:T(8,128)S(1)} %get-tuple-element.42), channel_id=1, source_target_pairs={{0,1},{1,0},{2,3},{3,2},{4,5},{5,4},{6,7},{7,6},{8,9},{9,8},{10,11... | collective-permute-start | bytes 196616 | tf_op jit(solution)/shard_map/ppermute | solution.py:95
  25.0 1.7 %collective-permute-start.3 = (f32[32,512]{1,0:T(8,128)S(1)}, f32[32,512]{1,0:T(8,128)S(1)}, u32[]{:S(2)}, u32[]{:S(2)}) collective-permute-start(f32[32,512]{1,0:T(8,128)S(1)} %get-tuple-element.46), channel_id=1, source_target_pairs={{0,1},{1,0},{2,3},{3,2},{4,5},{5,4},{6,7},{7,6},{8,9},{9,8},{10,11... | collective-permute-start | bytes 196616 | tf_op jit(solution)/shard_map/ppermute | solution.py:95
  26.8 2.7 %collective-permute-start.20 = (f32[16,512]{1,0:T(8,128)S(1)}, f32[16,512]{1,0:T(8,128)S(1)}, u32[]{:S(2)}, u32[]{:S(2)}) collective-permute-start(f32[16,512]{1,0:T(8,128)S(1)} %slice_add_fusion.12), channel_id=1, source_target_pairs={{0,2},{1,3},{2,0},{3,1},{4,6},{5,7},{6,4},{7,5},{8,10},{9,11},{10,... | collective-permute-start | bytes 98312 | tf_op jit(solution)/shard_map/ppermute | solution.py:95
  32.6 1.8 %collective-permute-start.21 = (f32[16,512]{1,0:T(8,128)S(1)}, f32[16,512]{1,0:T(8,128)S(1)}, u32[]{:S(2)}, u32[]{:S(2)}) collective-permute-start(f32[16,512]{1,0:T(8,128)S(1)} %get-tuple-element.30), channel_id=1, source_target_pairs={{0,2},{1,3},{2,0},{3,1},{4,6},{5,7},{6,4},{7,5},{8,10},{9,11},{10,... | collective-permute-start | bytes 98312 | tf_op jit(solution)/shard_map/ppermute | solution.py:95
  34.4 2.4 %collective-permute-done.4 = f32[16,512]{1,0:T(8,128)S(1)} collective-permute-done((f32[16,512]{1,0:T(8,128)S(1)}, f32[16,512]{1,0:T(8,128)S(1)}, u32[]{:S(2)}, u32[]{:S(2)}) %collective-permute-start.4) | collective-permute-done | bytes 32800 | tf_op jit(solution)/shard_map/ppermute | solution.py:95
  37.7 2.1 %collective-permute-start.13 = (f32[16,512]{1,0:T(8,128)S(1)}, f32[16,512]{1,0:T(8,128)S(1)}, u32[]{:S(2)}, u32[]{:S(2)}) collective-permute-start(f32[16,512]{1,0:T(8,128)S(1)} %get-tuple-element.32), channel_id=1, source_target_pairs={{0,2},{1,3},{2,0},{3,1},{4,6},{5,7},{6,4},{7,5},{8,10},{9,11},{10,... | collective-permute-start | bytes 98312 | tf_op jit(solution)/shard_map/ppermute | solution.py:95
  40.0 1.7 %collective-permute-done.5 = f32[16,512]{1,0:T(8,128)S(1)} collective-permute-done((f32[16,512]{1,0:T(8,128)S(1)}, f32[16,512]{1,0:T(8,128)S(1)}, u32[]{:S(2)}, u32[]{:S(2)}) %collective-permute-start.5) | collective-permute-done | bytes 32800 | tf_op jit(solution)/shard_map/ppermute | solution.py:95
  44.2 1.8 %collective-permute-start.23 = (f32[64,512]{1,0:T(8,128)S(1)}, f32[64,512]{1,0:T(8,128)S(1)}, u32[]{:S(2)}, u32[]{:S(2)}) collective-permute-start(f32[64,512]{1,0:T(8,128)S(1)} %pad_maximum_fusion.6), channel_id=1, source_target_pairs={{0,16},{1,17},{2,18},{3,19},{4,12},{5,13},{6,14},{7,15},{8,24},{9,... | collective-permute-start | bytes 393224 | tf_op jit(solution)/shard_map/ppermute | solution.py:95
  48.2 2.4 %collective-permute-done.23 = f32[64,512]{1,0:T(8,128)S(1)} collective-permute-done((f32[64,512]{1,0:T(8,128)S(1)}, f32[64,512]{1,0:T(8,128)S(1)}, u32[]{:S(2)}, u32[]{:S(2)}) %collective-permute-start.23) | collective-permute-done | bytes 131104 | tf_op jit(solution)/shard_map/ppermute | solution.py:95
  60.0 2.8 %collective-permute-done.16 = f32[128,512]{1,0:T(8,128)S(1)} collective-permute-done((f32[128,512]{1,0:T(8,128)S(1)}, f32[128,512]{1,0:T(8,128)S(1)}, u32[]{:S(2)}, u32[]{:S(2)}) %collective-permute-start.16) | collective-permute-done | bytes 262176 | tf_op jit(solution)/shard_map/ppermute | solution.py:95
  66.3 1.8 %collective-permute-start.26 = (f32[160,128]{1,0:T(8,128)S(1)}, f32[160,128]{1,0:T(8,128)S(1)}, u32[]{:S(2)}, u32[]{:S(2)}) collective-permute-start(f32[160,128]{1,0:T(8,128)S(1)} %get-tuple-element.25), channel_id=1, source_target_pairs={{0,16},{1,17},{2,18},{3,19},{4,12},{5,13},{6,14},{7,15},{8,24},{9,... | collective-permute-start | bytes 245768 | tf_op jit(solution)/shard_map/ppermute | solution.py:95
  71.4 1.9 %collective-permute-done.27 = f32[160,128]{1,0:T(8,128)S(1)} collective-permute-done((f32[160,128]{1,0:T(8,128)S(1)}, f32[160,128]{1,0:T(8,128)S(1)}, u32[]{:S(2)}, u32[]{:S(2)}) %collective-permute-start.27) | collective-permute-done | bytes 81952 | tf_op jit(solution)/shard_map/ppermute | solution.py:95
  74.7 1.9 %collective-permute-start.31 = (f32[160,128]{1,0:T(8,128)S(1)}, f32[160,128]{1,0:T(8,128)S(1)}, u32[]{:S(2)}, u32[]{:S(2)}) collective-permute-start(f32[160,128]{1,0:T(8,128)S(1)} %add_add_fusion.1), channel_id=1, source_target_pairs={{0,3},{1,2},{2,1},{3,0},{4,7},{5,6},{6,5},{7,4},{8,11},{9,10},{10,... | collective-permute-start | bytes 245768 | tf_op jit(solution)/shard_map/ppermute | solution.py:95
  76.6 2.5 %collective-permute-start.29 = (f32[160,128]{1,0:T(8,128)S(1)}, f32[160,128]{1,0:T(8,128)S(1)}, u32[]{:S(2)}, u32[]{:S(2)}) collective-permute-start(f32[160,128]{1,0:T(8,128)S(1)} %add_add_fusion.1), channel_id=1, source_target_pairs={{0,2},{1,3},{2,0},{3,1},{4,6},{5,7},{6,4},{7,5},{8,10},{9,11},{10,... | collective-permute-start | bytes 245768 | tf_op jit(solution)/shard_map/ppermute | solution.py:95
  79.2 2.2 %collective-permute-done.31 = f32[160,128]{1,0:T(8,128)S(1)} collective-permute-done((f32[160,128]{1,0:T(8,128)S(1)}, f32[160,128]{1,0:T(8,128)S(1)}, u32[]{:S(2)}, u32[]{:S(2)}) %collective-permute-start.31) | collective-permute-done | bytes 81952 | tf_op jit(solution)/shard_map/ppermute | solution.py:95
  87.3 1.9 %collective-permute-done.34 = f32[160,128]{1,0:T(8,128)S(1)} collective-permute-done((f32[160,128]{1,0:T(8,128)S(1)}, f32[160,128]{1,0:T(8,128)S(1)}, u32[]{:S(2)}, u32[]{:S(2)}) %collective-permute-start.34) | collective-permute-done | bytes 81952 | tf_op jit(solution)/shard_map/ppermute | solution.py:95
  91.1 1.6 %collective-permute-done.35.other_ref = f32[640,128]{1,0:T(8,128)S(1)} collective-permute-done((f32[640,128]{1,0:T(8,128)S(1)}, f32[640,128]{1,0:T(8,128)S(1)}, u32[]{:S(2)}, u32[]{:S(2)}) %collective-permute-start.35) | collective-permute-done | bytes 327712 | tf_op jit(solution)/shard_map/ppermute | solution.py:95
  92.7 12.3 %shard_map.24 = f32[512,128]{1,0:T(8,128)} custom-call(f32[640,128]{1,0:T(8,128)S(1)} %pad_maximum_fusion.mine_ref, f32[640,128]{1,0:T(8,128)S(1)} %collective-permute-done.35.other_ref, f32[512,128]{1,0:T(8,128)S(1)} %get-tuple-element.28.p_ref), custom_call_target="tpu_custom_call" | custom-call | bytes 1179648 | tf_op jit(solution)/shard_map/pallas_call | solution.py:297
  (95 shorter events, 43.8 us)
Async XLA Ops:
  3.8 7.4 %collective-permute-start.17 = (f32[128,512]{1,0:T(8,128)S(1)}, f32[128,512]{1,0:T(8,128)S(1)}, u32[]{:S(2)}, u32[]{:S(2)}) collective-permute-start(f32[128,512]{1,0:T(8,128)S(1)} %get-tuple-element.23), channel_id=1, source_target_pairs={{0,8},{1,9},{2,10},{3,11},{4,20},{5,21},{6,22},{7,23},{8,0},{9,1},... | collective-permute-start | bytes 786440 | tf_op jit(solution)/shard_map/ppermute | solution.py:95
  7.8 7.4 %collective-permute-start.9 = (f32[128,512]{1,0:T(8,128)S(1)}, f32[128,512]{1,0:T(8,128)S(1)}, u32[]{:S(2)}, u32[]{:S(2)}) collective-permute-start(f32[128,512]{1,0:T(8,128)S(1)} %get-tuple-element.21), channel_id=1, source_target_pairs={{0,8},{1,9},{2,10},{3,11},{4,20},{5,21},{6,22},{7,23},{8,0},{9,1},... | collective-permute-start | bytes 786440 | tf_op jit(solution)/shard_map/ppermute | solution.py:95
  9.1 10.8 %collective-permute-start.1 = (f32[128,512]{1,0:T(8,128)S(1)}, f32[128,512]{1,0:T(8,128)S(1)}, u32[]{:S(2)}, u32[]{:S(2)}) collective-permute-start(f32[128,512]{1,0:T(8,128)S(1)} %get-tuple-element.19), channel_id=1, source_target_pairs={{0,8},{1,9},{2,10},{3,11},{4,20},{5,21},{6,22},{7,23},{8,0},{9,1},... | collective-permute-start | bytes 786440 | tf_op jit(solution)/shard_map/ppermute | solution.py:95
  11.2 10.4 %collective-permute-start.18 = (f32[64,512]{1,0:T(8,128)S(1)}, f32[64,512]{1,0:T(8,128)S(1)}, u32[]{:S(2)}, u32[]{:S(2)}) collective-permute-start(f32[64,512]{1,0:T(8,128)S(1)} %get-tuple-element.36), channel_id=1, source_target_pairs={{0,16},{1,17},{2,18},{3,19},{4,12},{5,13},{6,14},{7,15},{8,24},{9,... | collective-permute-start | bytes 393224 | tf_op jit(solution)/shard_map/ppermute | solution.py:95
  15.3 8.0 %collective-permute-start.10 = (f32[64,512]{1,0:T(8,128)S(1)}, f32[64,512]{1,0:T(8,128)S(1)}, u32[]{:S(2)}, u32[]{:S(2)}) collective-permute-start(f32[64,512]{1,0:T(8,128)S(1)} %get-tuple-element.38), channel_id=1, source_target_pairs={{0,16},{1,17},{2,18},{3,19},{4,12},{5,13},{6,14},{7,15},{8,24},{9,... | collective-permute-start | bytes 393224 | tf_op jit(solution)/shard_map/ppermute | solution.py:95
  21.7 5.1 %collective-permute-start.19 = (f32[32,512]{1,0:T(8,128)S(1)}, f32[32,512]{1,0:T(8,128)S(1)}, u32[]{:S(2)}, u32[]{:S(2)}) collective-permute-start(f32[32,512]{1,0:T(8,128)S(1)} %get-tuple-element.42), channel_id=1, source_target_pairs={{0,1},{1,0},{2,3},{3,2},{4,5},{5,4},{6,7},{7,6},{8,9},{9,8},{10,11... | collective-permute-start | bytes 196616 | tf_op jit(solution)/shard_map/ppermute | solution.py:95
  23.3 6.1 %collective-permute-start.11 = (f32[32,512]{1,0:T(8,128)S(1)}, f32[32,512]{1,0:T(8,128)S(1)}, u32[]{:S(2)}, u32[]{:S(2)}) collective-permute-start(f32[32,512]{1,0:T(8,128)S(1)} %get-tuple-element.44), channel_id=1, source_target_pairs={{0,1},{1,0},{2,3},{3,2},{4,5},{5,4},{6,7},{7,6},{8,9},{9,8},{10,11... | collective-permute-start | bytes 196616 | tf_op jit(solution)/shard_map/ppermute | solution.py:95
  25.0 5.9 %collective-permute-start.3 = (f32[32,512]{1,0:T(8,128)S(1)}, f32[32,512]{1,0:T(8,128)S(1)}, u32[]{:S(2)}, u32[]{:S(2)}) collective-permute-start(f32[32,512]{1,0:T(8,128)S(1)} %get-tuple-element.46), channel_id=1, source_target_pairs={{0,1},{1,0},{2,3},{3,2},{4,5},{5,4},{6,7},{7,6},{8,9},{9,8},{10,11... | collective-permute-start | bytes 196616 | tf_op jit(solution)/shard_map/ppermute | solution.py:95
  26.8 5.8 %collective-permute-start.20 = (f32[16,512]{1,0:T(8,128)S(1)}, f32[16,512]{1,0:T(8,128)S(1)}, u32[]{:S(2)}, u32[]{:S(2)}) collective-permute-start(f32[16,512]{1,0:T(8,128)S(1)} %slice_add_fusion.12), channel_id=1, source_target_pairs={{0,2},{1,3},{2,0},{3,1},{4,6},{5,7},{6,4},{7,5},{8,10},{9,11},{10,... | collective-permute-start | bytes 98312 | tf_op jit(solution)/shard_map/ppermute | solution.py:95
  29.4 8.3 %collective-permute-start.12 = (f32[16,512]{1,0:T(8,128)S(1)}, f32[16,512]{1,0:T(8,128)S(1)}, u32[]{:S(2)}, u32[]{:S(2)}) collective-permute-start(f32[16,512]{1,0:T(8,128)S(1)} %slice_add_fusion.14), channel_id=1, source_target_pairs={{0,2},{1,3},{2,0},{3,1},{4,6},{5,7},{6,4},{7,5},{8,10},{9,11},{10,... | collective-permute-start | bytes 98312 | tf_op jit(solution)/shard_map/ppermute | solution.py:95
  30.9 5.8 %collective-permute-start.4 = (f32[16,512]{1,0:T(8,128)S(1)}, f32[16,512]{1,0:T(8,128)S(1)}, u32[]{:S(2)}, u32[]{:S(2)}) collective-permute-start(f32[16,512]{1,0:T(8,128)S(1)} %slice_add_fusion.16), channel_id=1, source_target_pairs={{0,2},{1,3},{2,0},{3,1},{4,6},{5,7},{6,4},{7,5},{8,10},{9,11},{10,... | collective-permute-start | bytes 98312 | tf_op jit(solution)/shard_map/ppermute | solution.py:95
  32.6 7.3 %collective-permute-start.21 = (f32[16,512]{1,0:T(8,128)S(1)}, f32[16,512]{1,0:T(8,128)S(1)}, u32[]{:S(2)}, u32[]{:S(2)}) collective-permute-start(f32[16,512]{1,0:T(8,128)S(1)} %get-tuple-element.30), channel_id=1, source_target_pairs={{0,2},{1,3},{2,0},{3,1},{4,6},{5,7},{6,4},{7,5},{8,10},{9,11},{10,... | collective-permute-start | bytes 98312 | tf_op jit(solution)/shard_map/ppermute | solution.py:95
  44.2 6.4 %collective-permute-start.23 = (f32[64,512]{1,0:T(8,128)S(1)}, f32[64,512]{1,0:T(8,128)S(1)}, u32[]{:S(2)}, u32[]{:S(2)}) collective-permute-start(f32[64,512]{1,0:T(8,128)S(1)} %pad_maximum_fusion.6), channel_id=1, source_target_pairs={{0,16},{1,17},{2,18},{3,19},{4,12},{5,13},{6,14},{7,15},{8,24},{9,... | collective-permute-start | bytes 393224 | tf_op jit(solution)/shard_map/ppermute | solution.py:95
  46.0 7.5 %collective-permute-start.7 = (f32[64,512]{1,0:T(8,128)S(1)}, f32[64,512]{1,0:T(8,128)S(1)}, u32[]{:S(2)}, u32[]{:S(2)}) collective-permute-start(f32[64,512]{1,0:T(8,128)S(1)} %pad_maximum_fusion.4), channel_id=1, source_target_pairs={{0,16},{1,17},{2,18},{3,19},{4,12},{5,13},{6,14},{7,15},{8,24},{9,... | collective-permute-start | bytes 393224 | tf_op jit(solution)/shard_map/ppermute | solution.py:95
  46.9 9.3 %collective-permute-start.15 = (f32[64,512]{1,0:T(8,128)S(1)}, f32[64,512]{1,0:T(8,128)S(1)}, u32[]{:S(2)}, u32[]{:S(2)}) collective-permute-start(f32[64,512]{1,0:T(8,128)S(1)} %pad_maximum_fusion.5), channel_id=1, source_target_pairs={{0,16},{1,17},{2,18},{3,19},{4,12},{5,13},{6,14},{7,15},{8,24},{9,... | collective-permute-start | bytes 393224 | tf_op jit(solution)/shard_map/ppermute | solution.py:95
  50.7 7.2 %collective-permute-start.24 = (f32[128,512]{1,0:T(8,128)S(1)}, f32[128,512]{1,0:T(8,128)S(1)}, u32[]{:S(2)}, u32[]{:S(2)}) collective-permute-start(f32[128,512]{1,0:T(8,128)S(1)} %pad_maximum_fusion.3), channel_id=1, source_target_pairs={{0,8},{1,9},{2,10},{3,11},{4,20},{5,21},{6,22},{7,23},{8,0},{9,1},... | collective-permute-start | bytes 786440 | tf_op jit(solution)/shard_map/ppermute | solution.py:95
  53.5 6.4 %collective-permute-start.8 = (f32[128,512]{1,0:T(8,128)S(1)}, f32[128,512]{1,0:T(8,128)S(1)}, u32[]{:S(2)}, u32[]{:S(2)}) collective-permute-start(f32[128,512]{1,0:T(8,128)S(1)} %pad_maximum_fusion.1), channel_id=1, source_target_pairs={{0,8},{1,9},{2,10},{3,11},{4,20},{5,21},{6,22},{7,23},{8,0},{9,1},... | collective-permute-start | bytes 786440 | tf_op jit(solution)/shard_map/ppermute | solution.py:95
  56.2 6.5 %collective-permute-start.16 = (f32[128,512]{1,0:T(8,128)S(1)}, f32[128,512]{1,0:T(8,128)S(1)}, u32[]{:S(2)}, u32[]{:S(2)}) collective-permute-start(f32[128,512]{1,0:T(8,128)S(1)} %pad_maximum_fusion.2), channel_id=1, source_target_pairs={{0,8},{1,9},{2,10},{3,11},{4,20},{5,21},{6,22},{7,23},{8,0},{9,1},... | collective-permute-start | bytes 786440 | tf_op jit(solution)/shard_map/ppermute | solution.py:95
  68.1 5.2 %collective-permute-start.27 = (f32[160,128]{1,0:T(8,128)S(1)}, f32[160,128]{1,0:T(8,128)S(1)}, u32[]{:S(2)}, u32[]{:S(2)}) collective-permute-start(f32[160,128]{1,0:T(8,128)S(1)} %get-tuple-element.26), channel_id=1, source_target_pairs={{0,8},{1,9},{2,10},{3,11},{4,20},{5,21},{6,22},{7,23},{8,0},{9,1},... | collective-permute-start | bytes 245768 | tf_op jit(solution)/shard_map/ppermute | solution.py:95
  69.4 5.3 %collective-permute-start.28 = (f32[160,128]{1,0:T(8,128)S(1)}, f32[160,128]{1,0:T(8,128)S(1)}, u32[]{:S(2)}, u32[]{:S(2)}) collective-permute-start(f32[160,128]{1,0:T(8,128)S(1)} %get-tuple-element.27), channel_id=1, source_target_pairs={{0,24},{1,25},{2,26},{3,27},{4,28},{5,29},{6,30},{7,31},{8,16},{9,... | collective-permute-start | bytes 245768 | tf_op jit(solution)/shard_map/ppermute | solution.py:95
  74.7 6.7 %collective-permute-start.31 = (f32[160,128]{1,0:T(8,128)S(1)}, f32[160,128]{1,0:T(8,128)S(1)}, u32[]{:S(2)}, u32[]{:S(2)}) collective-permute-start(f32[160,128]{1,0:T(8,128)S(1)} %add_add_fusion.1), channel_id=1, source_target_pairs={{0,3},{1,2},{2,1},{3,0},{4,7},{5,6},{6,5},{7,4},{8,11},{9,10},{10,... | collective-permute-start | bytes 245768 | tf_op jit(solution)/shard_map/ppermute | solution.py:95
  76.6 6.3 %collective-permute-start.30 = (f32[160,128]{1,0:T(8,128)S(1)}, f32[160,128]{1,0:T(8,128)S(1)}, u32[]{:S(2)}, u32[]{:S(2)}) collective-permute-start(f32[160,128]{1,0:T(8,128)S(1)} %add_add_fusion.1), channel_id=1, source_target_pairs={{0,1},{1,0},{2,3},{3,2},{4,5},{5,4},{6,7},{7,6},{8,9},{9,8},{10,11... | collective-permute-start | bytes 245768 | tf_op jit(solution)/shard_map/ppermute | solution.py:95
  76.6 7.1 %collective-permute-start.29 = (f32[160,128]{1,0:T(8,128)S(1)}, f32[160,128]{1,0:T(8,128)S(1)}, u32[]{:S(2)}, u32[]{:S(2)}) collective-permute-start(f32[160,128]{1,0:T(8,128)S(1)} %add_add_fusion.1), channel_id=1, source_target_pairs={{0,2},{1,3},{2,0},{3,1},{4,6},{5,7},{6,4},{7,5},{8,10},{9,11},{10,... | collective-permute-start | bytes 245768 | tf_op jit(solution)/shard_map/ppermute | solution.py:95
  83.8 5.4 %collective-permute-start.34 = (f32[160,128]{1,0:T(8,128)S(1)}, f32[160,128]{1,0:T(8,128)S(1)}, u32[]{:S(2)}, u32[]{:S(2)}) collective-permute-start(f32[160,128]{1,0:T(8,128)S(1)} %add_add_fusion), channel_id=1, source_target_pairs={{0,24},{1,25},{2,26},{3,27},{4,28},{5,29},{6,30},{7,31},{8,16},{9,... | collective-permute-start | bytes 245768 | tf_op jit(solution)/shard_map/ppermute | solution.py:95
  (13 other events, 49.1 us)
